TPU v7x, 512 devices: a 8x2x16 block of a 8x16x16 slice. The times are simulated.
512 devices in a mesh: groups: 2 (over y), expert: 32 (over z, core), mp: 8 (over x).
Axes of the slice: x: 8, y: 2, z: 16, core: 2. Of those that a mesh axis runs over, the one named last changes fastest.
The devices are a block of a 8x16x16 slice.
Arguments:
- tokens: bfloat16 [49152, 1024], P(('groups', 'expert'), 'mp'), parts along dimension 0, may hold values from -60 to 60
- gain: float32 [1024], replicated, may hold values from 0.1 to 1.9
- w_res_in: bfloat16 [1024, 4096], P(None, 'mp'), may hold values from -0.1875 to 0.1875
- w_res_out: bfloat16 [4096, 1024], P('mp'), may hold values from -0.09375 to 0.09375
- w_exp_in: bfloat16 [32, 1024, 4096], P('expert', None, 'mp'), may hold values from -0.1875 to 0.1875
- w_exp_out: bfloat16 [32, 4096, 1024], P('expert', 'mp'), may hold values from -0.09375 to 0.09375
- expert_of: int32 [49152], P(('groups', 'expert')), parts along dimension 0, may hold values from 0 to 31
- slot_of: int32 [49152], P(('groups', 'expert')), parts along dimension 0, may hold values from -1 to 29, as said below
- gate_prob: float32 [49152], P(('groups', 'expert')), parts along dimension 0, may hold values from 0.2 to 1
Outputs:
- layer_out: bfloat16 [49152, 1024], P(('groups', 'expert'), 'mp'), parts along dimension 0
There are 2 independent parts, one for each index of `groups`. A program takes and returns all parts, laid end to end along the dimension named above; an argument that names none is the same for every part. Nothing has to cross between parts.
Inputs may be any that keep to these rules, and one draw needn't show every extreme that they name: slot_of[t] is the number of earlier tokens of t's aligned block of 768 tokens with the same expert_of, or -1 where that number is 30 or more. In every draw one expert has more than 30 tokens in every aligned block.
All inputs are finite; a program needn't handle non-finite values.
Results may differ from a plain program's by a relative error of at most 0.014.
Values may be sent and summed in bfloat16 or wider, within the bound.
No kernel may reach another device: no remote copies, remote signals or barrier semaphores. Data moves between devices by JAX's collectives and lax.ppermute only.
A program may use at most 64 MiB of HBM per device.

v0:
```python
import jax
import jax.numpy as jnp
from jax import lax
from jax.sharding import PartitionSpec as P


def laid_out(parts, dim):
    parts = jnp.moveaxis(parts, 0, dim)
    dims = parts.shape
    return parts.reshape(*dims[:dim], dims[dim] * dims[dim + 1], *dims[dim + 2 :])


def from_everyone(shard, axis):
    devices = lax.axis_size(axis)
    return lax.all_to_all(
        jnp.broadcast_to(shard[None], (devices, *shard.shape)), axis, 0, 0, tiled=True
    )


def collect(shard, axis, dim):
    return laid_out(from_everyone(shard, axis), dim)


def rms_rows(tokens, gain):
    values = tokens.astype(jnp.float32)
    inverse = lax.rsqrt(jnp.mean(values * values, axis=-1, keepdims=True) + 1e-05)
    return (values * inverse * gain).astype(jnp.bfloat16)


def per_device(
    tokens, gain, w_res_in, w_res_out, w_exp_in, w_exp_out, expert_of, slot_of, gate_prob
):
    full_rows = collect(tokens, "mp", 1)
    normed = rms_rows(full_rows, gain)
    res_hidden = jax.nn.gelu(jnp.dot(normed, w_res_in, preferred_element_type=jnp.float32)).astype(
        jnp.bfloat16
    )
    res_part = jnp.dot(res_hidden, w_res_out, preferred_element_type=jnp.float32)
    row_count = expert_of.shape[0]
    experts = lax.axis_size("expert")
    capacity = max(2, 5 * row_count // (4 * experts))
    feat_width = tokens.shape[1]
    slot_id = jnp.where(slot_of >= 0, expert_of * capacity + slot_of, -1)
    slot_index = jnp.arange(experts * capacity, dtype=jnp.int32)
    send_table = (slot_index[:, None] == slot_id[None, :]).astype(jnp.bfloat16)
    take_table = (slot_id[:, None] == slot_index[None, :]).astype(jnp.bfloat16)
    local_in = w_exp_in[0]
    local_out = w_exp_out[0]
    mp_index = lax.axis_index("mp")
    own_slice = lax.dynamic_slice_in_dim(normed, mp_index * feat_width, feat_width, 1)
    outgoing = jnp.dot(send_table, own_slice, preferred_element_type=jnp.float32).astype(
        jnp.bfloat16
    )
    incoming = lax.all_to_all(
        outgoing.reshape(experts, capacity, feat_width),
        "expert",
        split_axis=0,
        concat_axis=0,
        tiled=True,
    )
    piece = collect(incoming, "mp", 2)
    flat_piece = piece.reshape(-1, piece.shape[2])
    preact = jnp.dot(flat_piece, local_in, preferred_element_type=jnp.float32)
    exp_hidden = jax.nn.gelu(preact).astype(jnp.bfloat16)
    exp_part = jnp.dot(exp_hidden, local_out, preferred_element_type=jnp.float32)
    gate_column = gate_prob[:, None]
    summed = lax.psum_scatter(exp_part.astype(jnp.bfloat16), "mp", scatter_dimension=1, tiled=True)
    returned = lax.all_to_all(
        summed.reshape(experts, capacity, feat_width),
        "expert",
        split_axis=0,
        concat_axis=0,
        tiled=True,
    )
    moe_value = jnp.dot(
        take_table,
        returned.reshape(experts * capacity, feat_width),
        preferred_element_type=jnp.float32,
    )
    res_sum = lax.psum_scatter(
        res_part.astype(jnp.bfloat16), "mp", scatter_dimension=1, tiled=True
    ).astype(jnp.float32)
    return (res_sum + gate_column * moe_value).astype(jnp.bfloat16)


def solution(mesh):
    return jax.shard_map(
        per_device,
        mesh=mesh,
        in_specs=(
            P(("groups", "expert"), "mp"),
            P(),
            P(None, "mp"),
            P("mp", None),
            P("expert", None, "mp"),
            P("expert", "mp", None),
            P(("groups", "expert")),
            P(("groups", "expert")),
            P(("groups", "expert")),
        ),
        out_specs=P(("groups", "expert"), "mp"),
        check_vma=False,
    )
```

profile of v0, /device:TPU:65, one launch (start us, length us, event | category | flops | bytes accessed | tf_op | source)
XLA Modules:
  0.0 279.0 jit_solution(4909868781733401245)
XLA Ops:
  6.5 0.0 copy-start
  6.6 1.1 copy.13
  7.7 1.3 broadcast_in_dim.8
  9.0 0.0 copy-start.4
  9.0 0.0 copy-start.5
  9.0 0.0 copy-start.3
  9.0 8.0 %all-to-all-start = ((bf16[8,768,128]{1,2,0:T(8,128)(2,1)}), bf16[8,768,128]{1,2,0:T(8,128)(2,1)S(1)}, u32[]{:S(2)}, u32[]{:S(2)}) async-start(bf16[8,768,128]{1,2,0:T(8,128)(2,1)} %broadcast_in_dim.8), calls=%async_computation | async-start | bytes 3145728 | tf_op jit(solution)/shard_map/all_to_all | solution.py:15
  17.0 0.1 reduce-scatter.9.cloned.1.call-start
  17.0 0.0 copy-done.4
  17.0 0.0 copy-done.5
  17.1 23.3 %all-to-all-done = bf16[8,768,128]{1,2,0:T(8,128)(2,1)S(1)} async-done(((bf16[8,768,128]{1,2,0:T(8,128)(2,1)}), bf16[8,768,128]{1,2,0:T(8,128)(2,1)S(1)}, u32[]{:S(2)}, u32[]{:S(2)}) %all-to-all-start) | async-done | bytes 1572896 | tf_op jit(solution)/shard_map/all_to_all | solution.py:15
  40.4 0.4 multiply_reduce_fusion
  40.8 0.0 copy-done.3
  40.8 0.4 fusion.1
  41.2 0.0 copy-start.1
  41.2 1.2 copy-done.1
  42.4 0.6 fusion.27
  43.0 0.1 reshape.26
  43.1 83.1 %all_to_all.20 = bf16[32,30,128]{2,1,0:T(8,128)(2,1)S(1)} all-to-all(bf16[32,30,128]{2,1,0:T(8,128)(2,1)S(1)} %reshape.26), channel_id=1, replica_groups=mesh['groups'=2,'expert'=32,'mp'=8] {'expert'}, dimensions={0} | all-to-all | bytes 491520 | tf_op jit(solution)/shard_map/all_to_all | solution.py:54
  126.2 0.1 copy.14
  126.3 0.3 broadcast_in_dim.10
  126.7 50.4 %all_to_all.21 = bf16[8,32,30,128]{3,1,2,0:T(8,128)(2,1)S(1)} all-to-all(bf16[8,32,30,128]{3,1,2,0:T(8,128)(2,1)S(1)} %broadcast_in_dim.10), channel_id=1, replica_groups=mesh['groups'=2,'expert'=32,'mp'=8] {'mp'}, dimensions={0} | all-to-all | bytes 3932160 | tf_op jit(solution)/shard_map/all_to_all | solution.py:15
  177.0 1.3 copy.15
  178.3 0.0 copy-done
  178.3 5.0 %convolution_convert_fusion = bf16[960,1024]{1,0:T(8,128)(2,1)} fusion(bf16[1,512,1024]{2,1,0:T(8,128)(2,1)S(1)} %copy-done, bf16[120,8,8,128]{3,2,1,0:T(8,128)(2,1)S(1)} %bitcast.37, bf16[1,1024,512]{2,1,0:T(8,128)(2,1)} %param.13), kind=kOutput, calls=%fused_computation.21 | convolution fusion | flops 2018672640 | bytes 6029312 | tf_op jit(solution)/shard_map/dot_general | solution.py:65
  183.3 3.9 %copy.18 = bf16[960,1024]{0,1:T(8,128)(2,1)} copy(bf16[960,1024]{1,0:T(8,128)(2,1)} %convolution_convert_fusion) | data formatting | bytes 3932160
  187.1 0.0 copy-start.2
  187.1 0.1 reduce-scatter.9.cloned.1.call-update
  187.2 0.1 reduce-scatter.7.cloned.1.call-start
  187.3 1.3 copy-done.2
  188.6 4.7 %convolution_convert_fusion.1 = bf16[768,1024]{1,0:T(8,128)(2,1)} fusion(bf16[512,1024]{1,0:T(8,128)(2,1)} %param.12, bf16[768,1024]{0,1:T(8,128)(2,1)S(1)} %copy-done.2, bf16[1024,512]{1,0:T(8,128)(2,1)} %param.11), kind=kOutput, calls=%fused_computation.22 | convolution fusion | flops 1614938112 | bytes 5242880 | tf_op jit(solution)/shard_map/dot_general | solution.py:38
  193.3 2.6 copy.16
  195.9 0.0 copy-start.6
  195.9 0.1 reduce-scatter.7.cloned.1.call-update
  195.9 24.2 %reduce-scatter.9.cloned.1.call-done = bf16[128,960]{1,0:T(8,128)(2,1)} async-done(((bf16[1024,960]{1,0:T(8,128)(2,1)}), bf16[128,960]{1,0:T(8,128)(2,1)}) %reduce-scatter.9.cloned.1.call-update) | async-done | bytes 245776
  220.2 1.1 copy.19
  221.3 0.8 reshape.27
  222.1 17.9 %all-to-all-start.3 = ((bf16[32,30,128]{2,1,0:T(8,128)(2,1)}), bf16[32,30,128]{2,1,0:T(8,128)(2,1)S(1)}, u32[]{:S(2)}, u32[]{:S(2)}) async-start(bf16[32,30,128]{2,1,0:T(8,128)(2,1)} %reshape.27), calls=%async_computation.3 | async-start | bytes 524288 | tf_op jit(solution)/shard_map/all_to_all | solution.py:68
  239.9 29.6 %reduce-scatter.7.cloned.1.call-done = bf16[128,768]{1,0:T(8,128)(2,1)} async-done(((bf16[1024,768]{1,0:T(8,128)(2,1)}), bf16[128,768]{1,0:T(8,128)(2,1)}) %reduce-scatter.7.cloned.1.call-update) | async-done | bytes 196624
  269.5 1.1 copy.17
  270.6 0.0 all-to-all-done.3
  270.6 0.1 reshape.28
  270.7 0.0 copy-done.6
  270.7 1.4 fusion.28
  (2 shorter events, 0.0 us)
Async XLA Ops:
  6.5 171.8 %copy-start = (bf16[1,512,1024]{2,1,0:T(8,128)(2,1)S(1)}, bf16[1,512,1024]{2,1,0:T(8,128)(2,1)}, u32[]{:S(2)}) copy-start(bf16[1,512,1024]{2,1,0:T(8,128)(2,1)} %param.14) | copy-start | bytes 3145732
  9.0 8.1 %copy-start.4 = (s32[768]{0:T(1024)S(1)}, s32[768]{0:T(1024)}, u32[]{:S(2)}) copy-start(s32[768]{0:T(1024)} %param.16) | copy-start | bytes 9220
  9.0 8.1 %copy-start.5 = (s32[768]{0:T(1024)S(1)}, s32[768]{0:T(1024)}, u32[]{:S(2)}) copy-start(s32[768]{0:T(1024)} %param.15) | copy-start | bytes 9220
  9.0 31.8 %copy-start.3 = (f32[1024]{0:T(1024)S(1)}, f32[1024]{0:T(1024)}, u32[]{:S(2)}) copy-start(f32[1024]{0:T(1024)} %param.10) | copy-start | bytes 12292
  9.0 31.4 %all-to-all-start = ((bf16[8,768,128]{1,2,0:T(8,128)(2,1)}), bf16[8,768,128]{1,2,0:T(8,128)(2,1)S(1)}, u32[]{:S(2)}, u32[]{:S(2)}) async-start(bf16[8,768,128]{1,2,0:T(8,128)(2,1)} %broadcast_in_dim.8), calls=%async_computation | async-start | bytes 3145728 | tf_op jit(solution)/shard_map/all_to_all | solution.py:15
  17.0 203.2 %reduce-scatter.9.cloned.1.call-start = ((), (), s32[]{:S(2)}) async-start(), calls=%async_computation.7 | async-start | bytes 2359296
  41.2 1.2 copy-start.1
  187.1 1.4 copy-start.2
  187.2 82.3 %reduce-scatter.7.cloned.1.call-start = ((), (), s32[]{:S(2)}) async-start(), calls=%async_computation.6 | async-start | bytes 1769472
  195.9 74.8 %copy-start.6 = (f32[768]{0:T(1024)S(1)}, f32[768]{0:T(1024)}, u32[]{:S(2)}) copy-start(f32[768]{0:T(1024)} %param.17) | copy-start | bytes 9220
  222.1 48.5 %all-to-all-start.3 = ((bf16[32,30,128]{2,1,0:T(8,128)(2,1)}), bf16[32,30,128]{2,1,0:T(8,128)(2,1)S(1)}, u32[]{:S(2)}, u32[]{:S(2)}) async-start(bf16[32,30,128]{2,1,0:T(8,128)(2,1)} %reshape.27), calls=%async_computation.3 | async-start | bytes 524288 | tf_op jit(solution)/shard_map/all_to_all | solution.py:68
Sparse Core Ops, SparseCore 0:
  187.3 32.7 reduce-scatter.8
  223.0 46.4 reduce-scatter.6
where the time goes:
time: 282 us; the launch traced here: 279 us
  blocking collectives  134 us (48%)
  waiting for transfers between devices  77.2 us (27%)
  starting transfers between devices  26 us (9%)
  local copies, waits for them, and re-layouts  16.2 us (6%)
  between operations  13.6 us (5%)
  matrix products  11.7 us (4%)
    all_to_all x1, blocking collectives, per_device(): lax.all_to_all(outgoing.reshape(experts, capacity, feat_width), 'expert',...  83.1 us
    unnamed x4, waiting for transfers between devices  53.9 us
    all_to_all x1, blocking collectives, from_everyone(): lax.all_to_all(jnp.broadcast_to(shard[None], (devices, *shard.shape)), ax...  50.4 us
    all_to_all x1, waiting for transfers between devices, from_everyone(): lax.all_to_all(jnp.broadcast_to(shard[None], (devices, *shard.shape)), ax...  23.3 us
    all_to_all x1, starting transfers between devices, per_device(): lax.all_to_all(summed.reshape(experts, capacity, feat_width), 'expert', s...  17.9 us
    unnamed x19, local copies, waits for them, and re-layouts  12.3 us
    all_to_all x1, starting transfers between devices, from_everyone(): lax.all_to_all(jnp.broadcast_to(shard[None], (devices, *shard.shape)), ax...  7.99 us
  transfers between devices with their start and end apart: 4, of which 3 were waited for; matrix products, arithmetic and copies ran while one was open for 4% of the time, Pallas kernels for 0%

commit v1 on v0

v1 whole, which is shorter than its diff:
```python
import functools

import jax
import jax.numpy as jnp
from jax import lax
from jax.experimental import pallas as pl
from jax.experimental.pallas import tpu as pltpu
from jax.sharding import PartitionSpec as P


def from_everyone(shard, axis):
    devices = lax.axis_size(axis)
    return lax.all_to_all(
        jnp.broadcast_to(shard[None], (devices, *shard.shape)), axis, 0, 0, tiled=True
    )


def ffn_body(rows_ref, gain_ref, w_in_ref, w_out_ref, *rest):
    out_ref = rest[-1]
    parts = rows_ref.shape[0]
    width = rows_ref.shape[2]
    values = jnp.concatenate([rows_ref[k] for k in range(parts)], axis=1).astype(jnp.float32)
    inverse = lax.rsqrt(jnp.mean(values * values, axis=1, keepdims=True) + 1e-05)
    normed = (values * inverse * gain_ref[...]).astype(jnp.bfloat16)
    preact = jnp.dot(normed, w_in_ref[...], preferred_element_type=jnp.float32)
    hidden = jax.nn.gelu(preact, approximate=True).astype(jnp.bfloat16)
    sums = jnp.dot(hidden, w_out_ref[...], preferred_element_type=jnp.float32).astype(jnp.bfloat16)
    for k in range(parts):
        out_ref[k] = sums[:, k * width : (k + 1) * width]


def ffn(rows, gain, w_in, w_out, block, total, offset, into=None):
    parts, count, width = rows.shape
    model = parts * width
    first = offset // block
    in_specs = [
        pl.BlockSpec((parts, block, width), lambda i: (0, i, 0)),
        pl.BlockSpec((1, model), lambda i: (0, 0)),
        pl.BlockSpec(w_in.shape, lambda i: (0, 0)),
        pl.BlockSpec(w_out.shape, lambda i: (0, 0)),
    ]
    operands = [rows, gain.reshape(1, model), w_in, w_out]
    aliases = {}
    if into is not None:
        in_specs.append(pl.BlockSpec(memory_space=pl.ANY))
        operands.append(into)
        aliases = {4: 0}
    return pl.pallas_call(
        ffn_body,
        grid=(count // block,),
        in_specs=in_specs,
        out_specs=pl.BlockSpec((parts, block, width), lambda i: (0, first + i, 0)),
        out_shape=jax.ShapeDtypeStruct((parts, total, width), jnp.bfloat16),
        input_output_aliases=aliases,
        compiler_params=pltpu.CompilerParams(
            dimension_semantics=("arbitrary",), vmem_limit_bytes=40 * 1024 * 1024
        ),
        cost_estimate=pl.CostEstimate(
            flops=4 * count * model * w_in.shape[1],
            transcendentals=count * w_in.shape[1],
            bytes_accessed=4 * count * model + 4 * model * w_in.shape[1],
        ),
        name="ffn",
    )(*operands)


def per_device(
    tokens, gain, w_res_in, w_res_out, w_exp_in, w_exp_out, expert_of, slot_of, gate_prob
):
    row_count, feat_width = tokens.shape
    experts = lax.axis_size("expert")
    capacity = max(2, 5 * row_count // (4 * experts))
    slots = experts * capacity
    half = slots // 2
    slot_id = jnp.where(slot_of >= 0, expert_of * capacity + slot_of, -1)
    slot_index = jnp.arange(slots, dtype=jnp.int32)
    send_table = (slot_index[:, None] == slot_id[None, :]).astype(jnp.bfloat16)
    take_table = (slot_id[:, None] == slot_index[None, :]).astype(jnp.bfloat16)
    res_rows = lax.all_gather(tokens, "mp", axis=0)
    outgoing = jnp.dot(send_table, tokens, preferred_element_type=jnp.float32).astype(jnp.bfloat16)
    incoming = lax.all_to_all(
        outgoing.reshape(experts, capacity, feat_width),
        "expert",
        split_axis=0,
        concat_axis=0,
        tiled=True,
    ).reshape(slots, feat_width)
    rows_b = from_everyone(incoming[half:], "mp")
    rows_a = lax.all_gather(incoming[:half], "mp", axis=0)
    total = slots + row_count
    sums = ffn(res_rows, gain, w_res_in, w_res_out, row_count // 4, total, slots)
    sums = ffn(rows_a, gain, w_exp_in[0], w_exp_out[0], half // 2, total, 0, sums)
    sums = ffn(rows_b, gain, w_exp_in[0], w_exp_out[0], half // 2, total, half, sums)
    summed = lax.psum_scatter(sums, "mp", scatter_dimension=0, tiled=False)
    returned = lax.all_to_all(
        summed[:slots].reshape(experts, capacity, feat_width),
        "expert",
        split_axis=0,
        concat_axis=0,
        tiled=True,
    )
    moe_value = jnp.dot(
        take_table, returned.reshape(slots, feat_width), preferred_element_type=jnp.float32
    )
    res_sum = summed[slots:].astype(jnp.float32)
    return (res_sum + gate_prob[:, None] * moe_value).astype(jnp.bfloat16)


def solution(mesh):
    return jax.shard_map(
        per_device,
        mesh=mesh,
        in_specs=(
            P(("groups", "expert"), "mp"),
            P(),
            P(None, "mp"),
            P("mp", None),
            P("expert", None, "mp"),
            P("expert", "mp", None),
            P(("groups", "expert")),
            P(("groups", "expert")),
            P(("groups", "expert")),
        ),
        out_specs=P(("groups", "expert"), "mp"),
        check_vma=False,
    )
```

time: 282 us -> 244 us (0.87)
  waiting for transfers between devices: 77.2 us -> 56.4 us
  starting transfers between devices: 26 us -> 7.1 us
  blocking collectives: 134 us -> 146 us
  Pallas kernels: 0 us -> 10 us
  local copies, waits for them, and re-layouts: 16.2 us -> 6.24 us
  matrix products: 11.7 us -> 3.88 us
    reduce_scatter x0 -> x1, waiting for transfers between devices: none -> 55.6 us  [per_device(): summed = lax.psum_scatter(sums, 'mp', scatter_dimension=0, tiled=False)]
    unnamed x4 -> x2, waiting for transfers between devices: 53.9 us -> 0.8 us
    all_gather x0 -> x1, blocking collectives: none -> 42.3 us  [per_device(): rows_a = lax.all_gather(incoming[:half], 'mp', axis=0)]
    all_to_all x1, waiting for transfers between devices: 23.3 us -> 0.01 us  [from_everyone(): lax.all_to_all(jnp.broadcast_to(shard[None], (devices, *shard.shape)), ax...]
    all_to_all x1 -> x0, starting transfers between devices: 17.9 us -> none  [per_device(): lax.all_to_all(summed.reshape(experts, capacity, feat_width), 'expert', s...]
    all_to_all x1, blocking collectives: 83.1 us -> 67.1 us  [per_device(): lax.all_to_all(outgoing.reshape(experts, capacity, feat_width), 'expert',...]
    all_to_all x1, blocking collectives: 50.4 us -> 36.4 us  [per_device(): lax.all_to_all(summed[:slots].reshape(experts, capacity, feat_width), 'ex...]
    pallas_call x0 -> x3, Pallas kernels: none -> 10 us  [ffn(): pl.pallas_call(ffn_body, grid=(count // block,), in_specs=in_specs, out_s...]
  transfers between devices with their start and end apart: 4 -> 3, of which waited for: 3 -> 1; matrix products, arithmetic and copies ran while one was open for 4% -> 1% of each run, Pallas kernels for 0% -> 3%
where the time goes in v1:
time: 244 us
  blocking collectives  146 us (60%)
  waiting for transfers between devices  56.4 us (23%)
  between operations  13.5 us (6%)
  Pallas kernels  10 us (4%)
  starting transfers between devices  7.1 us (3%)
  local copies, waits for them, and re-layouts  6.24 us (3%)
  matrix products  3.88 us (2%)
    all_to_all x1, blocking collectives, per_device(): lax.all_to_all(outgoing.reshape(experts, capacity, feat_width), 'expert',...  67.1 us
    reduce_scatter x1, waiting for transfers between devices, per_device(): summed = lax.psum_scatter(sums, 'mp', scatter_dimension=0, tiled=False)  55.6 us
    all_gather x1, blocking collectives, per_device(): rows_a = lax.all_gather(incoming[:half], 'mp', axis=0)  42.3 us
    all_to_all x1, blocking collectives, per_device(): lax.all_to_all(summed[:slots].reshape(experts, capacity, feat_width), 'ex...  36.4 us
    pallas_call x3, Pallas kernels, ffn(): pl.pallas_call(ffn_body, grid=(count // block,), in_specs=in_specs, out_s...  10 us
    all_to_all x1, starting transfers between devices, from_everyone(): lax.all_to_all(jnp.broadcast_to(shard[None], (devices, *shard.shape)), ax...  7.04 us
  transfers between devices with their start and end apart: 3, of which 1 were waited for; matrix products, arithmetic and copies ran while one was open for 1% of the time, Pallas kernels for 3%

profile of v1, /device:TPU:65, one launch (start us, length us, event | category | flops | bytes accessed | tf_op | source)
XLA Modules:
  0.0 243.5 jit_solution(3012862517481523122)
XLA Ops:
  6.5 0.0 all-gather.3.cloned.1.call-start
  6.6 0.7 all-gather.3.cloned.1.call-update
  7.3 0.7 add_select_fusion
  8.0 1.5 fusion.6
  9.6 0.0 copy-start.6
  9.6 0.1 reshape.28
  9.7 67.1 %all_to_all.15 = bf16[32,30,128]{2,1,0:T(8,128)(2,1)S(1)} all-to-all(bf16[32,30,128]{2,1,0:T(8,128)(2,1)S(1)} %reshape.28), channel_id=1, replica_groups=mesh['groups'=2,'expert'=32,'mp'=8] {'expert'}, dimensions={0} | all-to-all | bytes 491520 | tf_op jit(solution)/shard_map/all_to_all | solution.py:81
  76.8 1.1 broadcast_in_dim.10
  77.9 7.0 %all-to-all-start.1 = ((bf16[8,480,128]{2,1,0:T(8,128)(2,1)}), bf16[8,480,128]{2,1,0:T(8,128)(2,1)S(1)}, u32[]{:S(2)}, u32[]{:S(2)}) async-start(bf16[8,480,128]{2,1,0:T(8,128)(2,1)} %broadcast_in_dim.10), calls=%async_computation.1 | async-start | bytes 1966080 | tf_op jit(solution)/shard_map/all_to_all | solution.py:13
  84.9 0.1 reduce-scatter.2.cloned.1.call-start
  85.0 42.3 %all_gather.13.rows_ref = bf16[8,480,128]{2,1,0:T(8,128)(2,1)} all-gather(bf16[1,480,128]{2,1,0:T(8,128)(2,1)S(1)} %all_gather.12), channel_id=1, replica_groups=mesh['groups'=2,'expert'=32,'mp'=8] {'mp'}, dimensions={0}, use_global_device_ids=true | all-gather | bytes 1105920 | tf_op jit(solution)/shard_map/all_gather | solution.py:89
  127.3 0.0 all-gather.3.cloned.1.call-done
  127.3 0.0 copy-done.6
  127.3 0.0 copy-start.3
  127.3 1.4 copy-done.3
  128.7 0.0 copy-start.4
  128.7 1.2 copy-done.4
  129.9 0.0 copy-start.5
  129.9 1.2 copy-done.5
  131.2 0.0 copy-start
  131.2 0.0 copy-start.1
  131.2 0.0 copy-start.2
  131.2 4.3 %ffn.3.rest_0_ = bf16[8,1728,128]{2,1,0:T(8,128)(2,1)} custom-call(bf16[8,768,128]{2,1,0:T(8,128)(2,1)S(1)} %bitcast.15, f32[1,1024]{1,0:T(1,128)S(1)} %bitcast.16, bf16[1024,512]{1,0:T(8,128)(2,1)S(1)} %copy-done.4, bf16[512,1024]{1,0:T(8,128)(2,1)S(1)} %copy-done.5), custom_call_target="tpu_custom_call" | custom-call | flops 1610612736 | bytes 5242880 | tf_op jit(solution)/shard_map/ffn/pallas_call | solution.py:48
  135.4 0.0 copy-done
  135.4 0.0 copy-done.1
  135.4 0.0 copy-done.2
  135.5 2.9 %ffn.4.rest_0_ = bf16[8,1728,128]{2,1,0:T(8,128)(2,1)} custom-call(bf16[8,480,128]{2,1,0:T(8,128)(2,1)S(1)} %copy-done.2, f32[1,1024]{1,0:T(1,128)S(1)} %bitcast.17, bf16[1024,512]{1,0:T(8,128)(2,1)S(1)} %bitcast.11, bf16[512,1024]{1,0:T(8,128)(2,1)S(1)} %bitcast.13, bf16[8,1728,128]{2,1,0:T(8,128)(2,1)} %ffn.3.rest_0_), custom_call_target="tpu_custom_call", output_to_operand_aliasing={{}: (4, {})} | custom-call | flops 1006632960 | bytes 4063232 | tf_op jit(solution)/shard_map/ffn/pallas_call | solution.py:48
  138.3 0.0 all-to-all-done.1.rows_ref
  138.3 2.9 %ffn.5 = bf16[8,1728,128]{2,1,0:T(8,128)(2,1)} custom-call(bf16[8,480,128]{2,1,0:T(8,128)(2,1)S(1)} %all-to-all-done.1.rows_ref, f32[1,1024]{1,0:T(1,128)S(1)} %bitcast.18, bf16[1024,512]{1,0:T(8,128)(2,1)S(1)} %bitcast.12, bf16[512,1024]{1,0:T(8,128)(2,1)S(1)} %bitcast.14, bf16[8,1728,128]{2,1,0:T(8,128)(2,1)} %ffn.4.rest_0_), custom_call_target="tpu_custom_call", output_to_operand_aliasing={{}: (4, {})} | custom-call | flops 1006632960 | bytes 4063232 | tf_op jit(solution)/shard_map/ffn/pallas_call | solution.py:48
  141.2 0.0 copy-start.7
  141.2 0.1 reduce-scatter.2.cloned.1.call-update
  141.3 55.6 %reduce-scatter.2.cloned.1.call-done = bf16[1,1728,128]{2,1,0:T(8,128)(2,1)} async-done(((bf16[8,1728,128]{2,1,0:T(8,128)(2,1)}), bf16[1,1728,128]{2,1,0:T(8,128)(2,1)}) %reduce-scatter.2.cloned.1.call-update) | async-done | bytes 442384 | tf_op jit(solution)/shard_map/reduce_scatter | solution.py:94
  196.8 1.0 slice.23
  197.8 0.1 reshape.30
  197.9 36.4 %all_to_all.16 = bf16[32,30,128]{2,1,0:T(8,128)(2,1)S(1)} all-to-all(bf16[32,30,128]{2,1,0:T(8,128)(2,1)S(1)} %reshape.30), channel_id=1, replica_groups=mesh['groups'=2,'expert'=32,'mp'=8] {'expert'}, dimensions={0} | all-to-all | bytes 491520 | tf_op jit(solution)/shard_map/all_to_all | solution.py:95
  234.3 0.1 reshape.31
  234.3 0.0 copy-done.7
  234.3 2.3 fusion.7
  (3 shorter events, 0.1 us)
Async XLA Ops:
  6.5 120.8 %all-gather.3.cloned.1.call-start = ((), (), s32[]{:S(2)}) async-start(), calls=%async_computation.5 | async-start | bytes 1769472 | tf_op jit(solution)/shard_map/all_gather | solution.py:79
  9.6 117.7 %copy-start.6 = (f32[1024]{0:T(1024)S(1)}, f32[1024]{0:T(1024)}, u32[]{:S(2)}) copy-start(f32[1024]{0:T(1024)} %param.10) | copy-start | bytes 12292
  77.9 60.4 %all-to-all-start.1 = ((bf16[8,480,128]{2,1,0:T(8,128)(2,1)}), bf16[8,480,128]{2,1,0:T(8,128)(2,1)S(1)}, u32[]{:S(2)}, u32[]{:S(2)}) async-start(bf16[8,480,128]{2,1,0:T(8,128)(2,1)} %broadcast_in_dim.10), calls=%async_computation.1 | async-start | bytes 1966080 | tf_op jit(solution)/shard_map/all_to_all | solution.py:13
  84.9 111.9 %reduce-scatter.2.cloned.1.call-start = ((), (), s32[]{:S(2)}) async-start(), calls=%async_computation.4 | async-start | bytes 3981312 | tf_op jit(solution)/shard_map/reduce_scatter | solution.py:94
  127.3 1.4 copy-start.3
  128.7 1.2 copy-start.4
  129.9 1.2 copy-start.5
  131.2 4.3 %copy-start = (bf16[1,1024,512]{2,1,0:T(8,128)(2,1)S(1)}, bf16[1,1024,512]{2,1,0:T(8,128)(2,1)}, u32[]{:S(2)}) copy-start(bf16[1,1024,512]{2,1,0:T(8,128)(2,1)} %param.13) | copy-start | bytes 3145732
  131.2 4.3 %copy-start.1 = (bf16[1,512,1024]{2,1,0:T(8,128)(2,1)S(1)}, bf16[1,512,1024]{2,1,0:T(8,128)(2,1)}, u32[]{:S(2)}) copy-start(bf16[1,512,1024]{2,1,0:T(8,128)(2,1)} %param.14) | copy-start | bytes 3145732
  131.2 4.3 %copy-start.2 = (bf16[8,480,128]{2,1,0:T(8,128)(2,1)S(1)}, bf16[8,480,128]{2,1,0:T(8,128)(2,1)}, u32[]{:S(2)}) copy-start(bf16[8,480,128]{2,1,0:T(8,128)(2,1)} %all_gather.13.rows_ref) | copy-start | bytes 2949124
  141.2 93.1 %copy-start.7 = (f32[768]{0:T(1024)S(1)}, f32[768]{0:T(1024)}, u32[]{:S(2)}) copy-start(f32[768]{0:T(1024)} %param.17) | copy-start | bytes 9220
Sparse Core Ops, SparseCore 0:
  9.4 75.9 all-gather.2
  141.4 55.4 reduce-scatter.1

commit v2 on v1

v2 whole, which is shorter than its diff:
```python
import functools

import jax
import jax.numpy as jnp
from jax import lax
from jax.experimental import pallas as pl
from jax.experimental.pallas import tpu as pltpu
from jax.sharding import PartitionSpec as P

RING = 8


def shift(value, step, axis="mp"):
    ring = lax.axis_size(axis)
    return lax.ppermute(value, axis, [(i, (i + step) % ring) for i in range(ring)])


def gather_far(own):
    return shift(own, 3), shift(own, -3)


def gather_near(own, below, above):
    half = own.shape[0] // 2
    from_left = shift(jnp.concatenate([own, above, below[:half]], axis=0), 1)
    from_right = shift(jnp.concatenate([own, below, above[half:]], axis=0), -1)
    return from_left, from_right


def ffn_body(
    me_ref,
    own_ref,
    below_ref,
    above_ref,
    left_ref,
    right_ref,
    gain_ref,
    w_in_ref,
    w_out_ref,
    to_right_ref,
    to_left_ref,
    keep_ref,
    rows_ref,
    sums_ref,
    *,
    block,
):
    me = me_ref[0]
    count, width = own_ref.shape
    half = count // 2
    place = [lax.rem(me + step, RING) for step in range(RING)]
    for start in range(0, count, block):
        at = pl.ds(start, block)
        rows_ref[place[0], at] = own_ref[at]
        rows_ref[place[1], at] = right_ref[at]
        rows_ref[place[7], at] = left_ref[at]
        rows_ref[place[3], at] = above_ref[at]
        rows_ref[place[5], at] = below_ref[at]
        rows_ref[place[2], at] = left_ref[pl.ds(count + start, block)]
        rows_ref[place[6], at] = right_ref[pl.ds(count + start, block)]
        if start < half:
            rows_ref[place[4], at] = left_ref[pl.ds(2 * count + start, block)]
        else:
            rows_ref[place[4], at] = right_ref[pl.ds(2 * count + start - half, block)]
        values = jnp.concatenate([rows_ref[k, at] for k in range(RING)], axis=1)
        values = values.astype(jnp.float32)
        inverse = lax.rsqrt(jnp.mean(values * values, axis=1, keepdims=True) + 1e-05)
        normed = (values * inverse * gain_ref[...]).astype(jnp.bfloat16)
        preact = jnp.dot(normed, w_in_ref[...], preferred_element_type=jnp.float32)
        hidden = jax.nn.gelu(preact, approximate=True).astype(jnp.bfloat16)
        sums = jnp.dot(hidden, w_out_ref[...], preferred_element_type=jnp.float32)
        sums = sums.astype(jnp.bfloat16)
        for k in range(RING):
            sums_ref[k, at] = sums[:, k * width : (k + 1) * width]
        to_right_ref[at] = sums_ref[place[1], at]
        to_right_ref[pl.ds(count + start, block)] = sums_ref[place[6], at]
        to_left_ref[at] = sums_ref[place[7], at]
        to_left_ref[pl.ds(count + start, block)] = sums_ref[place[2], at]
        if start < half:
            to_right_ref[pl.ds(2 * count + start, block)] = sums_ref[place[4], at]
        else:
            to_left_ref[pl.ds(2 * count + start - half, block)] = sums_ref[place[4], at]
        keep_ref[0, at] = sums_ref[place[0], at]
        keep_ref[1, at] = sums_ref[place[3], at]
        keep_ref[2, at] = sums_ref[place[5], at]


def ffn(me, own, below, above, left, right, gain, w_in, w_out, name):
    count, width = own.shape
    model = RING * width
    vmem = pl.BlockSpec(memory_space=pltpu.VMEM)
    edge = jax.ShapeDtypeStruct((5 * count // 2, width), jnp.bfloat16)
    return pl.pallas_call(
        functools.partial(ffn_body, block=count // 4),
        in_specs=[pl.BlockSpec(memory_space=pltpu.SMEM)] + [vmem] * 8,
        out_specs=[vmem] * 3,
        out_shape=[edge, edge, jax.ShapeDtypeStruct((3, count, width), jnp.bfloat16)],
        scratch_shapes=[
            pltpu.VMEM((RING, count, width), jnp.bfloat16),
            pltpu.VMEM((RING, count, width), jnp.bfloat16),
        ],
        compiler_params=pltpu.CompilerParams(vmem_limit_bytes=32 * 1024 * 1024),
        cost_estimate=pl.CostEstimate(
            flops=4 * count * model * w_in.shape[1],
            transcendentals=count * w_in.shape[1],
            bytes_accessed=4 * count * model + 4 * model * w_in.shape[1],
        ),
        name=name,
    )(me, own, below, above, left, right, gain.reshape(1, model), w_in, w_out)


def scatter_near(to_right, to_left):
    return shift(to_right, 1), shift(to_left, -1)


def scatter_far(keep, from_left, from_right):
    count = keep.shape[1]
    half = count // 2
    keep = keep.astype(jnp.float32)
    from_left = from_left.astype(jnp.float32)
    from_right = from_right.astype(jnp.float32)
    own = keep[0] + from_left[:count] + from_right[:count]
    above = keep[1] + from_right[count : 2 * count]
    above = jnp.concatenate([above[:half] + from_left[2 * count :], above[half:]], axis=0)
    below = keep[2] + from_left[count : 2 * count]
    below = jnp.concatenate([below[:half], below[half:] + from_right[2 * count :]], axis=0)
    first = shift(above.astype(jnp.bfloat16), 3)
    second = shift(below.astype(jnp.bfloat16), -3)
    return own, first, second


def per_device(
    tokens, gain, w_res_in, w_res_out, w_exp_in, w_exp_out, expert_of, slot_of, gate_prob
):
    row_count, feat_width = tokens.shape
    experts = lax.axis_size("expert")
    capacity = max(2, 5 * row_count // (4 * experts))
    slots = experts * capacity
    me = lax.axis_index("mp").astype(jnp.int32).reshape(1)
    slot_id = jnp.where(slot_of >= 0, expert_of * capacity + slot_of, -1)
    slot_index = jnp.arange(slots, dtype=jnp.int32)
    send_table = (slot_index[:, None] == slot_id[None, :]).astype(jnp.bfloat16)
    take_table = (slot_id[:, None] == slot_index[None, :]).astype(jnp.bfloat16)
    outgoing = jnp.dot(send_table, tokens, preferred_element_type=jnp.float32).astype(jnp.bfloat16)
    incoming = lax.all_to_all(
        outgoing.reshape(experts, capacity, feat_width),
        "expert",
        split_axis=0,
        concat_axis=0,
        tiled=True,
    ).reshape(slots, feat_width)
    with jax.named_scope("res_gather"):
        res_below, res_above = gather_far(tokens)
        res_left, res_right = gather_near(tokens, res_below, res_above)
    with jax.named_scope("exp_gather"):
        exp_below, exp_above = gather_far(incoming)
        exp_left, exp_right = gather_near(incoming, exp_below, exp_above)
    res_to_right, res_to_left, res_keep = ffn(
        me, tokens, res_below, res_above, res_left, res_right, gain, w_res_in, w_res_out, "res_ffn"
    )
    exp_to_right, exp_to_left, exp_keep = ffn(
        me,
        incoming,
        exp_below,
        exp_above,
        exp_left,
        exp_right,
        gain,
        w_exp_in[0],
        w_exp_out[0],
        "exp_ffn",
    )
    with jax.named_scope("exp_scatter"):
        exp_own, exp_first, exp_second = scatter_far(
            exp_keep, *scatter_near(exp_to_right, exp_to_left)
        )
        summed = exp_own + exp_first.astype(jnp.float32) + exp_second.astype(jnp.float32)
        summed = summed.astype(jnp.bfloat16)
    returned = lax.all_to_all(
        summed.reshape(experts, capacity, feat_width),
        "expert",
        split_axis=0,
        concat_axis=0,
        tiled=True,
    )
    with jax.named_scope("res_scatter"):
        res_own, res_first, res_second = scatter_far(
            res_keep, *scatter_near(res_to_right, res_to_left)
        )
        res_sum = res_own + res_first.astype(jnp.float32) + res_second.astype(jnp.float32)
    moe_value = jnp.dot(
        take_table, returned.reshape(slots, feat_width), preferred_element_type=jnp.float32
    )
    return (res_sum + gate_prob[:, None] * moe_value).astype(jnp.bfloat16)


def solution(mesh):
    return jax.shard_map(
        per_device,
        mesh=mesh,
        in_specs=(
            P(("groups", "expert"), "mp"),
            P(),
            P(None, "mp"),
            P("mp", None),
            P("expert", None, "mp"),
            P("expert", "mp", None),
            P(("groups", "expert")),
            P(("groups", "expert")),
            P(("groups", "expert")),
        ),
        out_specs=P(("groups", "expert"), "mp"),
        check_vma=False,
    )
```

time: 244 us -> 222 us (0.910); the launches traced: 244 us -> 219 us
  blocking collectives: 146 us -> 67.1 us
  starting transfers between devices: 7.1 us -> 82.9 us
  between operations: 13.5 us -> 0.47 us
  waiting for transfers between devices: 56.4 us -> 50.6 us
  local copies, waits for them, and re-layouts: 6.24 us -> 1.8 us
  other arithmetic: 0.71 us -> 4.22 us
    ppermute x0 -> x16, starting transfers between devices: none -> 68.7 us  [shift(): lax.ppermute(value, axis, [(i, (i + step) % ring) for i in range(ring)])]
    reduce_scatter x1 -> x0, waiting for transfers between devices: 55.6 us -> none  [per_device(): summed = lax.psum_scatter(sums, 'mp', scatter_dimension=0, tiled=False)]
    all_gather x1 -> x0, blocking collectives: 42.3 us -> none  [per_device(): rows_a = lax.all_gather(incoming[:half], 'mp', axis=0)]
    ppermute x0 -> x16, waiting for transfers between devices: none -> 39.4 us  [shift(): lax.ppermute(value, axis, [(i, (i + step) % ring) for i in range(ring)])]
    all_to_all x1 -> x0, blocking collectives: 36.4 us -> none  [per_device(): lax.all_to_all(summed[:slots].reshape(experts, capacity, feat_width), 'ex...]
    all_to_all x1, waiting for transfers between devices: 0.01 us -> 11.1 us  [per_device(): lax.all_to_all(summed.reshape(experts, capacity, feat_width), 'expert', s...]
    all_to_all x1, starting transfers between devices: 7.04 us -> 14.1 us  [per_device(): lax.all_to_all(summed.reshape(experts, capacity, feat_width), 'expert', s...]
    unnamed x16 -> x14, local copies, waits for them, and re-layouts: 3.88 us -> 0.04 us
  transfers between devices with their start and end apart: 3 -> 17, of which waited for: 1 -> 7; matrix products, arithmetic and copies ran while one was open for 1% -> 1% of each run, Pallas kernels for 3% -> 3%
where the time goes in v2:
time: 222 us; the launch traced here: 219 us
  starting transfers between devices  82.9 us (37%)
  blocking collectives  67.1 us (30%)
  waiting for transfers between devices  50.6 us (23%)
  Pallas kernels  7.64 us (3%)
  other arithmetic  4.22 us (2%)
  matrix products  4.12 us (2%)
    ppermute x16, starting transfers between devices, shift(): lax.ppermute(value, axis, [(i, (i + step) % ring) for i in range(ring)])  68.7 us
    all_to_all x1, blocking collectives, per_device(): lax.all_to_all(outgoing.reshape(experts, capacity, feat_width), 'expert',...  67.1 us
    ppermute x16, waiting for transfers between devices, shift(): lax.ppermute(value, axis, [(i, (i + step) % ring) for i in range(ring)])  39.4 us
    all_to_all x1, starting transfers between devices, per_device(): lax.all_to_all(summed.reshape(experts, capacity, feat_width), 'expert', s...  14.1 us
    all_to_all x1, waiting for transfers between devices, per_device(): lax.all_to_all(summed.reshape(experts, capacity, feat_width), 'expert', s...  11.1 us
    pallas_call x2, Pallas kernels, ffn(): pl.pallas_call(functools.partial(ffn_body, block=count // 4), in_specs=[p...  7.64 us
  transfers between devices with their start and end apart: 17, of which 7 were waited for; matrix products, arithmetic and copies ran while one was open for 1% of the time, Pallas kernels for 3%

profile of v2, /device:TPU:65, one launch (start us, length us, event | category | flops | bytes accessed | tf_op | source)
XLA Modules:
  0.0 218.8 jit_solution(9550470283204706854)
XLA Ops:
  0.0 0.7 add_select_fusion
  0.7 1.5 fusion.5
  2.3 0.1 reshape.24
  2.3 67.1 %all_to_all.10 = bf16[32,30,128]{2,1,0:T(8,128)(2,1)S(1)} all-to-all(bf16[32,30,128]{2,1,0:T(8,128)(2,1)S(1)} %reshape.24), channel_id=1, replica_groups=mesh['groups'=2,'expert'=32,'mp'=8] {'expert'}, dimensions={0} | all-to-all | bytes 491520 | tf_op jit(solution)/shard_map/all_to_all | solution.py:144
  69.4 0.1 reshape.25.own_ref
  69.5 5.4 %collective-permute-start.8 = (bf16[960,128]{1,0:T(8,128)(2,1)S(1)}, bf16[960,128]{1,0:T(8,128)(2,1)S(1)}, u32[]{:S(2)}, u32[]{:S(2)}) collective-permute-start(bf16[960,128]{1,0:T(8,128)(2,1)S(1)} %reshape.25.own_ref), channel_id=1, source_target_pairs={{0,3},{1,4},{2,5},{3,6},{4,7},{5,0},{6,1},{7,2},{8,11},{9,12},{10,... | collective-permute-start | bytes 737288 | tf_op jit(solution)/shard_map/exp_gather/ppermute | solution.py:15
  74.9 3.5 %collective-permute-start.9 = (bf16[960,128]{1,0:T(8,128)(2,1)S(1)}, bf16[960,128]{1,0:T(8,128)(2,1)S(1)}, u32[]{:S(2)}, u32[]{:S(2)}) collective-permute-start(bf16[960,128]{1,0:T(8,128)(2,1)S(1)} %reshape.25.own_ref), channel_id=1, source_target_pairs={{0,5},{1,6},{2,7},{3,0},{4,1},{5,2},{6,3},{7,4},{8,13},{9,14},{10,... | collective-permute-start | bytes 737288 | tf_op jit(solution)/shard_map/exp_gather/ppermute | solution.py:15
  78.4 13.3 %collective-permute-done.8.below_ref = bf16[960,128]{1,0:T(8,128)(2,1)S(1)} collective-permute-done((bf16[960,128]{1,0:T(8,128)(2,1)S(1)}, bf16[960,128]{1,0:T(8,128)(2,1)S(1)}, u32[]{:S(2)}, u32[]{:S(2)}) %collective-permute-start.8) | collective-permute-done | bytes 245792 | tf_op jit(solution)/shard_map/exp_gather/ppermute | solution.py:15
  91.8 0.0 copy-start
  91.8 0.0 collective-permute-done.9.above_ref
  91.8 1.2 fusion.7
  93.0 10.9 %collective-permute-start.10 = (bf16[2400,128]{1,0:T(8,128)(2,1)}, bf16[2400,128]{1,0:T(8,128)(2,1)}, u32[]{:S(2)}, u32[]{:S(2)}) collective-permute-start(bf16[2400,128]{1,0:T(8,128)(2,1)} %get-tuple-element.22), channel_id=1, source_target_pairs={{0,1},{1,2},{2,3},{3,4},{4,5},{5,6},{6,7},{7,0},{8,9},{9,10},{10,1... | collective-permute-start | bytes 1843208 | tf_op jit(solution)/shard_map/exp_gather/ppermute | solution.py:15
  103.9 2.0 collective-permute-start.11
  105.9 2.1 collective-permute-start
  108.0 6.2 %collective-permute-start.1 = (bf16[768,128]{1,0:T(8,128)(2,1)S(1)}, bf16[768,128]{1,0:T(8,128)(2,1)S(1)}, u32[]{:S(2)}, u32[]{:S(2)}) collective-permute-start(bf16[768,128]{1,0:T(8,128)(2,1)S(1)} %copy-done), channel_id=1, source_target_pairs={{0,5},{1,6},{2,7},{3,0},{4,1},{5,2},{6,3},{7,4},{8,13},{9,14},{10,... | collective-permute-start | bytes 589832 | tf_op jit(solution)/shard_map/res_gather/ppermute | solution.py:15
  114.2 13.4 %collective-permute-done.below_ref = bf16[768,128]{1,0:T(8,128)(2,1)S(1)} collective-permute-done((bf16[768,128]{1,0:T(8,128)(2,1)S(1)}, bf16[768,128]{1,0:T(8,128)(2,1)S(1)}, u32[]{:S(2)}, u32[]{:S(2)}) %collective-permute-start) | collective-permute-done | bytes 196640 | tf_op jit(solution)/shard_map/res_gather/ppermute | solution.py:15
  127.7 0.0 collective-permute-done.1.above_ref
  127.7 0.1 fusion.9
  127.8 5.2 %collective-permute-start.2 = (bf16[1920,128]{1,0:T(8,128)(2,1)S(1)}, bf16[1920,128]{1,0:T(8,128)(2,1)S(1)}, u32[]{:S(2)}, u32[]{:S(2)}) collective-permute-start(bf16[1920,128]{1,0:T(8,128)(2,1)S(1)} %get-tuple-element.24), channel_id=1, source_target_pairs={{0,1},{1,2},{2,3},{3,4},{4,5},{5,6},{6,7},{7,0},{8,9},{9,10},{10,1... | collective-permute-start | bytes 1474568 | tf_op jit(solution)/shard_map/res_gather/ppermute | solution.py:15
  133.0 2.7 %collective-permute-start.3 = (bf16[1920,128]{1,0:T(8,128)(2,1)S(1)}, bf16[1920,128]{1,0:T(8,128)(2,1)S(1)}, u32[]{:S(2)}, u32[]{:S(2)}) collective-permute-start(bf16[1920,128]{1,0:T(8,128)(2,1)S(1)} %get-tuple-element.23), channel_id=1, source_target_pairs={{0,7},{1,0},{2,1},{3,2},{4,3},{5,4},{6,5},{7,6},{8,15},{9,8},{10,9... | collective-permute-start | bytes 1474568 | tf_op jit(solution)/shard_map/res_gather/ppermute | solution.py:15
  135.7 0.0 collective-permute-done.10.left_ref
  135.7 0.0 collective-permute-done.11.right_ref
  135.7 0.0 copy-done.1
  135.7 0.0 copy-done.2
  135.7 0.0 copy-start.3
  135.7 0.0 copy-start.4
  135.7 4.8 %exp_ffn.1 = (bf16[2400,128]{1,0:T(8,128)(2,1)S(1)}, bf16[2400,128]{1,0:T(8,128)(2,1)S(1)}, bf16[3,960,128]{2,1,0:T(8,128)(2,1)S(1)}) custom-call(s32[1]{0:T(128)} %bitcast.me_ref, bf16[960,128]{1,0:T(8,128)(2,1)S(1)} %reshape.25.own_ref, bf16[960,128]{1,0:T(8,128)(2,1)S(1)} %collective-permute-done.8.below_ref, ...), custom_call_target="tpu_custom_call" | custom-call | flops 2013265920 | bytes 6029312 | tf_op jit(solution)/shard_map/exp_ffn/pallas_call | solution.py:92
  140.6 2.6 %collective-permute-start.12 = (bf16[2400,128]{1,0:T(8,128)(2,1)S(1)}, bf16[2400,128]{1,0:T(8,128)(2,1)S(1)}, u32[]{:S(2)}, u32[]{:S(2)}) collective-permute-start(bf16[2400,128]{1,0:T(8,128)(2,1)S(1)} %get-tuple-element.15), channel_id=1, source_target_pairs={{0,1},{1,2},{2,3},{3,4},{4,5},{5,6},{6,7},{7,0},{8,9},{9,10},{10,1... | collective-permute-start | bytes 1843208 | tf_op jit(solution)/shard_map/exp_scatter/ppermute | solution.py:15
  143.2 4.5 %collective-permute-start.13 = (bf16[2400,128]{1,0:T(8,128)(2,1)S(1)}, bf16[2400,128]{1,0:T(8,128)(2,1)S(1)}, u32[]{:S(2)}, u32[]{:S(2)}) collective-permute-start(bf16[2400,128]{1,0:T(8,128)(2,1)S(1)} %get-tuple-element.16), channel_id=1, source_target_pairs={{0,7},{1,0},{2,1},{3,2},{4,3},{5,4},{6,5},{7,6},{8,15},{9,8},{10,9... | collective-permute-start | bytes 1843208 | tf_op jit(solution)/shard_map/exp_scatter/ppermute | solution.py:15
  147.7 0.0 collective-permute-done.2.left_ref
  147.7 0.0 collective-permute-done.3.right_ref
  147.8 2.8 %res_ffn.1 = (bf16[1920,128]{1,0:T(8,128)(2,1)S(1)}, bf16[1920,128]{1,0:T(8,128)(2,1)S(1)}, bf16[3,768,128]{2,1,0:T(8,128)(2,1)S(1)}) custom-call(s32[1]{0:T(128)} %bitcast.me_ref, bf16[768,128]{1,0:T(8,128)(2,1)S(1)} %copy-done, bf16[768,128]{1,0:T(8,128)(2,1)S(1)} %collective-permute-done.below_ref, bf16[768,128]{1,0:T(8,128)(2,1)S(1)} %collective-permute-done.1.above_ref, ...), custom_call_target="tpu_custom_call" | custom-call | flops 1610612736 | bytes 5242880 | tf_op jit(solution)/shard_map/res_ffn/pallas_call | solution.py:92
  150.6 2.0 collective-permute-start.4
  152.5 4.6 %collective-permute-start.5 = (bf16[1920,128]{1,0:T(8,128)(2,1)S(1)}, bf16[1920,128]{1,0:T(8,128)(2,1)S(1)}, u32[]{:S(2)}, u32[]{:S(2)}) collective-permute-start(bf16[1920,128]{1,0:T(8,128)(2,1)S(1)} %get-tuple-element.13), channel_id=1, source_target_pairs={{0,7},{1,0},{2,1},{3,2},{4,3},{5,4},{6,5},{7,6},{8,15},{9,8},{10,9... | collective-permute-start | bytes 1474568 | tf_op jit(solution)/shard_map/res_scatter/ppermute | solution.py:15
  157.2 0.1 convert_element_type.51
  157.3 0.0 collective-permute-done.12
  157.3 0.1 convert_element_type.52
  157.4 0.0 collective-permute-done.13
  157.4 0.1 convert_element_type.53
  157.5 0.1 slice_add_fusion.1
  157.6 0.1 fusion.17
  157.7 6.3 %collective-permute-start.14 = (bf16[960,128]{1,0:T(8,128)(2,1)S(1)}, bf16[960,128]{1,0:T(8,128)(2,1)S(1)}, u32[]{:S(2)}, u32[]{:S(2)}) collective-permute-start(bf16[960,128]{1,0:T(8,128)(2,1)S(1)} %pad_maximum_fusion.4), channel_id=1, source_target_pairs={{0,3},{1,4},{2,5},{3,6},{4,7},{5,0},{6,1},{7,2},{8,11},{9,12},{10,... | collective-permute-start | bytes 737288 | tf_op jit(solution)/shard_map/exp_scatter/ppermute | solution.py:15
  164.0 2.1 collective-permute-start.15
  166.1 0.1 convert_element_type.45
  166.2 0.8 collective-permute-done.4
  167.0 0.1 convert_element_type.46
  167.0 2.7 %collective-permute-done.5 = bf16[1920,128]{1,0:T(8,128)(2,1)S(1)} collective-permute-done((bf16[1920,128]{1,0:T(8,128)(2,1)S(1)}, bf16[1920,128]{1,0:T(8,128)(2,1)S(1)}, u32[]{:S(2)}, u32[]{:S(2)}) %collective-permute-start.5) | collective-permute-done | bytes 491552 | tf_op jit(solution)/shard_map/res_scatter/ppermute | solution.py:15
  169.8 0.1 convert_element_type.47
  169.8 8.9 %collective-permute-done.14 = bf16[960,128]{1,0:T(8,128)(2,1)S(1)} collective-permute-done((bf16[960,128]{1,0:T(8,128)(2,1)S(1)}, bf16[960,128]{1,0:T(8,128)(2,1)S(1)}, u32[]{:S(2)}, u32[]{:S(2)}) %collective-permute-start.14) | collective-permute-done | bytes 245792 | tf_op jit(solution)/shard_map/exp_scatter/ppermute | solution.py:15
  178.7 0.3 collective-permute-done.15
  179.0 0.1 fusion.12
  179.1 0.8 reshape.26
  179.9 14.1 %all-to-all-start.1 = ((bf16[32,30,128]{2,1,0:T(8,128)(2,1)}), bf16[32,30,128]{2,1,0:T(8,128)(2,1)S(1)}, u32[]{:S(2)}, u32[]{:S(2)}) async-start(bf16[32,30,128]{2,1,0:T(8,128)(2,1)} %reshape.26), calls=%async_computation.1 | async-start | bytes 524288 | tf_op jit(solution)/shard_map/all_to_all | solution.py:178
  194.0 0.1 slice_add_fusion.5
  194.1 0.0 copy-start.6
  194.2 0.7 pad_maximum_fusion.6
  194.9 5.6 %collective-permute-start.6 = (bf16[768,128]{1,0:T(8,128)(2,1)}, bf16[768,128]{1,0:T(8,128)(2,1)}, u32[]{:S(2)}, u32[]{:S(2)}) collective-permute-start(bf16[768,128]{1,0:T(8,128)(2,1)} %pad_maximum_fusion.6), channel_id=1, source_target_pairs={{0,3},{1,4},{2,5},{3,6},{4,7},{5,0},{6,1},{7,2},{8,11},{9,12},{10,... | collective-permute-start | bytes 589832 | tf_op jit(solution)/shard_map/res_scatter/ppermute | solution.py:15
  200.5 0.7 pad_maximum_fusion.7
  201.2 3.1 %collective-permute-start.7 = (bf16[768,128]{1,0:T(8,128)(2,1)}, bf16[768,128]{1,0:T(8,128)(2,1)}, u32[]{:S(2)}, u32[]{:S(2)}) collective-permute-start(bf16[768,128]{1,0:T(8,128)(2,1)} %pad_maximum_fusion.7), channel_id=1, source_target_pairs={{0,5},{1,6},{2,7},{3,0},{4,1},{5,2},{6,3},{7,4},{8,13},{9,14},{10,... | collective-permute-start | bytes 589832 | tf_op jit(solution)/shard_map/res_scatter/ppermute | solution.py:15
  204.3 11.1 %all-to-all-done.1 = bf16[32,30,128]{2,1,0:T(8,128)(2,1)S(1)} async-done(((bf16[32,30,128]{2,1,0:T(8,128)(2,1)}), bf16[32,30,128]{2,1,0:T(8,128)(2,1)S(1)}, u32[]{:S(2)}, u32[]{:S(2)}) %all-to-all-start.1) | async-done | bytes 245792 | tf_op jit(solution)/shard_map/all_to_all | solution.py:178
  215.4 0.8 reshape.27
  216.2 0.0 collective-permute-done.6
  216.2 0.0 collective-permute-done.7
  216.2 2.6 %fusion.16 = bf16[768,128]{1,0:T(8,128)(2,1)} fusion(f32[1920,128]{1,0:T(8,128)S(1)} %convert_element_type.47, f32[1920,128]{1,0:T(8,128)S(1)} %convert_element_type.46, f32[3,768,128]{2,1,0:T(8,128)S(1)} %convert_element_type.45, bf16[768,128]{1,0:T(8,128)(2,1)} %collective-permute-done.7, bf16[768,128]{1,0:T(8,128)(2,1)} %collective-permute-done.6, ...), kind=kOutput, calls=%fused_computation.34 | convolution fusion | flops 190365696 | bytes 2021376 | tf_op jit(solution)/shard_map/dot_general | solution.py:190
  (19 shorter events, 0.2 us)
Async XLA Ops:
  69.5 22.3 %collective-permute-start.8 = (bf16[960,128]{1,0:T(8,128)(2,1)S(1)}, bf16[960,128]{1,0:T(8,128)(2,1)S(1)}, u32[]{:S(2)}, u32[]{:S(2)}) collective-permute-start(bf16[960,128]{1,0:T(8,128)(2,1)S(1)} %reshape.25.own_ref), channel_id=1, source_target_pairs={{0,3},{1,4},{2,5},{3,6},{4,7},{5,0},{6,1},{7,2},{8,11},{9,12},{10,... | collective-permute-start | bytes 737288 | tf_op jit(solution)/shard_map/exp_gather/ppermute | solution.py:15
  74.9 16.9 %collective-permute-start.9 = (bf16[960,128]{1,0:T(8,128)(2,1)S(1)}, bf16[960,128]{1,0:T(8,128)(2,1)S(1)}, u32[]{:S(2)}, u32[]{:S(2)}) collective-permute-start(bf16[960,128]{1,0:T(8,128)(2,1)S(1)} %reshape.25.own_ref), channel_id=1, source_target_pairs={{0,5},{1,6},{2,7},{3,0},{4,1},{5,2},{6,3},{7,4},{8,13},{9,14},{10,... | collective-permute-start | bytes 737288 | tf_op jit(solution)/shard_map/exp_gather/ppermute | solution.py:15
  91.8 14.1 %copy-start = (bf16[768,128]{1,0:T(8,128)(2,1)S(1)}, bf16[768,128]{1,0:T(8,128)(2,1)}, u32[]{:S(2)}) copy-start(bf16[768,128]{1,0:T(8,128)(2,1)} %own_ref.1) | copy-start | bytes 589828
  93.0 42.7 %copy-start.1 = (bf16[1,1024,512]{2,1,0:T(8,128)(2,1)S(1)}, bf16[1,1024,512]{2,1,0:T(8,128)(2,1)}, u32[]{:S(2)}) copy-start(bf16[1,1024,512]{2,1,0:T(8,128)(2,1)} %param.13) | copy-start | bytes 3145732
  93.0 42.7 %copy-start.2 = (bf16[1,512,1024]{2,1,0:T(8,128)(2,1)S(1)}, bf16[1,512,1024]{2,1,0:T(8,128)(2,1)}, u32[]{:S(2)}) copy-start(bf16[1,512,1024]{2,1,0:T(8,128)(2,1)} %param.14) | copy-start | bytes 3145732
  93.0 42.8 %copy-start.5 = (f32[1024]{0:T(1024)S(1)}, f32[1024]{0:T(1024)}, u32[]{:S(2)}) copy-start(f32[1024]{0:T(1024)} %param.10) | copy-start | bytes 12292
  93.0 42.7 %collective-permute-start.10 = (bf16[2400,128]{1,0:T(8,128)(2,1)}, bf16[2400,128]{1,0:T(8,128)(2,1)}, u32[]{:S(2)}, u32[]{:S(2)}) collective-permute-start(bf16[2400,128]{1,0:T(8,128)(2,1)} %get-tuple-element.22), channel_id=1, source_target_pairs={{0,1},{1,2},{2,3},{3,4},{4,5},{5,6},{6,7},{7,0},{8,9},{9,10},{10,1... | collective-permute-start | bytes 1843208 | tf_op jit(solution)/shard_map/exp_gather/ppermute | solution.py:15
  103.9 31.8 %collective-permute-start.11 = (bf16[2400,128]{1,0:T(8,128)(2,1)}, bf16[2400,128]{1,0:T(8,128)(2,1)}, u32[]{:S(2)}, u32[]{:S(2)}) collective-permute-start(bf16[2400,128]{1,0:T(8,128)(2,1)} %get-tuple-element.21), channel_id=1, source_target_pairs={{0,7},{1,0},{2,1},{3,2},{4,3},{5,4},{6,5},{7,6},{8,15},{9,8},{10,9... | collective-permute-start | bytes 1843208 | tf_op jit(solution)/shard_map/exp_gather/ppermute | solution.py:15
  105.9 21.8 %collective-permute-start = (bf16[768,128]{1,0:T(8,128)(2,1)S(1)}, bf16[768,128]{1,0:T(8,128)(2,1)S(1)}, u32[]{:S(2)}, u32[]{:S(2)}) collective-permute-start(bf16[768,128]{1,0:T(8,128)(2,1)S(1)} %copy-done), channel_id=1, source_target_pairs={{0,3},{1,4},{2,5},{3,6},{4,7},{5,0},{6,1},{7,2},{8,11},{9,12},{10,... | collective-permute-start | bytes 589832 | tf_op jit(solution)/shard_map/res_gather/ppermute | solution.py:15
  108.0 19.7 %collective-permute-start.1 = (bf16[768,128]{1,0:T(8,128)(2,1)S(1)}, bf16[768,128]{1,0:T(8,128)(2,1)S(1)}, u32[]{:S(2)}, u32[]{:S(2)}) collective-permute-start(bf16[768,128]{1,0:T(8,128)(2,1)S(1)} %copy-done), channel_id=1, source_target_pairs={{0,5},{1,6},{2,7},{3,0},{4,1},{5,2},{6,3},{7,4},{8,13},{9,14},{10,... | collective-permute-start | bytes 589832 | tf_op jit(solution)/shard_map/res_gather/ppermute | solution.py:15
  127.8 19.9 %collective-permute-start.2 = (bf16[1920,128]{1,0:T(8,128)(2,1)S(1)}, bf16[1920,128]{1,0:T(8,128)(2,1)S(1)}, u32[]{:S(2)}, u32[]{:S(2)}) collective-permute-start(bf16[1920,128]{1,0:T(8,128)(2,1)S(1)} %get-tuple-element.24), channel_id=1, source_target_pairs={{0,1},{1,2},{2,3},{3,4},{4,5},{5,6},{6,7},{7,0},{8,9},{9,10},{10,1... | collective-permute-start | bytes 1474568 | tf_op jit(solution)/shard_map/res_gather/ppermute | solution.py:15
  133.0 14.8 %collective-permute-start.3 = (bf16[1920,128]{1,0:T(8,128)(2,1)S(1)}, bf16[1920,128]{1,0:T(8,128)(2,1)S(1)}, u32[]{:S(2)}, u32[]{:S(2)}) collective-permute-start(bf16[1920,128]{1,0:T(8,128)(2,1)S(1)} %get-tuple-element.23), channel_id=1, source_target_pairs={{0,7},{1,0},{2,1},{3,2},{4,3},{5,4},{6,5},{7,6},{8,15},{9,8},{10,9... | collective-permute-start | bytes 1474568 | tf_op jit(solution)/shard_map/res_gather/ppermute | solution.py:15
  135.7 12.0 %copy-start.3 = (bf16[1024,512]{1,0:T(8,128)(2,1)S(1)}, bf16[1024,512]{1,0:T(8,128)(2,1)}, u32[]{:S(2)}) copy-start(bf16[1024,512]{1,0:T(8,128)(2,1)} %w_in_ref.1) | copy-start | bytes 3145732
  135.7 12.0 %copy-start.4 = (bf16[512,1024]{1,0:T(8,128)(2,1)S(1)}, bf16[512,1024]{1,0:T(8,128)(2,1)}, u32[]{:S(2)}) copy-start(bf16[512,1024]{1,0:T(8,128)(2,1)} %w_out_ref.1) | copy-start | bytes 3145732
  140.6 16.7 %collective-permute-start.12 = (bf16[2400,128]{1,0:T(8,128)(2,1)S(1)}, bf16[2400,128]{1,0:T(8,128)(2,1)S(1)}, u32[]{:S(2)}, u32[]{:S(2)}) collective-permute-start(bf16[2400,128]{1,0:T(8,128)(2,1)S(1)} %get-tuple-element.15), channel_id=1, source_target_pairs={{0,1},{1,2},{2,3},{3,4},{4,5},{5,6},{6,7},{7,0},{8,9},{9,10},{10,1... | collective-permute-start | bytes 1843208 | tf_op jit(solution)/shard_map/exp_scatter/ppermute | solution.py:15
  143.2 14.2 %collective-permute-start.13 = (bf16[2400,128]{1,0:T(8,128)(2,1)S(1)}, bf16[2400,128]{1,0:T(8,128)(2,1)S(1)}, u32[]{:S(2)}, u32[]{:S(2)}) collective-permute-start(bf16[2400,128]{1,0:T(8,128)(2,1)S(1)} %get-tuple-element.16), channel_id=1, source_target_pairs={{0,7},{1,0},{2,1},{3,2},{4,3},{5,4},{6,5},{7,6},{8,15},{9,8},{10,9... | collective-permute-start | bytes 1843208 | tf_op jit(solution)/shard_map/exp_scatter/ppermute | solution.py:15
  150.6 16.4 %collective-permute-start.4 = (bf16[1920,128]{1,0:T(8,128)(2,1)S(1)}, bf16[1920,128]{1,0:T(8,128)(2,1)S(1)}, u32[]{:S(2)}, u32[]{:S(2)}) collective-permute-start(bf16[1920,128]{1,0:T(8,128)(2,1)S(1)} %get-tuple-element.12), channel_id=1, source_target_pairs={{0,1},{1,2},{2,3},{3,4},{4,5},{5,6},{6,7},{7,0},{8,9},{9,10},{10,1... | collective-permute-start | bytes 1474568 | tf_op jit(solution)/shard_map/res_scatter/ppermute | solution.py:15
  152.5 17.2 %collective-permute-start.5 = (bf16[1920,128]{1,0:T(8,128)(2,1)S(1)}, bf16[1920,128]{1,0:T(8,128)(2,1)S(1)}, u32[]{:S(2)}, u32[]{:S(2)}) collective-permute-start(bf16[1920,128]{1,0:T(8,128)(2,1)S(1)} %get-tuple-element.13), channel_id=1, source_target_pairs={{0,7},{1,0},{2,1},{3,2},{4,3},{5,4},{6,5},{7,6},{8,15},{9,8},{10,9... | collective-permute-start | bytes 1474568 | tf_op jit(solution)/shard_map/res_scatter/ppermute | solution.py:15
  157.7 21.0 %collective-permute-start.14 = (bf16[960,128]{1,0:T(8,128)(2,1)S(1)}, bf16[960,128]{1,0:T(8,128)(2,1)S(1)}, u32[]{:S(2)}, u32[]{:S(2)}) collective-permute-start(bf16[960,128]{1,0:T(8,128)(2,1)S(1)} %pad_maximum_fusion.4), channel_id=1, source_target_pairs={{0,3},{1,4},{2,5},{3,6},{4,7},{5,0},{6,1},{7,2},{8,11},{9,12},{10,... | collective-permute-start | bytes 737288 | tf_op jit(solution)/shard_map/exp_scatter/ppermute | solution.py:15
  164.0 15.0 %collective-permute-start.15 = (bf16[960,128]{1,0:T(8,128)(2,1)S(1)}, bf16[960,128]{1,0:T(8,128)(2,1)S(1)}, u32[]{:S(2)}, u32[]{:S(2)}) collective-permute-start(bf16[960,128]{1,0:T(8,128)(2,1)S(1)} %pad_maximum_fusion.5), channel_id=1, source_target_pairs={{0,5},{1,6},{2,7},{3,0},{4,1},{5,2},{6,3},{7,4},{8,13},{9,14},{10,... | collective-permute-start | bytes 737288 | tf_op jit(solution)/shard_map/exp_scatter/ppermute | solution.py:15
  179.9 35.6 %all-to-all-start.1 = ((bf16[32,30,128]{2,1,0:T(8,128)(2,1)}), bf16[32,30,128]{2,1,0:T(8,128)(2,1)S(1)}, u32[]{:S(2)}, u32[]{:S(2)}) async-start(bf16[32,30,128]{2,1,0:T(8,128)(2,1)} %reshape.26), calls=%async_computation.1 | async-start | bytes 524288 | tf_op jit(solution)/shard_map/all_to_all | solution.py:178
  194.1 22.1 %copy-start.6 = (f32[768]{0:T(1024)S(1)}, f32[768]{0:T(1024)}, u32[]{:S(2)}) copy-start(f32[768]{0:T(1024)} %param.17) | copy-start | bytes 9220
  194.9 21.3 %collective-permute-start.6 = (bf16[768,128]{1,0:T(8,128)(2,1)}, bf16[768,128]{1,0:T(8,128)(2,1)}, u32[]{:S(2)}, u32[]{:S(2)}) collective-permute-start(bf16[768,128]{1,0:T(8,128)(2,1)} %pad_maximum_fusion.6), channel_id=1, source_target_pairs={{0,3},{1,4},{2,5},{3,6},{4,7},{5,0},{6,1},{7,2},{8,11},{9,12},{10,... | collective-permute-start | bytes 589832 | tf_op jit(solution)/shard_map/res_scatter/ppermute | solution.py:15
  201.2 15.0 %collective-permute-start.7 = (bf16[768,128]{1,0:T(8,128)(2,1)}, bf16[768,128]{1,0:T(8,128)(2,1)}, u32[]{:S(2)}, u32[]{:S(2)}) collective-permute-start(bf16[768,128]{1,0:T(8,128)(2,1)} %pad_maximum_fusion.7), channel_id=1, source_target_pairs={{0,5},{1,6},{2,7},{3,0},{4,1},{5,2},{6,3},{7,4},{8,13},{9,14},{10,... | collective-permute-start | bytes 589832 | tf_op jit(solution)/shard_map/res_scatter/ppermute | solution.py:15

commit v3 on v2

--- a/solution.py
+++ b/solution.py
@@ -6,6 +6,7 @@
 from jax.experimental import pallas as pl
 from jax.experimental.pallas import tpu as pltpu
 from jax.sharding import PartitionSpec as P
+
 
 RING = 8
 
@@ -84,7 +85,7 @@
         keep_ref[2, at] = sums_ref[place[5], at]
 
 
-def ffn(me, own, below, above, left, right, gain, w_in, w_out, name):
+def ffn(me, own, below, above, left, right, gain, w_in, w_out):
     count, width = own.shape
     model = RING * width
     vmem = pl.BlockSpec(memory_space=pltpu.VMEM)
@@ -104,7 +105,6 @@
             transcendentals=count * w_in.shape[1],
             bytes_accessed=4 * count * model + 4 * model * w_in.shape[1],
         ),
-        name=name,
     )(me, own, below, above, left, right, gain.reshape(1, model), w_in, w_out)
 
 
@@ -140,56 +140,37 @@
     slot_index = jnp.arange(slots, dtype=jnp.int32)
     send_table = (slot_index[:, None] == slot_id[None, :]).astype(jnp.bfloat16)
     take_table = (slot_id[:, None] == slot_index[None, :]).astype(jnp.bfloat16)
-    outgoing = jnp.dot(send_table, tokens, preferred_element_type=jnp.float32).astype(jnp.bfloat16)
-    incoming = lax.all_to_all(
-        outgoing.reshape(experts, capacity, feat_width),
-        "expert",
-        split_axis=0,
-        concat_axis=0,
-        tiled=True,
-    ).reshape(slots, feat_width)
-    with jax.named_scope("res_gather"):
-        res_below, res_above = gather_far(tokens)
-        res_left, res_right = gather_near(tokens, res_below, res_above)
-    with jax.named_scope("exp_gather"):
-        exp_below, exp_above = gather_far(incoming)
-        exp_left, exp_right = gather_near(incoming, exp_below, exp_above)
+
+    def exchange(rows):
+        return lax.all_to_all(
+            rows.reshape(experts, capacity, feat_width),
+            "expert",
+            split_axis=0,
+            concat_axis=0,
+            tiled=True,
+        ).reshape(slots, feat_width)
+
+    res_below, res_above = gather_far(tokens)
+    outgoing = jnp.dot(send_table, tokens, preferred_element_type=jnp.float32)
+    outgoing = outgoing.astype(jnp.bfloat16)
+    incoming = exchange(outgoing)
+    res_left, res_right = gather_near(tokens, res_below, res_above)
+    exp_below, exp_above = gather_far(incoming)
+    exp_left, exp_right = gather_near(incoming, exp_below, exp_above)
     res_to_right, res_to_left, res_keep = ffn(
-        me, tokens, res_below, res_above, res_left, res_right, gain, w_res_in, w_res_out, "res_ffn"
+        me, tokens, res_below, res_above, res_left, res_right, gain, w_res_in, w_res_out
     )
     exp_to_right, exp_to_left, exp_keep = ffn(
-        me,
-        incoming,
-        exp_below,
-        exp_above,
-        exp_left,
-        exp_right,
-        gain,
-        w_exp_in[0],
-        w_exp_out[0],
-        "exp_ffn",
+        me, incoming, exp_below, exp_above, exp_left, exp_right, gain, w_exp_in[0], w_exp_out[0]
     )
-    with jax.named_scope("exp_scatter"):
-        exp_own, exp_first, exp_second = scatter_far(
-            exp_keep, *scatter_near(exp_to_right, exp_to_left)
-        )
-        summed = exp_own + exp_first.astype(jnp.float32) + exp_second.astype(jnp.float32)
-        summed = summed.astype(jnp.bfloat16)
-    returned = lax.all_to_all(
-        summed.reshape(experts, capacity, feat_width),
-        "expert",
-        split_axis=0,
-        concat_axis=0,
-        tiled=True,
-    )
-    with jax.named_scope("res_scatter"):
-        res_own, res_first, res_second = scatter_far(
-            res_keep, *scatter_near(res_to_right, res_to_left)
-        )
-        res_sum = res_own + res_first.astype(jnp.float32) + res_second.astype(jnp.float32)
-    moe_value = jnp.dot(
-        take_table, returned.reshape(slots, feat_width), preferred_element_type=jnp.float32
-    )
+    exp_edges = scatter_near(exp_to_right, exp_to_left)
+    exp_own, exp_first, exp_second = scatter_far(exp_keep, *exp_edges)
+    summed = exp_own + exp_first.astype(jnp.float32) + exp_second.astype(jnp.float32)
+    returned = exchange(summed.astype(jnp.bfloat16))
+    res_edges = scatter_near(res_to_right, res_to_left)
+    res_own, res_first, res_second = scatter_far(res_keep, *res_edges)
+    res_sum = res_own + res_first.astype(jnp.float32) + res_second.astype(jnp.float32)
+    moe_value = jnp.dot(take_table, returned, preferred_element_type=jnp.float32)
     return (res_sum + gate_prob[:, None] * moe_value).astype(jnp.bfloat16)
 
 

time: 222 us -> 222 us (level)
  no operation moved by 1% of the time
where the time goes in v3:
time: 222 us; the launch traced here: 219 us
  starting transfers between devices  82.9 us (37%)
  blocking collectives  67.1 us (30%)
  waiting for transfers between devices  50.6 us (23%)
  Pallas kernels  7.64 us (3%)
  other arithmetic  4.22 us (2%)
  matrix products  4.12 us (2%)
    ppermute x16, starting transfers between devices, shift(): lax.ppermute(value, axis, [(i, (i + step) % ring) for i in range(ring)])  68.7 us
    all_to_all x1, blocking collectives, exchange(): lax.all_to_all(rows.reshape(experts, capacity, feat_width), 'expert', spl...  67.1 us
    ppermute x16, waiting for transfers between devices, shift(): lax.ppermute(value, axis, [(i, (i + step) % ring) for i in range(ring)])  39.4 us
    all_to_all x1, starting transfers between devices, exchange(): lax.all_to_all(rows.reshape(experts, capacity, feat_width), 'expert', spl...  14.1 us
    all_to_all x1, waiting for transfers between devices, exchange(): lax.all_to_all(rows.reshape(experts, capacity, feat_width), 'expert', spl...  11.1 us
    pallas_call x2, Pallas kernels, ffn(): pl.pallas_call(functools.partial(ffn_body, block=count // 4), in_specs=[p...  7.64 us
  transfers between devices with their start and end apart: 17, of which 7 were waited for; matrix products, arithmetic and copies ran while one was open for 1% of the time, Pallas kernels for 3%

profile of v3, /device:TPU:65, one launch (start us, length us, event | category | flops | bytes accessed | tf_op | source)
XLA Modules:
  0.0 218.8 jit_solution(9550470283204706854)
XLA Ops:
  0.0 0.7 add_select_fusion
  0.7 1.5 fusion.5
  2.3 0.1 reshape.24
  2.3 67.1 %all_to_all.10 = bf16[32,30,128]{2,1,0:T(8,128)(2,1)S(1)} all-to-all(bf16[32,30,128]{2,1,0:T(8,128)(2,1)S(1)} %reshape.24), channel_id=1, replica_groups=mesh['groups'=2,'expert'=32,'mp'=8] {'expert'}, dimensions={0} | all-to-all | bytes 491520 | tf_op jit(solution)/shard_map/all_to_all | solution.py:145
  69.4 0.1 reshape.25.own_ref
  69.5 5.4 %collective-permute-start.8 = (bf16[960,128]{1,0:T(8,128)(2,1)S(1)}, bf16[960,128]{1,0:T(8,128)(2,1)S(1)}, u32[]{:S(2)}, u32[]{:S(2)}) collective-permute-start(bf16[960,128]{1,0:T(8,128)(2,1)S(1)} %reshape.25.own_ref), channel_id=1, source_target_pairs={{0,3},{1,4},{2,5},{3,6},{4,7},{5,0},{6,1},{7,2},{8,11},{9,12},{10,... | collective-permute-start | bytes 737288 | tf_op jit(solution)/shard_map/ppermute | solution.py:16
  74.9 3.5 %collective-permute-start.9 = (bf16[960,128]{1,0:T(8,128)(2,1)S(1)}, bf16[960,128]{1,0:T(8,128)(2,1)S(1)}, u32[]{:S(2)}, u32[]{:S(2)}) collective-permute-start(bf16[960,128]{1,0:T(8,128)(2,1)S(1)} %reshape.25.own_ref), channel_id=1, source_target_pairs={{0,5},{1,6},{2,7},{3,0},{4,1},{5,2},{6,3},{7,4},{8,13},{9,14},{10,... | collective-permute-start | bytes 737288 | tf_op jit(solution)/shard_map/ppermute | solution.py:16
  78.4 13.3 %collective-permute-done.8.below_ref = bf16[960,128]{1,0:T(8,128)(2,1)S(1)} collective-permute-done((bf16[960,128]{1,0:T(8,128)(2,1)S(1)}, bf16[960,128]{1,0:T(8,128)(2,1)S(1)}, u32[]{:S(2)}, u32[]{:S(2)}) %collective-permute-start.8) | collective-permute-done | bytes 245792 | tf_op jit(solution)/shard_map/ppermute | solution.py:16
  91.8 0.0 copy-start
  91.8 0.0 collective-permute-done.9.above_ref
  91.8 1.2 fusion.7
  93.0 10.9 %collective-permute-start.10 = (bf16[2400,128]{1,0:T(8,128)(2,1)}, bf16[2400,128]{1,0:T(8,128)(2,1)}, u32[]{:S(2)}, u32[]{:S(2)}) collective-permute-start(bf16[2400,128]{1,0:T(8,128)(2,1)} %get-tuple-element.22), channel_id=1, source_target_pairs={{0,1},{1,2},{2,3},{3,4},{4,5},{5,6},{6,7},{7,0},{8,9},{9,10},{10,1... | collective-permute-start | bytes 1843208 | tf_op jit(solution)/shard_map/ppermute | solution.py:16
  103.9 2.0 collective-permute-start.11
  105.8 0.0 copy-done
  105.9 2.1 collective-permute-start
  108.0 6.2 %collective-permute-start.1 = (bf16[768,128]{1,0:T(8,128)(2,1)S(1)}, bf16[768,128]{1,0:T(8,128)(2,1)S(1)}, u32[]{:S(2)}, u32[]{:S(2)}) collective-permute-start(bf16[768,128]{1,0:T(8,128)(2,1)S(1)} %copy-done), channel_id=1, source_target_pairs={{0,5},{1,6},{2,7},{3,0},{4,1},{5,2},{6,3},{7,4},{8,13},{9,14},{10,... | collective-permute-start | bytes 589832 | tf_op jit(solution)/shard_map/ppermute | solution.py:16
  114.2 13.4 %collective-permute-done.below_ref = bf16[768,128]{1,0:T(8,128)(2,1)S(1)} collective-permute-done((bf16[768,128]{1,0:T(8,128)(2,1)S(1)}, bf16[768,128]{1,0:T(8,128)(2,1)S(1)}, u32[]{:S(2)}, u32[]{:S(2)}) %collective-permute-start) | collective-permute-done | bytes 196640 | tf_op jit(solution)/shard_map/ppermute | solution.py:16
  127.7 0.0 collective-permute-done.1.above_ref
  127.7 0.1 fusion.9
  127.8 5.2 %collective-permute-start.2 = (bf16[1920,128]{1,0:T(8,128)(2,1)S(1)}, bf16[1920,128]{1,0:T(8,128)(2,1)S(1)}, u32[]{:S(2)}, u32[]{:S(2)}) collective-permute-start(bf16[1920,128]{1,0:T(8,128)(2,1)S(1)} %get-tuple-element.24), channel_id=1, source_target_pairs={{0,1},{1,2},{2,3},{3,4},{4,5},{5,6},{6,7},{7,0},{8,9},{9,10},{10,1... | collective-permute-start | bytes 1474568 | tf_op jit(solution)/shard_map/ppermute | solution.py:16
  133.0 2.7 %collective-permute-start.3 = (bf16[1920,128]{1,0:T(8,128)(2,1)S(1)}, bf16[1920,128]{1,0:T(8,128)(2,1)S(1)}, u32[]{:S(2)}, u32[]{:S(2)}) collective-permute-start(bf16[1920,128]{1,0:T(8,128)(2,1)S(1)} %get-tuple-element.23), channel_id=1, source_target_pairs={{0,7},{1,0},{2,1},{3,2},{4,3},{5,4},{6,5},{7,6},{8,15},{9,8},{10,9... | collective-permute-start | bytes 1474568 | tf_op jit(solution)/shard_map/ppermute | solution.py:16
  135.7 0.0 collective-permute-done.10.left_ref
  135.7 0.0 collective-permute-done.11.right_ref
  135.7 0.0 copy-done.1
  135.7 0.0 copy-start.3
  135.7 0.0 copy-start.4
  135.7 4.8 %shard_map.92 = (bf16[2400,128]{1,0:T(8,128)(2,1)S(1)}, bf16[2400,128]{1,0:T(8,128)(2,1)S(1)}, bf16[3,960,128]{2,1,0:T(8,128)(2,1)S(1)}) custom-call(s32[1]{0:T(128)} %bitcast.me_ref, bf16[960,128]{1,0:T(8,128)(2,1)S(1)} %reshape.25.own_ref, bf16[960,128]{1,0:T(8,128)(2,1)S(1)} %collective-permute-done.8.below_ref, ...), custom_call_target="tpu_custom_call" | custom-call | flops 2013265920 | bytes 6029312 | tf_op jit(solution)/shard_map/pallas_call | solution.py:93
  140.6 2.6 %collective-permute-start.12 = (bf16[2400,128]{1,0:T(8,128)(2,1)S(1)}, bf16[2400,128]{1,0:T(8,128)(2,1)S(1)}, u32[]{:S(2)}, u32[]{:S(2)}) collective-permute-start(bf16[2400,128]{1,0:T(8,128)(2,1)S(1)} %get-tuple-element.15), channel_id=1, source_target_pairs={{0,1},{1,2},{2,3},{3,4},{4,5},{5,6},{6,7},{7,0},{8,9},{9,10},{10,1... | collective-permute-start | bytes 1843208 | tf_op jit(solution)/shard_map/ppermute | solution.py:16
  143.2 4.5 %collective-permute-start.13 = (bf16[2400,128]{1,0:T(8,128)(2,1)S(1)}, bf16[2400,128]{1,0:T(8,128)(2,1)S(1)}, u32[]{:S(2)}, u32[]{:S(2)}) collective-permute-start(bf16[2400,128]{1,0:T(8,128)(2,1)S(1)} %get-tuple-element.16), channel_id=1, source_target_pairs={{0,7},{1,0},{2,1},{3,2},{4,3},{5,4},{6,5},{7,6},{8,15},{9,8},{10,9... | collective-permute-start | bytes 1843208 | tf_op jit(solution)/shard_map/ppermute | solution.py:16
  147.7 0.0 collective-permute-done.2.left_ref
  147.7 0.0 collective-permute-done.3.right_ref
  147.8 2.8 %shard_map.91 = (bf16[1920,128]{1,0:T(8,128)(2,1)S(1)}, bf16[1920,128]{1,0:T(8,128)(2,1)S(1)}, bf16[3,768,128]{2,1,0:T(8,128)(2,1)S(1)}) custom-call(s32[1]{0:T(128)} %bitcast.me_ref, bf16[768,128]{1,0:T(8,128)(2,1)S(1)} %copy-done, bf16[768,128]{1,0:T(8,128)(2,1)S(1)} %collective-permute-done.below_ref, ...), custom_call_target="tpu_custom_call" | custom-call | flops 1610612736 | bytes 5242880 | tf_op jit(solution)/shard_map/pallas_call | solution.py:93
  150.6 2.0 collective-permute-start.4
  152.5 4.6 %collective-permute-start.5 = (bf16[1920,128]{1,0:T(8,128)(2,1)S(1)}, bf16[1920,128]{1,0:T(8,128)(2,1)S(1)}, u32[]{:S(2)}, u32[]{:S(2)}) collective-permute-start(bf16[1920,128]{1,0:T(8,128)(2,1)S(1)} %get-tuple-element.13), channel_id=1, source_target_pairs={{0,7},{1,0},{2,1},{3,2},{4,3},{5,4},{6,5},{7,6},{8,15},{9,8},{10,9... | collective-permute-start | bytes 1474568 | tf_op jit(solution)/shard_map/ppermute | solution.py:16
  157.2 0.1 convert_element_type.51
  157.3 0.0 collective-permute-done.12
  157.3 0.1 convert_element_type.52
  157.4 0.0 collective-permute-done.13
  157.4 0.1 convert_element_type.53
  157.5 0.1 slice_add_fusion.1
  157.6 0.1 fusion.17
  157.7 6.3 %collective-permute-start.14 = (bf16[960,128]{1,0:T(8,128)(2,1)S(1)}, bf16[960,128]{1,0:T(8,128)(2,1)S(1)}, u32[]{:S(2)}, u32[]{:S(2)}) collective-permute-start(bf16[960,128]{1,0:T(8,128)(2,1)S(1)} %pad_maximum_fusion.4), channel_id=1, source_target_pairs={{0,3},{1,4},{2,5},{3,6},{4,7},{5,0},{6,1},{7,2},{8,11},{9,12},{10,... | collective-permute-start | bytes 737288 | tf_op jit(solution)/shard_map/ppermute | solution.py:16
  164.0 2.1 collective-permute-start.15
  166.1 0.1 convert_element_type.45
  166.2 0.8 collective-permute-done.4
  167.0 0.1 convert_element_type.46
  167.0 2.7 %collective-permute-done.5 = bf16[1920,128]{1,0:T(8,128)(2,1)S(1)} collective-permute-done((bf16[1920,128]{1,0:T(8,128)(2,1)S(1)}, bf16[1920,128]{1,0:T(8,128)(2,1)S(1)}, u32[]{:S(2)}, u32[]{:S(2)}) %collective-permute-start.5) | collective-permute-done | bytes 491552 | tf_op jit(solution)/shard_map/ppermute | solution.py:16
  169.8 0.1 convert_element_type.47
  169.8 8.9 %collective-permute-done.14 = bf16[960,128]{1,0:T(8,128)(2,1)S(1)} collective-permute-done((bf16[960,128]{1,0:T(8,128)(2,1)S(1)}, bf16[960,128]{1,0:T(8,128)(2,1)S(1)}, u32[]{:S(2)}, u32[]{:S(2)}) %collective-permute-start.14) | collective-permute-done | bytes 245792 | tf_op jit(solution)/shard_map/ppermute | solution.py:16
  178.7 0.3 collective-permute-done.15
  179.0 0.1 fusion.12
  179.1 0.8 reshape.26
  179.9 14.1 %all-to-all-start.1 = ((bf16[32,30,128]{2,1,0:T(8,128)(2,1)}), bf16[32,30,128]{2,1,0:T(8,128)(2,1)S(1)}, u32[]{:S(2)}, u32[]{:S(2)}) async-start(bf16[32,30,128]{2,1,0:T(8,128)(2,1)} %reshape.26), calls=%async_computation.1 | async-start | bytes 524288 | tf_op jit(solution)/shard_map/all_to_all | solution.py:145
  194.0 0.1 slice_add_fusion.5
  194.1 0.0 copy-start.6
  194.2 0.7 pad_maximum_fusion.6
  194.9 5.6 %collective-permute-start.6 = (bf16[768,128]{1,0:T(8,128)(2,1)}, bf16[768,128]{1,0:T(8,128)(2,1)}, u32[]{:S(2)}, u32[]{:S(2)}) collective-permute-start(bf16[768,128]{1,0:T(8,128)(2,1)} %pad_maximum_fusion.6), channel_id=1, source_target_pairs={{0,3},{1,4},{2,5},{3,6},{4,7},{5,0},{6,1},{7,2},{8,11},{9,12},{10,... | collective-permute-start | bytes 589832 | tf_op jit(solution)/shard_map/ppermute | solution.py:16
  200.5 0.7 pad_maximum_fusion.7
  201.2 3.1 %collective-permute-start.7 = (bf16[768,128]{1,0:T(8,128)(2,1)}, bf16[768,128]{1,0:T(8,128)(2,1)}, u32[]{:S(2)}, u32[]{:S(2)}) collective-permute-start(bf16[768,128]{1,0:T(8,128)(2,1)} %pad_maximum_fusion.7), channel_id=1, source_target_pairs={{0,5},{1,6},{2,7},{3,0},{4,1},{5,2},{6,3},{7,4},{8,13},{9,14},{10,... | collective-permute-start | bytes 589832 | tf_op jit(solution)/shard_map/ppermute | solution.py:16
  204.3 11.1 %all-to-all-done.1 = bf16[32,30,128]{2,1,0:T(8,128)(2,1)S(1)} async-done(((bf16[32,30,128]{2,1,0:T(8,128)(2,1)}), bf16[32,30,128]{2,1,0:T(8,128)(2,1)S(1)}, u32[]{:S(2)}, u32[]{:S(2)}) %all-to-all-start.1) | async-done | bytes 245792 | tf_op jit(solution)/shard_map/all_to_all | solution.py:145
  215.4 0.8 reshape.27
  216.2 0.0 collective-permute-done.6
  216.2 0.0 collective-permute-done.7
  216.2 2.6 %fusion.16 = bf16[768,128]{1,0:T(8,128)(2,1)} fusion(f32[1920,128]{1,0:T(8,128)S(1)} %convert_element_type.47, f32[1920,128]{1,0:T(8,128)S(1)} %convert_element_type.46, f32[3,768,128]{2,1,0:T(8,128)S(1)} %convert_element_type.45, bf16[768,128]{1,0:T(8,128)(2,1)} %collective-permute-done.7, bf16[768,128]{1,0:T(8,128)(2,1)} %collective-permute-done.6, ...), kind=kOutput, calls=%fused_computation.34 | convolution fusion | flops 190365696 | bytes 2021376 | tf_op jit(solution)/shard_map/dot_general | solution.py:173
  (19 shorter events, 0.2 us)
Async XLA Ops:
  69.5 22.3 %collective-permute-start.8 = (bf16[960,128]{1,0:T(8,128)(2,1)S(1)}, bf16[960,128]{1,0:T(8,128)(2,1)S(1)}, u32[]{:S(2)}, u32[]{:S(2)}) collective-permute-start(bf16[960,128]{1,0:T(8,128)(2,1)S(1)} %reshape.25.own_ref), channel_id=1, source_target_pairs={{0,3},{1,4},{2,5},{3,6},{4,7},{5,0},{6,1},{7,2},{8,11},{9,12},{10,... | collective-permute-start | bytes 737288 | tf_op jit(solution)/shard_map/ppermute | solution.py:16
  74.9 16.9 %collective-permute-start.9 = (bf16[960,128]{1,0:T(8,128)(2,1)S(1)}, bf16[960,128]{1,0:T(8,128)(2,1)S(1)}, u32[]{:S(2)}, u32[]{:S(2)}) collective-permute-start(bf16[960,128]{1,0:T(8,128)(2,1)S(1)} %reshape.25.own_ref), channel_id=1, source_target_pairs={{0,5},{1,6},{2,7},{3,0},{4,1},{5,2},{6,3},{7,4},{8,13},{9,14},{10,... | collective-permute-start | bytes 737288 | tf_op jit(solution)/shard_map/ppermute | solution.py:16
  91.8 14.1 %copy-start = (bf16[768,128]{1,0:T(8,128)(2,1)S(1)}, bf16[768,128]{1,0:T(8,128)(2,1)}, u32[]{:S(2)}) copy-start(bf16[768,128]{1,0:T(8,128)(2,1)} %own_ref.1) | copy-start | bytes 589828
  93.0 42.7 %copy-start.1 = (bf16[1,1024,512]{2,1,0:T(8,128)(2,1)S(1)}, bf16[1,1024,512]{2,1,0:T(8,128)(2,1)}, u32[]{:S(2)}) copy-start(bf16[1,1024,512]{2,1,0:T(8,128)(2,1)} %param.13) | copy-start | bytes 3145732
  93.0 42.7 %copy-start.2 = (bf16[1,512,1024]{2,1,0:T(8,128)(2,1)S(1)}, bf16[1,512,1024]{2,1,0:T(8,128)(2,1)}, u32[]{:S(2)}) copy-start(bf16[1,512,1024]{2,1,0:T(8,128)(2,1)} %param.14) | copy-start | bytes 3145732
  93.0 42.8 %copy-start.5 = (f32[1024]{0:T(1024)S(1)}, f32[1024]{0:T(1024)}, u32[]{:S(2)}) copy-start(f32[1024]{0:T(1024)} %param.10) | copy-start | bytes 12292
  93.0 42.7 %collective-permute-start.10 = (bf16[2400,128]{1,0:T(8,128)(2,1)}, bf16[2400,128]{1,0:T(8,128)(2,1)}, u32[]{:S(2)}, u32[]{:S(2)}) collective-permute-start(bf16[2400,128]{1,0:T(8,128)(2,1)} %get-tuple-element.22), channel_id=1, source_target_pairs={{0,1},{1,2},{2,3},{3,4},{4,5},{5,6},{6,7},{7,0},{8,9},{9,10},{10,1... | collective-permute-start | bytes 1843208 | tf_op jit(solution)/shard_map/ppermute | solution.py:16
  103.9 31.8 %collective-permute-start.11 = (bf16[2400,128]{1,0:T(8,128)(2,1)}, bf16[2400,128]{1,0:T(8,128)(2,1)}, u32[]{:S(2)}, u32[]{:S(2)}) collective-permute-start(bf16[2400,128]{1,0:T(8,128)(2,1)} %get-tuple-element.21), channel_id=1, source_target_pairs={{0,7},{1,0},{2,1},{3,2},{4,3},{5,4},{6,5},{7,6},{8,15},{9,8},{10,9... | collective-permute-start | bytes 1843208 | tf_op jit(solution)/shard_map/ppermute | solution.py:16
  105.9 21.8 %collective-permute-start = (bf16[768,128]{1,0:T(8,128)(2,1)S(1)}, bf16[768,128]{1,0:T(8,128)(2,1)S(1)}, u32[]{:S(2)}, u32[]{:S(2)}) collective-permute-start(bf16[768,128]{1,0:T(8,128)(2,1)S(1)} %copy-done), channel_id=1, source_target_pairs={{0,3},{1,4},{2,5},{3,6},{4,7},{5,0},{6,1},{7,2},{8,11},{9,12},{10,... | collective-permute-start | bytes 589832 | tf_op jit(solution)/shard_map/ppermute | solution.py:16
  108.0 19.7 %collective-permute-start.1 = (bf16[768,128]{1,0:T(8,128)(2,1)S(1)}, bf16[768,128]{1,0:T(8,128)(2,1)S(1)}, u32[]{:S(2)}, u32[]{:S(2)}) collective-permute-start(bf16[768,128]{1,0:T(8,128)(2,1)S(1)} %copy-done), channel_id=1, source_target_pairs={{0,5},{1,6},{2,7},{3,0},{4,1},{5,2},{6,3},{7,4},{8,13},{9,14},{10,... | collective-permute-start | bytes 589832 | tf_op jit(solution)/shard_map/ppermute | solution.py:16
  127.8 19.9 %collective-permute-start.2 = (bf16[1920,128]{1,0:T(8,128)(2,1)S(1)}, bf16[1920,128]{1,0:T(8,128)(2,1)S(1)}, u32[]{:S(2)}, u32[]{:S(2)}) collective-permute-start(bf16[1920,128]{1,0:T(8,128)(2,1)S(1)} %get-tuple-element.24), channel_id=1, source_target_pairs={{0,1},{1,2},{2,3},{3,4},{4,5},{5,6},{6,7},{7,0},{8,9},{9,10},{10,1... | collective-permute-start | bytes 1474568 | tf_op jit(solution)/shard_map/ppermute | solution.py:16
  133.0 14.8 %collective-permute-start.3 = (bf16[1920,128]{1,0:T(8,128)(2,1)S(1)}, bf16[1920,128]{1,0:T(8,128)(2,1)S(1)}, u32[]{:S(2)}, u32[]{:S(2)}) collective-permute-start(bf16[1920,128]{1,0:T(8,128)(2,1)S(1)} %get-tuple-element.23), channel_id=1, source_target_pairs={{0,7},{1,0},{2,1},{3,2},{4,3},{5,4},{6,5},{7,6},{8,15},{9,8},{10,9... | collective-permute-start | bytes 1474568 | tf_op jit(solution)/shard_map/ppermute | solution.py:16
  135.7 12.0 %copy-start.3 = (bf16[1024,512]{1,0:T(8,128)(2,1)S(1)}, bf16[1024,512]{1,0:T(8,128)(2,1)}, u32[]{:S(2)}) copy-start(bf16[1024,512]{1,0:T(8,128)(2,1)} %w_in_ref.1) | copy-start | bytes 3145732
  135.7 12.0 %copy-start.4 = (bf16[512,1024]{1,0:T(8,128)(2,1)S(1)}, bf16[512,1024]{1,0:T(8,128)(2,1)}, u32[]{:S(2)}) copy-start(bf16[512,1024]{1,0:T(8,128)(2,1)} %w_out_ref.1) | copy-start | bytes 3145732
  140.6 16.7 %collective-permute-start.12 = (bf16[2400,128]{1,0:T(8,128)(2,1)S(1)}, bf16[2400,128]{1,0:T(8,128)(2,1)S(1)}, u32[]{:S(2)}, u32[]{:S(2)}) collective-permute-start(bf16[2400,128]{1,0:T(8,128)(2,1)S(1)} %get-tuple-element.15), channel_id=1, source_target_pairs={{0,1},{1,2},{2,3},{3,4},{4,5},{5,6},{6,7},{7,0},{8,9},{9,10},{10,1... | collective-permute-start | bytes 1843208 | tf_op jit(solution)/shard_map/ppermute | solution.py:16
  143.2 14.2 %collective-permute-start.13 = (bf16[2400,128]{1,0:T(8,128)(2,1)S(1)}, bf16[2400,128]{1,0:T(8,128)(2,1)S(1)}, u32[]{:S(2)}, u32[]{:S(2)}) collective-permute-start(bf16[2400,128]{1,0:T(8,128)(2,1)S(1)} %get-tuple-element.16), channel_id=1, source_target_pairs={{0,7},{1,0},{2,1},{3,2},{4,3},{5,4},{6,5},{7,6},{8,15},{9,8},{10,9... | collective-permute-start | bytes 1843208 | tf_op jit(solution)/shard_map/ppermute | solution.py:16
  150.6 16.4 %collective-permute-start.4 = (bf16[1920,128]{1,0:T(8,128)(2,1)S(1)}, bf16[1920,128]{1,0:T(8,128)(2,1)S(1)}, u32[]{:S(2)}, u32[]{:S(2)}) collective-permute-start(bf16[1920,128]{1,0:T(8,128)(2,1)S(1)} %get-tuple-element.12), channel_id=1, source_target_pairs={{0,1},{1,2},{2,3},{3,4},{4,5},{5,6},{6,7},{7,0},{8,9},{9,10},{10,1... | collective-permute-start | bytes 1474568 | tf_op jit(solution)/shard_map/ppermute | solution.py:16
  152.5 17.2 %collective-permute-start.5 = (bf16[1920,128]{1,0:T(8,128)(2,1)S(1)}, bf16[1920,128]{1,0:T(8,128)(2,1)S(1)}, u32[]{:S(2)}, u32[]{:S(2)}) collective-permute-start(bf16[1920,128]{1,0:T(8,128)(2,1)S(1)} %get-tuple-element.13), channel_id=1, source_target_pairs={{0,7},{1,0},{2,1},{3,2},{4,3},{5,4},{6,5},{7,6},{8,15},{9,8},{10,9... | collective-permute-start | bytes 1474568 | tf_op jit(solution)/shard_map/ppermute | solution.py:16
  157.7 21.0 %collective-permute-start.14 = (bf16[960,128]{1,0:T(8,128)(2,1)S(1)}, bf16[960,128]{1,0:T(8,128)(2,1)S(1)}, u32[]{:S(2)}, u32[]{:S(2)}) collective-permute-start(bf16[960,128]{1,0:T(8,128)(2,1)S(1)} %pad_maximum_fusion.4), channel_id=1, source_target_pairs={{0,3},{1,4},{2,5},{3,6},{4,7},{5,0},{6,1},{7,2},{8,11},{9,12},{10,... | collective-permute-start | bytes 737288 | tf_op jit(solution)/shard_map/ppermute | solution.py:16
  164.0 15.0 %collective-permute-start.15 = (bf16[960,128]{1,0:T(8,128)(2,1)S(1)}, bf16[960,128]{1,0:T(8,128)(2,1)S(1)}, u32[]{:S(2)}, u32[]{:S(2)}) collective-permute-start(bf16[960,128]{1,0:T(8,128)(2,1)S(1)} %pad_maximum_fusion.5), channel_id=1, source_target_pairs={{0,5},{1,6},{2,7},{3,0},{4,1},{5,2},{6,3},{7,4},{8,13},{9,14},{10,... | collective-permute-start | bytes 737288 | tf_op jit(solution)/shard_map/ppermute | solution.py:16
  179.9 35.6 %all-to-all-start.1 = ((bf16[32,30,128]{2,1,0:T(8,128)(2,1)}), bf16[32,30,128]{2,1,0:T(8,128)(2,1)S(1)}, u32[]{:S(2)}, u32[]{:S(2)}) async-start(bf16[32,30,128]{2,1,0:T(8,128)(2,1)} %reshape.26), calls=%async_computation.1 | async-start | bytes 524288 | tf_op jit(solution)/shard_map/all_to_all | solution.py:145
  194.1 22.1 %copy-start.6 = (f32[768]{0:T(1024)S(1)}, f32[768]{0:T(1024)}, u32[]{:S(2)}) copy-start(f32[768]{0:T(1024)} %param.17) | copy-start | bytes 9220
  194.9 21.3 %collective-permute-start.6 = (bf16[768,128]{1,0:T(8,128)(2,1)}, bf16[768,128]{1,0:T(8,128)(2,1)}, u32[]{:S(2)}, u32[]{:S(2)}) collective-permute-start(bf16[768,128]{1,0:T(8,128)(2,1)} %pad_maximum_fusion.6), channel_id=1, source_target_pairs={{0,3},{1,4},{2,5},{3,6},{4,7},{5,0},{6,1},{7,2},{8,11},{9,12},{10,... | collective-permute-start | bytes 589832 | tf_op jit(solution)/shard_map/ppermute | solution.py:16
  201.2 15.0 %collective-permute-start.7 = (bf16[768,128]{1,0:T(8,128)(2,1)}, bf16[768,128]{1,0:T(8,128)(2,1)}, u32[]{:S(2)}, u32[]{:S(2)}) collective-permute-start(bf16[768,128]{1,0:T(8,128)(2,1)} %pad_maximum_fusion.7), channel_id=1, source_target_pairs={{0,5},{1,6},{2,7},{3,0},{4,1},{5,2},{6,3},{7,4},{8,13},{9,14},{10,... | collective-permute-start | bytes 589832 | tf_op jit(solution)/shard_map/ppermute | solution.py:16

commit v4 on v3

--- a/solution.py
+++ b/solution.py
@@ -8,6 +8,7 @@
 from jax.sharding import PartitionSpec as P
 
 
+CHUNKS = 2
 RING = 8
 
 
@@ -150,23 +151,31 @@
             tiled=True,
         ).reshape(slots, feat_width)
 
-    res_below, res_above = gather_far(tokens)
+    res_below = shift(tokens, 3)
     outgoing = jnp.dot(send_table, tokens, preferred_element_type=jnp.float32)
     outgoing = outgoing.astype(jnp.bfloat16)
     incoming = exchange(outgoing)
+    res_above = shift(tokens, -3)
     res_left, res_right = gather_near(tokens, res_below, res_above)
-    exp_below, exp_above = gather_far(incoming)
-    exp_left, exp_right = gather_near(incoming, exp_below, exp_above)
     res_to_right, res_to_left, res_keep = ffn(
         me, tokens, res_below, res_above, res_left, res_right, gain, w_res_in, w_res_out
     )
-    exp_to_right, exp_to_left, exp_keep = ffn(
-        me, incoming, exp_below, exp_above, exp_left, exp_right, gain, w_exp_in[0], w_exp_out[0]
-    )
-    exp_edges = scatter_near(exp_to_right, exp_to_left)
-    exp_own, exp_first, exp_second = scatter_far(exp_keep, *exp_edges)
-    summed = exp_own + exp_first.astype(jnp.float32) + exp_second.astype(jnp.float32)
-    returned = exchange(summed.astype(jnp.bfloat16))
+
+    chunk = slots // CHUNKS
+    summed = []
+    for c in range(CHUNKS):
+        rows = incoming[c * chunk : (c + 1) * chunk]
+        below, above = gather_far(rows)
+        left, right = gather_near(rows, below, above)
+        to_right, to_left, keep = ffn(
+            me, rows, below, above, left, right, gain, w_exp_in[0], w_exp_out[0]
+        )
+        edges = scatter_near(to_right, to_left)
+        own, first, second = scatter_far(keep, *edges)
+        own = own + first.astype(jnp.float32) + second.astype(jnp.float32)
+        summed.append(own.astype(jnp.bfloat16))
+
+    returned = exchange(jnp.concatenate(summed, axis=0))
     res_edges = scatter_near(res_to_right, res_to_left)
     res_own, res_first, res_second = scatter_far(res_keep, *res_edges)
     res_sum = res_own + res_first.astype(jnp.float32) + res_second.astype(jnp.float32)

time: 222 us -> 224 us (level)
  blocking collectives: 67.1 us -> 0 us
  starting transfers between devices: 82.9 us -> 146 us
  other arithmetic: 4.22 us -> 7.97 us
  local copies, waits for them, and re-layouts: 1.8 us -> 4.87 us
  waiting for transfers between devices: 50.6 us -> 47.8 us
  Pallas kernels: 7.64 us -> 9.99 us
    all_to_all x1 -> x0, blocking collectives: 67.1 us -> none  [exchange(): lax.all_to_all(rows.reshape(experts, capacity, feat_width), 'expert', spl...]
    all_to_all x1 -> x2, starting transfers between devices: 14.1 us -> 63.8 us  [exchange(): lax.all_to_all(rows.reshape(experts, capacity, feat_width), 'expert', spl...]
    ppermute x16 -> x24, starting transfers between devices: 68.7 us -> 82.7 us  [shift(): lax.ppermute(value, axis, [(i, (i + step) % ring) for i in range(ring)])]
    unnamed x14 -> x22, local copies, waits for them, and re-layouts: 0.04 us -> 3.07 us
    ppermute x16 -> x24, waiting for transfers between devices: 39.4 us -> 37 us  [shift(): lax.ppermute(value, axis, [(i, (i + step) % ring) for i in range(ring)])]
    pallas_call x2 -> x3, Pallas kernels: 7.64 us -> 9.99 us  [ffn(): pl.pallas_call(functools.partial(ffn_body, block=count // 4), in_specs=[p...]
    all_to_all x1 -> x2, waiting for transfers between devices: 11.1 us -> 10.8 us  [exchange(): lax.all_to_all(rows.reshape(experts, capacity, feat_width), 'expert', spl...]
  transfers between devices with their start and end apart: 17 -> 26, of which waited for: 7 -> 8; matrix products, arithmetic and copies ran while one was open for 1% -> 3% of each run, Pallas kernels for 3% -> 5%
where the time goes in v4:
time: 224 us; the launch traced here: 220 us
  starting transfers between devices  146 us (65%)
  waiting for transfers between devices  47.8 us (21%)
  Pallas kernels  9.99 us (4%)
  other arithmetic  7.97 us (4%)
  local copies, waits for them, and re-layouts  4.87 us (2%)
  matrix products  2.32 us (1%)
    ppermute x24, starting transfers between devices, shift(): lax.ppermute(value, axis, [(i, (i + step) % ring) for i in range(ring)])  82.7 us
    all_to_all x2, starting transfers between devices, exchange(): lax.all_to_all(rows.reshape(experts, capacity, feat_width), 'expert', spl...  63.8 us
    ppermute x24, waiting for transfers between devices, shift(): lax.ppermute(value, axis, [(i, (i + step) % ring) for i in range(ring)])  37 us
    all_to_all x2, waiting for transfers between devices, exchange(): lax.all_to_all(rows.reshape(experts, capacity, feat_width), 'expert', spl...  10.8 us
    pallas_call x3, Pallas kernels, ffn(): pl.pallas_call(functools.partial(ffn_body, block=count // 4), in_specs=[p...  9.99 us
  transfers between devices with their start and end apart: 26, of which 8 were waited for; matrix products, arithmetic and copies ran while one was open for 3% of the time, Pallas kernels for 5%

profile of v4, /device:TPU:65, one launch (start us, length us, event | category | flops | bytes accessed | tf_op | source)
XLA Modules:
  0.0 220.1 jit_solution(17291163725291248489)
XLA Ops:
  0.0 0.7 add_select_fusion
  0.7 1.6 fusion.5
  2.3 0.8 reshape.25
  3.1 45.2 %all-to-all-start = ((bf16[32,30,128]{2,1,0:T(8,128)(2,1)}), bf16[32,30,128]{2,1,0:T(8,128)(2,1)S(1)}, u32[]{:S(2)}, u32[]{:S(2)}) async-start(bf16[32,30,128]{2,1,0:T(8,128)(2,1)} %reshape.25), calls=%async_computation | async-start | bytes 524288 | tf_op jit(solution)/shard_map/all_to_all | solution.py:146
  48.3 6.9 %collective-permute-start.1 = (bf16[768,128]{1,0:T(8,128)(2,1)S(1)}, bf16[768,128]{1,0:T(8,128)(2,1)S(1)}, u32[]{:S(2)}, u32[]{:S(2)}) collective-permute-start(bf16[768,128]{1,0:T(8,128)(2,1)S(1)} %copy-done), channel_id=1, source_target_pairs={{0,5},{1,6},{2,7},{3,0},{4,1},{5,2},{6,3},{7,4},{8,13},{9,14},{10,... | collective-permute-start | bytes 589832 | tf_op jit(solution)/shard_map/ppermute | solution.py:17
  55.2 2.0 collective-permute-start
  57.2 10.4 %collective-permute-done.1.above_ref = bf16[768,128]{1,0:T(8,128)(2,1)S(1)} collective-permute-done((bf16[768,128]{1,0:T(8,128)(2,1)S(1)}, bf16[768,128]{1,0:T(8,128)(2,1)S(1)}, u32[]{:S(2)}, u32[]{:S(2)}) %collective-permute-start.1) | collective-permute-done | bytes 196640 | tf_op jit(solution)/shard_map/ppermute | solution.py:17
  67.6 7.4 %collective-permute-done.below_ref = bf16[768,128]{1,0:T(8,128)(2,1)S(1)} collective-permute-done((bf16[768,128]{1,0:T(8,128)(2,1)S(1)}, bf16[768,128]{1,0:T(8,128)(2,1)S(1)}, u32[]{:S(2)}, u32[]{:S(2)}) %collective-permute-start) | collective-permute-done | bytes 196640 | tf_op jit(solution)/shard_map/ppermute | solution.py:17
  75.0 0.0 all-to-all-done
  75.1 2.6 %collective-permute-start.9 = (bf16[480,128]{1,0:T(8,128)(2,1)S(1)}, bf16[480,128]{1,0:T(8,128)(2,1)S(1)}, u32[]{:S(2)}, u32[]{:S(2)}) collective-permute-start(bf16[480,128]{1,0:T(8,128)(2,1)S(1)} %slice.169.own_ref), channel_id=1, source_target_pairs={{0,5},{1,6},{2,7},{3,0},{4,1},{5,2},{6,3},{7,4},{8,13},{9,14},{10,... | collective-permute-start | bytes 368648 | tf_op jit(solution)/shard_map/ppermute | solution.py:17
  77.7 4.6 %collective-permute-start.8 = (bf16[480,128]{1,0:T(8,128)(2,1)S(1)}, bf16[480,128]{1,0:T(8,128)(2,1)S(1)}, u32[]{:S(2)}, u32[]{:S(2)}) collective-permute-start(bf16[480,128]{1,0:T(8,128)(2,1)S(1)} %slice.169.own_ref), channel_id=1, source_target_pairs={{0,3},{1,4},{2,5},{3,6},{4,7},{5,0},{6,1},{7,2},{8,11},{9,12},{10,... | collective-permute-start | bytes 368648 | tf_op jit(solution)/shard_map/ppermute | solution.py:17
  82.2 1.1 fusion.7
  83.3 2.0 collective-permute-start.3
  85.4 3.3 %collective-permute-start.2 = (bf16[1920,128]{1,0:T(8,128)(2,1)}, bf16[1920,128]{1,0:T(8,128)(2,1)}, u32[]{:S(2)}, u32[]{:S(2)}) collective-permute-start(bf16[1920,128]{1,0:T(8,128)(2,1)} %get-tuple-element.32), channel_id=1, source_target_pairs={{0,1},{1,2},{2,3},{3,4},{4,5},{5,6},{6,7},{7,0},{8,9},{9,10},{10,1... | collective-permute-start | bytes 1474568 | tf_op jit(solution)/shard_map/ppermute | solution.py:17
  88.7 3.8 %collective-permute-start.17 = (bf16[480,128]{1,0:T(8,128)(2,1)S(1)}, bf16[480,128]{1,0:T(8,128)(2,1)S(1)}, u32[]{:S(2)}, u32[]{:S(2)}) collective-permute-start(bf16[480,128]{1,0:T(8,128)(2,1)S(1)} %slice.186.own_ref), channel_id=1, source_target_pairs={{0,5},{1,6},{2,7},{3,0},{4,1},{5,2},{6,3},{7,4},{8,13},{9,14},{10,... | collective-permute-start | bytes 368648 | tf_op jit(solution)/shard_map/ppermute | solution.py:17
  92.5 3.3 %collective-permute-start.16 = (bf16[480,128]{1,0:T(8,128)(2,1)S(1)}, bf16[480,128]{1,0:T(8,128)(2,1)S(1)}, u32[]{:S(2)}, u32[]{:S(2)}) collective-permute-start(bf16[480,128]{1,0:T(8,128)(2,1)S(1)} %slice.186.own_ref), channel_id=1, source_target_pairs={{0,3},{1,4},{2,5},{3,6},{4,7},{5,0},{6,1},{7,2},{8,11},{9,12},{10,... | collective-permute-start | bytes 368648 | tf_op jit(solution)/shard_map/ppermute | solution.py:17
  95.9 0.0 copy-start.3
  95.9 0.0 copy-start.8
  95.9 0.9 fusion.15
  96.8 4.5 %collective-permute-start.11 = (bf16[1200,128]{1,0:T(8,128)(2,1)}, bf16[1200,128]{1,0:T(8,128)(2,1)S(1)}, u32[]{:S(2)}, u32[]{:S(2)}) collective-permute-start(bf16[1200,128]{1,0:T(8,128)(2,1)} %get-tuple-element.33), channel_id=1, source_target_pairs={{0,7},{1,0},{2,1},{3,2},{4,3},{5,4},{6,5},{7,6},{8,15},{9,8},{10,9... | collective-permute-start | bytes 921608 | tf_op jit(solution)/shard_map/ppermute | solution.py:17
  101.3 5.1 %collective-permute-done.17.above_ref = bf16[480,128]{1,0:T(8,128)(2,1)S(1)} collective-permute-done((bf16[480,128]{1,0:T(8,128)(2,1)S(1)}, bf16[480,128]{1,0:T(8,128)(2,1)S(1)}, u32[]{:S(2)}, u32[]{:S(2)}) %collective-permute-start.17) | collective-permute-done | bytes 122912 | tf_op jit(solution)/shard_map/ppermute | solution.py:17
  106.4 1.9 collective-permute-start.10
  108.4 4.6 %collective-permute-start.19 = (bf16[1200,128]{1,0:T(8,128)(2,1)S(1)}, bf16[1200,128]{1,0:T(8,128)(2,1)S(1)}, u32[]{:S(2)}, u32[]{:S(2)}) collective-permute-start(bf16[1200,128]{1,0:T(8,128)(2,1)S(1)} %get-tuple-element.35), channel_id=1, source_target_pairs={{0,7},{1,0},{2,1},{3,2},{4,3},{5,4},{6,5},{7,6},{8,15},{9,8},{10,9... | collective-permute-start | bytes 921608 | tf_op jit(solution)/shard_map/ppermute | solution.py:17
  113.0 0.0 collective-permute-done.11.right_ref
  113.1 2.1 collective-permute-start.18
  115.2 2.6 %collective-permute-done.10.left_ref = bf16[1200,128]{1,0:T(8,128)(2,1)} collective-permute-done((bf16[1200,128]{1,0:T(8,128)(2,1)}, bf16[1200,128]{1,0:T(8,128)(2,1)}, u32[]{:S(2)}, u32[]{:S(2)}) %collective-permute-start.10) | collective-permute-done | bytes 307232 | tf_op jit(solution)/shard_map/ppermute | solution.py:17
  117.8 1.2 copy-done.4
  119.0 3.2 %shard_map.92 = (bf16[1200,128]{1,0:T(8,128)(2,1)S(1)}, bf16[1200,128]{1,0:T(8,128)(2,1)S(1)}, bf16[3,480,128]{2,1,0:T(8,128)(2,1)S(1)}) custom-call(s32[1]{0:T(128)} %bitcast.me_ref, bf16[480,128]{1,0:T(8,128)(2,1)S(1)} %slice.169.own_ref, bf16[480,128]{1,0:T(8,128)(2,1)S(1)} %collective-permute-done.8.below_ref, ...), custom_call_target="tpu_custom_call" | custom-call | flops 1006632960 | bytes 4063232 | tf_op jit(solution)/shard_map/pallas_call | solution.py:94
  122.3 2.0 collective-permute-start.12
  124.2 0.8 copy-done.6
  125.0 4.7 %collective-permute-start.13 = (bf16[1200,128]{1,0:T(8,128)(2,1)S(1)}, bf16[1200,128]{1,0:T(8,128)(2,1)S(1)}, u32[]{:S(2)}, u32[]{:S(2)}) collective-permute-start(bf16[1200,128]{1,0:T(8,128)(2,1)S(1)} %get-tuple-element.19), channel_id=1, source_target_pairs={{0,7},{1,0},{2,1},{3,2},{4,3},{5,4},{6,5},{7,6},{8,15},{9,8},{10,9... | collective-permute-start | bytes 921608 | tf_op jit(solution)/shard_map/ppermute | solution.py:17
  129.8 1.0 copy-done.7
  130.8 4.6 %shard_map.91 = (bf16[1920,128]{1,0:T(8,128)(2,1)}, bf16[1920,128]{1,0:T(8,128)(2,1)S(1)}, bf16[3,768,128]{2,1,0:T(8,128)(2,1)S(1)}) custom-call(s32[1]{0:T(128)} %bitcast.me_ref, bf16[768,128]{1,0:T(8,128)(2,1)S(1)} %copy-done, bf16[768,128]{1,0:T(8,128)(2,1)S(1)} %collective-permute-done.below_ref, bf16[768,128]{1,0:T(8,128)(2,1)S(1)} %collective-permute-done.1.above_ref, ...), custom_call_target="tpu_custom_call" | custom-call | flops 1610612736 | bytes 5242880 | tf_op jit(solution)/shard_map/pallas_call | solution.py:94
  135.4 1.9 collective-permute-start.4
  137.4 0.1 convert_element_type.71
  137.4 4.6 %collective-permute-start.5 = (bf16[1920,128]{1,0:T(8,128)(2,1)S(1)}, bf16[1920,128]{1,0:T(8,128)(2,1)}, u32[]{:S(2)}, u32[]{:S(2)}) collective-permute-start(bf16[1920,128]{1,0:T(8,128)(2,1)S(1)} %get-tuple-element.16), channel_id=1, source_target_pairs={{0,7},{1,0},{2,1},{3,2},{4,3},{5,4},{6,5},{7,6},{8,15},{9,8},{10,9... | collective-permute-start | bytes 1474568 | tf_op jit(solution)/shard_map/ppermute | solution.py:17
  142.1 2.1 shard_map.93
  144.2 2.0 collective-permute-start.20
  146.2 0.1 convert_element_type.77
  146.2 4.6 %collective-permute-start.21 = (bf16[1200,128]{1,0:T(8,128)(2,1)S(1)}, bf16[1200,128]{1,0:T(8,128)(2,1)S(1)}, u32[]{:S(2)}, u32[]{:S(2)}) collective-permute-start(bf16[1200,128]{1,0:T(8,128)(2,1)S(1)} %get-tuple-element.22), channel_id=1, source_target_pairs={{0,7},{1,0},{2,1},{3,2},{4,3},{5,4},{6,5},{7,6},{8,15},{9,8},{10,9... | collective-permute-start | bytes 921608 | tf_op jit(solution)/shard_map/ppermute | solution.py:17
  151.0 0.1 slice_add_fusion.9
  151.1 2.0 collective-permute-start.14
  153.1 3.8 %collective-permute-done.20 = bf16[1200,128]{1,0:T(8,128)(2,1)S(1)} collective-permute-done((bf16[1200,128]{1,0:T(8,128)(2,1)S(1)}, bf16[1200,128]{1,0:T(8,128)(2,1)S(1)}, u32[]{:S(2)}, u32[]{:S(2)}) %collective-permute-start.20) | collective-permute-done | bytes 307232 | tf_op jit(solution)/shard_map/ppermute | solution.py:17
  156.9 2.6 %collective-permute-start.15 = (bf16[480,128]{1,0:T(8,128)(2,1)S(1)}, bf16[480,128]{1,0:T(8,128)(2,1)S(1)}, u32[]{:S(2)}, u32[]{:S(2)}) collective-permute-start(bf16[480,128]{1,0:T(8,128)(2,1)S(1)} %pad_maximum_fusion.10), channel_id=1, source_target_pairs={{0,5},{1,6},{2,7},{3,0},{4,1},{5,2},{6,3},{7,4},{8,13},{9,14},{10,... | collective-permute-start | bytes 368648 | tf_op jit(solution)/shard_map/ppermute | solution.py:17
  159.6 0.1 slice_add_fusion.5
  159.8 4.5 %collective-permute-start.22 = (bf16[480,128]{1,0:T(8,128)(2,1)S(1)}, bf16[480,128]{1,0:T(8,128)(2,1)S(1)}, u32[]{:S(2)}, u32[]{:S(2)}) collective-permute-start(bf16[480,128]{1,0:T(8,128)(2,1)S(1)} %pad_maximum_fusion.11), channel_id=1, source_target_pairs={{0,3},{1,4},{2,5},{3,6},{4,7},{5,0},{6,1},{7,2},{8,11},{9,12},{10,... | collective-permute-start | bytes 368648 | tf_op jit(solution)/shard_map/ppermute | solution.py:17
  164.3 3.9 %collective-permute-start.23 = (bf16[480,128]{1,0:T(8,128)(2,1)S(1)}, bf16[480,128]{1,0:T(8,128)(2,1)S(1)}, u32[]{:S(2)}, u32[]{:S(2)}) collective-permute-start(bf16[480,128]{1,0:T(8,128)(2,1)S(1)} %pad_maximum_fusion.12), channel_id=1, source_target_pairs={{0,5},{1,6},{2,7},{3,0},{4,1},{5,2},{6,3},{7,4},{8,13},{9,14},{10,... | collective-permute-start | bytes 368648 | tf_op jit(solution)/shard_map/ppermute | solution.py:17
  168.2 0.1 fusion.21
  168.3 0.5 collective-permute-done.22
  168.8 7.2 %collective-permute-done.23 = bf16[480,128]{1,0:T(8,128)(2,1)S(1)} collective-permute-done((bf16[480,128]{1,0:T(8,128)(2,1)S(1)}, bf16[480,128]{1,0:T(8,128)(2,1)S(1)}, u32[]{:S(2)}, u32[]{:S(2)}) %collective-permute-start.23) | collective-permute-done | bytes 122912 | tf_op jit(solution)/shard_map/ppermute | solution.py:17
  176.0 0.1 fusion.18
  176.1 0.8 reshape.26
  176.9 18.6 %all-to-all-start.1 = ((bf16[32,30,128]{2,1,0:T(8,128)(2,1)}), bf16[32,30,128]{2,1,0:T(8,128)(2,1)S(1)}, u32[]{:S(2)}, u32[]{:S(2)}) async-start(bf16[32,30,128]{2,1,0:T(8,128)(2,1)} %reshape.26), calls=%async_computation.1 | async-start | bytes 524288 | tf_op jit(solution)/shard_map/all_to_all | solution.py:146
  195.4 0.1 convert_element_type.65
  195.5 1.1 convert_element_type.66
  196.7 1.5 convert_element_type.67
  198.1 0.1 slice_add_fusion.1
  198.2 0.0 copy-start.10
  198.3 3.3 %collective-permute-start.6 = (bf16[768,128]{1,0:T(8,128)(2,1)S(1)}, bf16[768,128]{1,0:T(8,128)(2,1)S(1)}, u32[]{:S(2)}, u32[]{:S(2)}) collective-permute-start(bf16[768,128]{1,0:T(8,128)(2,1)S(1)} %pad_maximum_fusion.7), channel_id=1, source_target_pairs={{0,3},{1,4},{2,5},{3,6},{4,7},{5,0},{6,1},{7,2},{8,11},{9,12},{10,... | collective-permute-start | bytes 589832 | tf_op jit(solution)/shard_map/ppermute | solution.py:17
  201.6 5.1 %collective-permute-start.7 = (bf16[768,128]{1,0:T(8,128)(2,1)S(1)}, bf16[768,128]{1,0:T(8,128)(2,1)S(1)}, u32[]{:S(2)}, u32[]{:S(2)}) collective-permute-start(bf16[768,128]{1,0:T(8,128)(2,1)S(1)} %pad_maximum_fusion.8), channel_id=1, source_target_pairs={{0,5},{1,6},{2,7},{3,0},{4,1},{5,2},{6,3},{7,4},{8,13},{9,14},{10,... | collective-permute-start | bytes 589832 | tf_op jit(solution)/shard_map/ppermute | solution.py:17
  206.7 10.8 %all-to-all-done.1 = bf16[32,30,128]{2,1,0:T(8,128)(2,1)S(1)} async-done(((bf16[32,30,128]{2,1,0:T(8,128)(2,1)}), bf16[32,30,128]{2,1,0:T(8,128)(2,1)S(1)}, u32[]{:S(2)}, u32[]{:S(2)}) %all-to-all-start.1) | async-done | bytes 245792 | tf_op jit(solution)/shard_map/all_to_all | solution.py:146
  217.5 0.1 reshape.27
  217.6 0.7 fusion.4
  218.4 1.8 fusion.11
  (62 shorter events, 0.7 us)
Async XLA Ops:
  0.7 47.6 %copy-start = (bf16[768,128]{1,0:T(8,128)(2,1)S(1)}, bf16[768,128]{1,0:T(8,128)(2,1)}, u32[]{:S(2)}) copy-start(bf16[768,128]{1,0:T(8,128)(2,1)} %own_ref.1) | copy-start | bytes 589828
  3.1 71.9 %all-to-all-start = ((bf16[32,30,128]{2,1,0:T(8,128)(2,1)}), bf16[32,30,128]{2,1,0:T(8,128)(2,1)S(1)}, u32[]{:S(2)}, u32[]{:S(2)}) async-start(bf16[32,30,128]{2,1,0:T(8,128)(2,1)} %reshape.25), calls=%async_computation | async-start | bytes 524288 | tf_op jit(solution)/shard_map/all_to_all | solution.py:146
  48.3 19.3 %collective-permute-start.1 = (bf16[768,128]{1,0:T(8,128)(2,1)S(1)}, bf16[768,128]{1,0:T(8,128)(2,1)S(1)}, u32[]{:S(2)}, u32[]{:S(2)}) collective-permute-start(bf16[768,128]{1,0:T(8,128)(2,1)S(1)} %copy-done), channel_id=1, source_target_pairs={{0,5},{1,6},{2,7},{3,0},{4,1},{5,2},{6,3},{7,4},{8,13},{9,14},{10,... | collective-permute-start | bytes 589832 | tf_op jit(solution)/shard_map/ppermute | solution.py:17
  55.2 19.7 %collective-permute-start = (bf16[768,128]{1,0:T(8,128)(2,1)S(1)}, bf16[768,128]{1,0:T(8,128)(2,1)S(1)}, u32[]{:S(2)}, u32[]{:S(2)}) collective-permute-start(bf16[768,128]{1,0:T(8,128)(2,1)S(1)} %copy-done), channel_id=1, source_target_pairs={{0,3},{1,4},{2,5},{3,6},{4,7},{5,0},{6,1},{7,2},{8,11},{9,12},{10,... | collective-permute-start | bytes 589832 | tf_op jit(solution)/shard_map/ppermute | solution.py:17
  75.1 17.4 %collective-permute-start.9 = (bf16[480,128]{1,0:T(8,128)(2,1)S(1)}, bf16[480,128]{1,0:T(8,128)(2,1)S(1)}, u32[]{:S(2)}, u32[]{:S(2)}) collective-permute-start(bf16[480,128]{1,0:T(8,128)(2,1)S(1)} %slice.169.own_ref), channel_id=1, source_target_pairs={{0,5},{1,6},{2,7},{3,0},{4,1},{5,2},{6,3},{7,4},{8,13},{9,14},{10,... | collective-permute-start | bytes 368648 | tf_op jit(solution)/shard_map/ppermute | solution.py:17
  77.7 18.2 %collective-permute-start.8 = (bf16[480,128]{1,0:T(8,128)(2,1)S(1)}, bf16[480,128]{1,0:T(8,128)(2,1)S(1)}, u32[]{:S(2)}, u32[]{:S(2)}) collective-permute-start(bf16[480,128]{1,0:T(8,128)(2,1)S(1)} %slice.169.own_ref), channel_id=1, source_target_pairs={{0,3},{1,4},{2,5},{3,6},{4,7},{5,0},{6,1},{7,2},{8,11},{9,12},{10,... | collective-permute-start | bytes 368648 | tf_op jit(solution)/shard_map/ppermute | solution.py:17
  83.3 40.9 %collective-permute-start.3 = (bf16[1920,128]{1,0:T(8,128)(2,1)}, bf16[1920,128]{1,0:T(8,128)(2,1)S(1)}, u32[]{:S(2)}, u32[]{:S(2)}) collective-permute-start(bf16[1920,128]{1,0:T(8,128)(2,1)} %get-tuple-element.31), channel_id=1, source_target_pairs={{0,7},{1,0},{2,1},{3,2},{4,3},{5,4},{6,5},{7,6},{8,15},{9,8},{10,9... | collective-permute-start | bytes 1474568 | tf_op jit(solution)/shard_map/ppermute | solution.py:17
  85.4 44.4 %collective-permute-start.2 = (bf16[1920,128]{1,0:T(8,128)(2,1)}, bf16[1920,128]{1,0:T(8,128)(2,1)}, u32[]{:S(2)}, u32[]{:S(2)}) collective-permute-start(bf16[1920,128]{1,0:T(8,128)(2,1)} %get-tuple-element.32), channel_id=1, source_target_pairs={{0,1},{1,2},{2,3},{3,4},{4,5},{5,6},{6,7},{7,0},{8,9},{9,10},{10,1... | collective-permute-start | bytes 1474568 | tf_op jit(solution)/shard_map/ppermute | solution.py:17
  88.7 17.7 %collective-permute-start.17 = (bf16[480,128]{1,0:T(8,128)(2,1)S(1)}, bf16[480,128]{1,0:T(8,128)(2,1)S(1)}, u32[]{:S(2)}, u32[]{:S(2)}) collective-permute-start(bf16[480,128]{1,0:T(8,128)(2,1)S(1)} %slice.186.own_ref), channel_id=1, source_target_pairs={{0,5},{1,6},{2,7},{3,0},{4,1},{5,2},{6,3},{7,4},{8,13},{9,14},{10,... | collective-permute-start | bytes 368648 | tf_op jit(solution)/shard_map/ppermute | solution.py:17
  92.5 15.9 %collective-permute-start.16 = (bf16[480,128]{1,0:T(8,128)(2,1)S(1)}, bf16[480,128]{1,0:T(8,128)(2,1)S(1)}, u32[]{:S(2)}, u32[]{:S(2)}) collective-permute-start(bf16[480,128]{1,0:T(8,128)(2,1)S(1)} %slice.186.own_ref), channel_id=1, source_target_pairs={{0,3},{1,4},{2,5},{3,6},{4,7},{5,0},{6,1},{7,2},{8,11},{9,12},{10,... | collective-permute-start | bytes 368648 | tf_op jit(solution)/shard_map/ppermute | solution.py:17
  95.9 21.9 %copy-start.3 = (bf16[1,1024,512]{2,1,0:T(8,128)(2,1)S(1)}, bf16[1,1024,512]{2,1,0:T(8,128)(2,1)}, u32[]{:S(2)}) copy-start(bf16[1,1024,512]{2,1,0:T(8,128)(2,1)} %param.13) | copy-start | bytes 3145732
  95.9 21.9 %copy-start.8 = (f32[1024]{0:T(1024)S(1)}, f32[1024]{0:T(1024)}, u32[]{:S(2)}) copy-start(f32[1024]{0:T(1024)} %param.10) | copy-start | bytes 12292
  96.8 16.2 %collective-permute-start.11 = (bf16[1200,128]{1,0:T(8,128)(2,1)}, bf16[1200,128]{1,0:T(8,128)(2,1)S(1)}, u32[]{:S(2)}, u32[]{:S(2)}) collective-permute-start(bf16[1200,128]{1,0:T(8,128)(2,1)} %get-tuple-element.33), channel_id=1, source_target_pairs={{0,7},{1,0},{2,1},{3,2},{4,3},{5,4},{6,5},{7,6},{8,15},{9,8},{10,9... | collective-permute-start | bytes 921608 | tf_op jit(solution)/shard_map/ppermute | solution.py:17
  106.4 11.4 %collective-permute-start.10 = (bf16[1200,128]{1,0:T(8,128)(2,1)}, bf16[1200,128]{1,0:T(8,128)(2,1)}, u32[]{:S(2)}, u32[]{:S(2)}) collective-permute-start(bf16[1200,128]{1,0:T(8,128)(2,1)} %get-tuple-element.34), channel_id=1, source_target_pairs={{0,1},{1,2},{2,3},{3,4},{4,5},{5,6},{6,7},{7,0},{8,9},{9,10},{10,1... | collective-permute-start | bytes 921608 | tf_op jit(solution)/shard_map/ppermute | solution.py:17
  108.4 29.0 %collective-permute-start.19 = (bf16[1200,128]{1,0:T(8,128)(2,1)S(1)}, bf16[1200,128]{1,0:T(8,128)(2,1)S(1)}, u32[]{:S(2)}, u32[]{:S(2)}) collective-permute-start(bf16[1200,128]{1,0:T(8,128)(2,1)S(1)} %get-tuple-element.35), channel_id=1, source_target_pairs={{0,7},{1,0},{2,1},{3,2},{4,3},{5,4},{6,5},{7,6},{8,15},{9,8},{10,9... | collective-permute-start | bytes 921608 | tf_op jit(solution)/shard_map/ppermute | solution.py:17
  113.1 29.0 %collective-permute-start.18 = (bf16[1200,128]{1,0:T(8,128)(2,1)S(1)}, bf16[1200,128]{1,0:T(8,128)(2,1)S(1)}, u32[]{:S(2)}, u32[]{:S(2)}) collective-permute-start(bf16[1200,128]{1,0:T(8,128)(2,1)S(1)} %get-tuple-element.36), channel_id=1, source_target_pairs={{0,1},{1,2},{2,3},{3,4},{4,5},{5,6},{6,7},{7,0},{8,9},{9,10},{10,1... | collective-permute-start | bytes 921608 | tf_op jit(solution)/shard_map/ppermute | solution.py:17
  117.8 1.2 copy-start.4
  119.0 10.8 %copy-start.1 = (bf16[1024,512]{1,0:T(8,128)(2,1)S(1)}, bf16[1024,512]{1,0:T(8,128)(2,1)}, u32[]{:S(2)}) copy-start(bf16[1024,512]{1,0:T(8,128)(2,1)} %w_in_ref.1) | copy-start | bytes 3145732
  119.0 10.8 %copy-start.2 = (bf16[512,1024]{1,0:T(8,128)(2,1)S(1)}, bf16[512,1024]{1,0:T(8,128)(2,1)}, u32[]{:S(2)}) copy-start(bf16[512,1024]{1,0:T(8,128)(2,1)} %w_out_ref.1) | copy-start | bytes 3145732
  122.3 24.0 %collective-permute-start.12 = (bf16[1200,128]{1,0:T(8,128)(2,1)S(1)}, bf16[1200,128]{1,0:T(8,128)(2,1)S(1)}, u32[]{:S(2)}, u32[]{:S(2)}) collective-permute-start(bf16[1200,128]{1,0:T(8,128)(2,1)S(1)} %get-tuple-element.18), channel_id=1, source_target_pairs={{0,1},{1,2},{2,3},{3,4},{4,5},{5,6},{6,7},{7,0},{8,9},{9,10},{10,1... | collective-permute-start | bytes 921608 | tf_op jit(solution)/shard_map/ppermute | solution.py:17
  124.2 0.8 copy-start.6
  125.0 17.1 %copy-start.5 = (bf16[1,512,1024]{2,1,0:T(8,128)(2,1)S(1)}, bf16[1,512,1024]{2,1,0:T(8,128)(2,1)}, u32[]{:S(2)}) copy-start(bf16[1,512,1024]{2,1,0:T(8,128)(2,1)} %param.14) | copy-start | bytes 3145732
  125.0 25.9 %collective-permute-start.13 = (bf16[1200,128]{1,0:T(8,128)(2,1)S(1)}, bf16[1200,128]{1,0:T(8,128)(2,1)S(1)}, u32[]{:S(2)}, u32[]{:S(2)}) collective-permute-start(bf16[1200,128]{1,0:T(8,128)(2,1)S(1)} %get-tuple-element.19), channel_id=1, source_target_pairs={{0,7},{1,0},{2,1},{3,2},{4,3},{5,4},{6,5},{7,6},{8,15},{9,8},{10,9... | collective-permute-start | bytes 921608 | tf_op jit(solution)/shard_map/ppermute | solution.py:17
  129.8 1.0 copy-start.7
  135.4 60.1 %collective-permute-start.4 = (bf16[1920,128]{1,0:T(8,128)(2,1)}, bf16[1920,128]{1,0:T(8,128)(2,1)}, u32[]{:S(2)}, u32[]{:S(2)}) collective-permute-start(bf16[1920,128]{1,0:T(8,128)(2,1)} %get-tuple-element.15), channel_id=1, source_target_pairs={{0,1},{1,2},{2,3},{3,4},{4,5},{5,6},{6,7},{7,0},{8,9},{9,10},{10,1... | collective-permute-start | bytes 1474568 | tf_op jit(solution)/shard_map/ppermute | solution.py:17
  137.4 59.2 %collective-permute-start.5 = (bf16[1920,128]{1,0:T(8,128)(2,1)S(1)}, bf16[1920,128]{1,0:T(8,128)(2,1)}, u32[]{:S(2)}, u32[]{:S(2)}) collective-permute-start(bf16[1920,128]{1,0:T(8,128)(2,1)S(1)} %get-tuple-element.16), channel_id=1, source_target_pairs={{0,7},{1,0},{2,1},{3,2},{4,3},{5,4},{6,5},{7,6},{8,15},{9,8},{10,9... | collective-permute-start | bytes 1474568 | tf_op jit(solution)/shard_map/ppermute | solution.py:17
  144.2 12.7 %collective-permute-start.20 = (bf16[1200,128]{1,0:T(8,128)(2,1)S(1)}, bf16[1200,128]{1,0:T(8,128)(2,1)S(1)}, u32[]{:S(2)}, u32[]{:S(2)}) collective-permute-start(bf16[1200,128]{1,0:T(8,128)(2,1)S(1)} %get-tuple-element.21), channel_id=1, source_target_pairs={{0,1},{1,2},{2,3},{3,4},{4,5},{5,6},{6,7},{7,0},{8,9},{9,10},{10,1... | collective-permute-start | bytes 921608 | tf_op jit(solution)/shard_map/ppermute | solution.py:17
  146.2 13.3 %collective-permute-start.21 = (bf16[1200,128]{1,0:T(8,128)(2,1)S(1)}, bf16[1200,128]{1,0:T(8,128)(2,1)S(1)}, u32[]{:S(2)}, u32[]{:S(2)}) collective-permute-start(bf16[1200,128]{1,0:T(8,128)(2,1)S(1)} %get-tuple-element.22), channel_id=1, source_target_pairs={{0,7},{1,0},{2,1},{3,2},{4,3},{5,4},{6,5},{7,6},{8,15},{9,8},{10,9... | collective-permute-start | bytes 921608 | tf_op jit(solution)/shard_map/ppermute | solution.py:17
  151.1 13.2 %collective-permute-start.14 = (bf16[480,128]{1,0:T(8,128)(2,1)S(1)}, bf16[480,128]{1,0:T(8,128)(2,1)S(1)}, u32[]{:S(2)}, u32[]{:S(2)}) collective-permute-start(bf16[480,128]{1,0:T(8,128)(2,1)S(1)} %pad_maximum_fusion.9), channel_id=1, source_target_pairs={{0,3},{1,4},{2,5},{3,6},{4,7},{5,0},{6,1},{7,2},{8,11},{9,12},{10,... | collective-permute-start | bytes 368648 | tf_op jit(solution)/shard_map/ppermute | solution.py:17
  156.9 11.3 %collective-permute-start.15 = (bf16[480,128]{1,0:T(8,128)(2,1)S(1)}, bf16[480,128]{1,0:T(8,128)(2,1)S(1)}, u32[]{:S(2)}, u32[]{:S(2)}) collective-permute-start(bf16[480,128]{1,0:T(8,128)(2,1)S(1)} %pad_maximum_fusion.10), channel_id=1, source_target_pairs={{0,5},{1,6},{2,7},{3,0},{4,1},{5,2},{6,3},{7,4},{8,13},{9,14},{10,... | collective-permute-start | bytes 368648 | tf_op jit(solution)/shard_map/ppermute | solution.py:17
  159.8 9.0 %collective-permute-start.22 = (bf16[480,128]{1,0:T(8,128)(2,1)S(1)}, bf16[480,128]{1,0:T(8,128)(2,1)S(1)}, u32[]{:S(2)}, u32[]{:S(2)}) collective-permute-start(bf16[480,128]{1,0:T(8,128)(2,1)S(1)} %pad_maximum_fusion.11), channel_id=1, source_target_pairs={{0,3},{1,4},{2,5},{3,6},{4,7},{5,0},{6,1},{7,2},{8,11},{9,12},{10,... | collective-permute-start | bytes 368648 | tf_op jit(solution)/shard_map/ppermute | solution.py:17
  164.3 11.6 %collective-permute-start.23 = (bf16[480,128]{1,0:T(8,128)(2,1)S(1)}, bf16[480,128]{1,0:T(8,128)(2,1)S(1)}, u32[]{:S(2)}, u32[]{:S(2)}) collective-permute-start(bf16[480,128]{1,0:T(8,128)(2,1)S(1)} %pad_maximum_fusion.12), channel_id=1, source_target_pairs={{0,5},{1,6},{2,7},{3,0},{4,1},{5,2},{6,3},{7,4},{8,13},{9,14},{10,... | collective-permute-start | bytes 368648 | tf_op jit(solution)/shard_map/ppermute | solution.py:17
  176.9 40.7 %all-to-all-start.1 = ((bf16[32,30,128]{2,1,0:T(8,128)(2,1)}), bf16[32,30,128]{2,1,0:T(8,128)(2,1)S(1)}, u32[]{:S(2)}, u32[]{:S(2)}) async-start(bf16[32,30,128]{2,1,0:T(8,128)(2,1)} %reshape.26), calls=%async_computation.1 | async-start | bytes 524288 | tf_op jit(solution)/shard_map/all_to_all | solution.py:146
  196.6 1.6 copy-start.9
  198.2 19.4 %copy-start.10 = (f32[768]{0:T(1024)S(1)}, f32[768]{0:T(1024)}, u32[]{:S(2)}) copy-start(f32[768]{0:T(1024)} %param.17) | copy-start | bytes 9220
  198.3 20.0 %collective-permute-start.6 = (bf16[768,128]{1,0:T(8,128)(2,1)S(1)}, bf16[768,128]{1,0:T(8,128)(2,1)S(1)}, u32[]{:S(2)}, u32[]{:S(2)}) collective-permute-start(bf16[768,128]{1,0:T(8,128)(2,1)S(1)} %pad_maximum_fusion.7), channel_id=1, source_target_pairs={{0,3},{1,4},{2,5},{3,6},{4,7},{5,0},{6,1},{7,2},{8,11},{9,12},{10,... | collective-permute-start | bytes 589832 | tf_op jit(solution)/shard_map/ppermute | solution.py:17
  201.6 16.7 %collective-permute-start.7 = (bf16[768,128]{1,0:T(8,128)(2,1)S(1)}, bf16[768,128]{1,0:T(8,128)(2,1)S(1)}, u32[]{:S(2)}, u32[]{:S(2)}) collective-permute-start(bf16[768,128]{1,0:T(8,128)(2,1)S(1)} %pad_maximum_fusion.8), channel_id=1, source_target_pairs={{0,5},{1,6},{2,7},{3,0},{4,1},{5,2},{6,3},{7,4},{8,13},{9,14},{10,... | collective-permute-start | bytes 589832 | tf_op jit(solution)/shard_map/ppermute | solution.py:17

commit v5 on v4

--- a/solution.py
+++ b/solution.py
@@ -26,6 +26,24 @@
     from_left = shift(jnp.concatenate([own, above, below[:half]], axis=0), 1)
     from_right = shift(jnp.concatenate([own, below, above[half:]], axis=0), -1)
     return from_left, from_right
+
+
+def mlp(values, gain_ref, w_in_ref, w_out_ref):
+    values = values.astype(jnp.float32)
+    inverse = lax.rsqrt(jnp.mean(values * values, axis=1, keepdims=True) + 1e-05)
+    normed = (values * inverse * gain_ref[...]).astype(jnp.bfloat16)
+    preact = jnp.dot(normed, w_in_ref[...], preferred_element_type=jnp.float32)
+    hidden = jax.nn.gelu(preact, approximate=True).astype(jnp.bfloat16)
+    sums = jnp.dot(hidden, w_out_ref[...], preferred_element_type=jnp.float32)
+    return sums.astype(jnp.bfloat16)
+
+
+def estimate(count, model, hidden):
+    return pl.CostEstimate(
+        flops=4 * count * model * hidden,
+        transcendentals=count * hidden,
+        bytes_accessed=4 * count * model + 4 * model * hidden,
+    )
 
 
 def ffn_body(
@@ -64,13 +82,7 @@
         else:
             rows_ref[place[4], at] = right_ref[pl.ds(2 * count + start - half, block)]
         values = jnp.concatenate([rows_ref[k, at] for k in range(RING)], axis=1)
-        values = values.astype(jnp.float32)
-        inverse = lax.rsqrt(jnp.mean(values * values, axis=1, keepdims=True) + 1e-05)
-        normed = (values * inverse * gain_ref[...]).astype(jnp.bfloat16)
-        preact = jnp.dot(normed, w_in_ref[...], preferred_element_type=jnp.float32)
-        hidden = jax.nn.gelu(preact, approximate=True).astype(jnp.bfloat16)
-        sums = jnp.dot(hidden, w_out_ref[...], preferred_element_type=jnp.float32)
-        sums = sums.astype(jnp.bfloat16)
+        sums = mlp(values, gain_ref, w_in_ref, w_out_ref)
         for k in range(RING):
             sums_ref[k, at] = sums[:, k * width : (k + 1) * width]
         to_right_ref[at] = sums_ref[place[1], at]
@@ -101,12 +113,33 @@
             pltpu.VMEM((RING, count, width), jnp.bfloat16),
         ],
         compiler_params=pltpu.CompilerParams(vmem_limit_bytes=32 * 1024 * 1024),
-        cost_estimate=pl.CostEstimate(
-            flops=4 * count * model * w_in.shape[1],
-            transcendentals=count * w_in.shape[1],
-            bytes_accessed=4 * count * model + 4 * model * w_in.shape[1],
-        ),
+        cost_estimate=estimate(count, model, w_in.shape[1]),
     )(me, own, below, above, left, right, gain.reshape(1, model), w_in, w_out)
+
+
+def res_body(rows_ref, gain_ref, w_in_ref, w_out_ref, out_ref, *, block):
+    parts, count, width = rows_ref.shape
+    for start in range(0, count, block):
+        at = pl.ds(start, block)
+        values = jnp.concatenate([rows_ref[k, at] for k in range(parts)], axis=1)
+        sums = mlp(values, gain_ref, w_in_ref, w_out_ref)
+        for k in range(parts):
+            out_ref[k, at] = sums[:, k * width : (k + 1) * width]
+
+
+def res_ffn(rows, gain, w_in, w_out):
+    parts, count, width = rows.shape
+    model = parts * width
+    vmem = pl.BlockSpec(memory_space=pltpu.VMEM)
+    return pl.pallas_call(
+        functools.partial(res_body, block=count // 4),
+        in_specs=[vmem] * 4,
+        out_specs=vmem,
+        out_shape=jax.ShapeDtypeStruct(rows.shape, jnp.bfloat16),
+        compiler_params=pltpu.CompilerParams(vmem_limit_bytes=32 * 1024 * 1024),
+        cost_estimate=estimate(count, model, w_in.shape[1]),
+        name="res",
+    )(rows, gain.reshape(1, model), w_in, w_out)
 
 
 def scatter_near(to_right, to_left):
@@ -151,15 +184,13 @@
             tiled=True,
         ).reshape(slots, feat_width)
 
-    res_below = shift(tokens, 3)
+    res_rows = lax.all_gather(tokens, "mp", axis=0)
     outgoing = jnp.dot(send_table, tokens, preferred_element_type=jnp.float32)
     outgoing = outgoing.astype(jnp.bfloat16)
     incoming = exchange(outgoing)
-    res_above = shift(tokens, -3)
-    res_left, res_right = gather_near(tokens, res_below, res_above)
-    res_to_right, res_to_left, res_keep = ffn(
-        me, tokens, res_below, res_above, res_left, res_right, gain, w_res_in, w_res_out
-    )
+    res_parts = res_ffn(res_rows, gain, w_res_in, w_res_out)
+    res_sum = lax.psum_scatter(res_parts, "mp", scatter_dimension=0, tiled=False)
+    res_sum = res_sum.astype(jnp.float32)
 
     chunk = slots // CHUNKS
     summed = []
@@ -176,9 +207,6 @@
         summed.append(own.astype(jnp.bfloat16))
 
     returned = exchange(jnp.concatenate(summed, axis=0))
-    res_edges = scatter_near(res_to_right, res_to_left)
-    res_own, res_first, res_second = scatter_far(res_keep, *res_edges)
-    res_sum = res_own + res_first.astype(jnp.float32) + res_second.astype(jnp.float32)
     moe_value = jnp.dot(take_table, returned, preferred_element_type=jnp.float32)
     return (res_sum + gate_prob[:, None] * moe_value).astype(jnp.bfloat16)
 

time: 224 us -> 218 us (0.973)
  blocking collectives: 0 us -> 101 us
  starting transfers between devices: 146 us -> 57.8 us
  waiting for transfers between devices: 47.8 us -> 16.7 us
  between operations: 0.74 us -> 13.9 us
  local copies, waits for them, and re-layouts: 4.87 us -> 9.01 us
  other arithmetic: 7.97 us -> 4.28 us
    all_to_all x0 -> x2, blocking collectives: none -> 101 us  [exchange(): lax.all_to_all(rows.reshape(experts, capacity, feat_width), 'expert', spl...]
    all_to_all x2 -> x0, starting transfers between devices: 63.8 us -> none  [exchange(): lax.all_to_all(rows.reshape(experts, capacity, feat_width), 'expert', spl...]
    ppermute x24 -> x16, starting transfers between devices: 82.7 us -> 57.7 us  [shift(): lax.ppermute(value, axis, [(i, (i + step) % ring) for i in range(ring)])]
    ppermute x24 -> x16, waiting for transfers between devices: 37 us -> 15.8 us  [shift(): lax.ppermute(value, axis, [(i, (i + step) % ring) for i in range(ring)])]
    all_to_all x2 -> x0, waiting for transfers between devices: 10.8 us -> none  [exchange(): lax.all_to_all(rows.reshape(experts, capacity, feat_width), 'expert', spl...]
    unnamed x22 -> x26, local copies, waits for them, and re-layouts: 3.07 us -> 8.64 us
    pallas_call x3 -> x2, Pallas kernels: 9.99 us -> 6.16 us  [ffn(): pl.pallas_call(functools.partial(ffn_body, block=count // 4), in_specs=[p...]
    pallas_call x0 -> x1, Pallas kernels: none -> 3.74 us  [res_ffn(): pl.pallas_call(functools.partial(res_body, block=count // 4), in_specs=[v...]
  transfers between devices with their start and end apart: 26 -> 18, of which waited for: 8 -> 4; matrix products, arithmetic and copies ran while one was open for 3% -> 3% of each run, Pallas kernels for 5% -> 5%
where the time goes in v5:
time: 218 us; the launch traced here: 216 us
  blocking collectives  101 us (46%)
  starting transfers between devices  57.8 us (27%)
  waiting for transfers between devices  16.7 us (8%)
  between operations  13.9 us (6%)
  Pallas kernels  9.9 us (5%)
  local copies, waits for them, and re-layouts  9.01 us (4%)
  other arithmetic  4.28 us (2%)
  matrix products  3.88 us (2%)
    all_to_all x2, blocking collectives, exchange(): lax.all_to_all(rows.reshape(experts, capacity, feat_width), 'expert', spl...  101 us
    ppermute x16, starting transfers between devices, shift(): lax.ppermute(value, axis, [(i, (i + step) % ring) for i in range(ring)])  57.7 us
    ppermute x16, waiting for transfers between devices, shift(): lax.ppermute(value, axis, [(i, (i + step) % ring) for i in range(ring)])  15.8 us
    unnamed x26, local copies, waits for them, and re-layouts  8.64 us
    pallas_call x2, Pallas kernels, ffn(): pl.pallas_call(functools.partial(ffn_body, block=count // 4), in_specs=[p...  6.16 us
  transfers between devices with their start and end apart: 18, of which 4 were waited for; matrix products, arithmetic and copies ran while one was open for 3% of the time, Pallas kernels for 5%

profile of v5, /device:TPU:65, one launch (start us, length us, event | category | flops | bytes accessed | tf_op | source)
XLA Modules:
  0.0 216.0 jit_solution(6841152597177130568)
XLA Ops:
  6.6 0.7 all-gather.3.cloned.1.call-update
  7.3 0.1 reduce-scatter.2.cloned.1.call-start
  7.4 0.7 add_select_fusion
  8.1 1.5 fusion.6
  9.6 0.1 reshape.27
  9.7 67.1 %all_to_all.10 = bf16[32,30,128]{2,1,0:T(8,128)(2,1)S(1)} all-to-all(bf16[32,30,128]{2,1,0:T(8,128)(2,1)S(1)} %reshape.27), channel_id=1, replica_groups=mesh['groups'=2,'expert'=32,'mp'=8] {'expert'}, dimensions={0} | all-to-all | bytes 491520 | tf_op jit(solution)/shard_map/all_to_all | solution.py:179
  76.8 0.0 copy-start.11
  76.9 7.0 %collective-permute-start.1 = (bf16[480,128]{1,0:T(8,128)(2,1)S(1)}, bf16[480,128]{1,0:T(8,128)(2,1)S(1)}, u32[]{:S(2)}, u32[]{:S(2)}) collective-permute-start(bf16[480,128]{1,0:T(8,128)(2,1)S(1)} %slice.107.own_ref), channel_id=1, source_target_pairs={{0,5},{1,6},{2,7},{3,0},{4,1},{5,2},{6,3},{7,4},{8,13},{9,14},{10,... | collective-permute-start | bytes 368648 | tf_op jit(solution)/shard_map/ppermute | solution.py:17
  83.8 2.0 collective-permute-start
  85.8 6.4 %collective-permute-start.9 = (bf16[480,128]{1,0:T(8,128)(2,1)S(1)}, bf16[480,128]{1,0:T(8,128)(2,1)S(1)}, u32[]{:S(2)}, u32[]{:S(2)}) collective-permute-start(bf16[480,128]{1,0:T(8,128)(2,1)S(1)} %slice.124.own_ref), channel_id=1, source_target_pairs={{0,5},{1,6},{2,7},{3,0},{4,1},{5,2},{6,3},{7,4},{8,13},{9,14},{10,... | collective-permute-start | bytes 368648 | tf_op jit(solution)/shard_map/ppermute | solution.py:17
  92.2 2.0 collective-permute-start.8
  94.2 0.0 collective-permute-done.1.above_ref
  94.2 4.9 %collective-permute-done.below_ref = bf16[480,128]{1,0:T(8,128)(2,1)S(1)} collective-permute-done((bf16[480,128]{1,0:T(8,128)(2,1)S(1)}, bf16[480,128]{1,0:T(8,128)(2,1)S(1)}, u32[]{:S(2)}, u32[]{:S(2)}) %collective-permute-start) | collective-permute-done | bytes 122912 | tf_op jit(solution)/shard_map/ppermute | solution.py:17
  99.2 2.0 collective-permute-start.3
  101.2 3.4 %collective-permute-start.2 = (bf16[1200,128]{1,0:T(8,128)(2,1)S(1)}, bf16[1200,128]{1,0:T(8,128)(2,1)S(1)}, u32[]{:S(2)}, u32[]{:S(2)}) collective-permute-start(bf16[1200,128]{1,0:T(8,128)(2,1)S(1)} %get-tuple-element.24), channel_id=1, source_target_pairs={{0,1},{1,2},{2,3},{3,4},{4,5},{5,6},{6,7},{7,0},{8,9},{9,10},{10,1... | collective-permute-start | bytes 921608 | tf_op jit(solution)/shard_map/ppermute | solution.py:17
  104.6 0.0 collective-permute-done.9.above_ref
  104.6 0.8 collective-permute-done.8.below_ref
  105.4 0.9 fusion.9
  106.3 2.3 %collective-permute-start.11 = (bf16[1200,128]{1,0:T(8,128)(2,1)}, bf16[1200,128]{1,0:T(8,128)(2,1)}, u32[]{:S(2)}, u32[]{:S(2)}) collective-permute-start(bf16[1200,128]{1,0:T(8,128)(2,1)} %get-tuple-element.25), channel_id=1, source_target_pairs={{0,7},{1,0},{2,1},{3,2},{4,3},{5,4},{6,5},{7,6},{8,15},{9,8},{10,9... | collective-permute-start | bytes 921608 | tf_op jit(solution)/shard_map/ppermute | solution.py:17
  108.7 3.0 %collective-permute-start.10 = (bf16[1200,128]{1,0:T(8,128)(2,1)}, bf16[1200,128]{1,0:T(8,128)(2,1)}, u32[]{:S(2)}, u32[]{:S(2)}) collective-permute-start(bf16[1200,128]{1,0:T(8,128)(2,1)} %get-tuple-element.26), channel_id=1, source_target_pairs={{0,1},{1,2},{2,3},{3,4},{4,5},{5,6},{6,7},{7,0},{8,9},{9,10},{10,1... | collective-permute-start | bytes 921608 | tf_op jit(solution)/shard_map/ppermute | solution.py:17
  111.7 0.0 collective-permute-done.3.right_ref
  111.7 0.7 copy-done.7
  112.4 0.0 collective-permute-done.2.left_ref
  112.4 0.7 copy-done.9
  113.1 1.2 copy-done.3
  114.4 1.2 copy-done.5
  115.6 1.0 copy-done.8
  116.6 1.0 copy-done.10
  117.5 2.9 %shard_map.91 = (bf16[1200,128]{1,0:T(8,128)(2,1)}, bf16[1200,128]{1,0:T(8,128)(2,1)S(1)}, bf16[3,480,128]{2,1,0:T(8,128)(2,1)S(1)}) custom-call(s32[1]{0:T(128)} %bitcast.3.me_ref, bf16[480,128]{1,0:T(8,128)(2,1)S(1)} %slice.107.own_ref, bf16[480,128]{1,0:T(8,128)(2,1)S(1)} %collective-permute-done.below_ref, ...), custom_call_target="tpu_custom_call" | custom-call | flops 1006632960 | bytes 4063232 | tf_op jit(solution)/shard_map/pallas_call | solution.py:106
  120.5 2.5 %collective-permute-start.4 = (bf16[1200,128]{1,0:T(8,128)(2,1)}, bf16[1200,128]{1,0:T(8,128)(2,1)}, u32[]{:S(2)}, u32[]{:S(2)}) collective-permute-start(bf16[1200,128]{1,0:T(8,128)(2,1)} %get-tuple-element.12), channel_id=1, source_target_pairs={{0,1},{1,2},{2,3},{3,4},{4,5},{5,6},{6,7},{7,0},{8,9},{9,10},{10,1... | collective-permute-start | bytes 921608 | tf_op jit(solution)/shard_map/ppermute | solution.py:17
  123.0 4.0 %collective-permute-start.5 = (bf16[1200,128]{1,0:T(8,128)(2,1)S(1)}, bf16[1200,128]{1,0:T(8,128)(2,1)}, u32[]{:S(2)}, u32[]{:S(2)}) collective-permute-start(bf16[1200,128]{1,0:T(8,128)(2,1)S(1)} %get-tuple-element.13), channel_id=1, source_target_pairs={{0,7},{1,0},{2,1},{3,2},{4,3},{5,4},{6,5},{7,6},{8,15},{9,8},{10,9... | collective-permute-start | bytes 921608 | tf_op jit(solution)/shard_map/ppermute | solution.py:17
  127.0 0.0 all-gather.3.cloned.1.call-done
  127.1 1.4 copy-done
  128.5 3.7 %res.1 = bf16[8,768,128]{2,1,0:T(8,128)(2,1)} custom-call(bf16[8,768,128]{2,1,0:T(8,128)(2,1)S(1)} %bitcast.34, f32[1,1024]{1,0:T(1,128)S(1)} %bitcast.40, bf16[1024,512]{1,0:T(8,128)(2,1)S(1)} %copy-done.1, bf16[512,1024]{1,0:T(8,128)(2,1)S(1)} %copy-done.2), custom_call_target="tpu_custom_call" | custom-call | flops 1610612736 | bytes 5242880 | tf_op jit(solution)/shard_map/res/pallas_call | solution.py:134
  132.2 0.1 reduce-scatter.2.cloned.1.call-update
  132.3 0.1 convert_element_type.57
  132.4 1.1 copy-done.4
  133.4 0.3 copy-done.6
  133.8 3.2 %shard_map.92 = (bf16[1200,128]{1,0:T(8,128)(2,1)S(1)}, bf16[1200,128]{1,0:T(8,128)(2,1)S(1)}, bf16[3,480,128]{2,1,0:T(8,128)(2,1)S(1)}) custom-call(s32[1]{0:T(128)} %bitcast.3.me_ref, bf16[480,128]{1,0:T(8,128)(2,1)S(1)} %slice.124.own_ref, bf16[480,128]{1,0:T(8,128)(2,1)S(1)} %collective-permute-done.8.below_ref, ...), custom_call_target="tpu_custom_call" | custom-call | flops 1006632960 | bytes 4063232 | tf_op jit(solution)/shard_map/pallas_call | solution.py:106
  137.0 2.0 collective-permute-start.12
  138.9 4.6 %collective-permute-start.13 = (bf16[1200,128]{1,0:T(8,128)(2,1)S(1)}, bf16[1200,128]{1,0:T(8,128)(2,1)S(1)}, u32[]{:S(2)}, u32[]{:S(2)}) collective-permute-start(bf16[1200,128]{1,0:T(8,128)(2,1)S(1)} %get-tuple-element.16), channel_id=1, source_target_pairs={{0,7},{1,0},{2,1},{3,2},{4,3},{5,4},{6,5},{7,6},{8,15},{9,8},{10,9... | collective-permute-start | bytes 921608 | tf_op jit(solution)/shard_map/ppermute | solution.py:17
  143.6 0.1 convert_element_type.63
  143.6 0.0 collective-permute-done.4
  143.6 1.0 convert_element_type.58
  144.6 0.0 collective-permute-done.5
  144.6 1.0 convert_element_type.59
  145.7 0.1 slice_add_fusion.5
  145.8 2.0 collective-permute-start.6
  147.8 6.4 %collective-permute-start.7 = (bf16[480,128]{1,0:T(8,128)(2,1)S(1)}, bf16[480,128]{1,0:T(8,128)(2,1)S(1)}, u32[]{:S(2)}, u32[]{:S(2)}) collective-permute-start(bf16[480,128]{1,0:T(8,128)(2,1)S(1)} %pad_maximum_fusion.6), channel_id=1, source_target_pairs={{0,5},{1,6},{2,7},{3,0},{4,1},{5,2},{6,3},{7,4},{8,13},{9,14},{10,... | collective-permute-start | bytes 368648 | tf_op jit(solution)/shard_map/ppermute | solution.py:17
  154.2 0.0 collective-permute-done.12
  154.3 0.1 slice_add_fusion.1
  154.5 2.0 collective-permute-start.14
  156.5 6.4 %collective-permute-start.15 = (bf16[480,128]{1,0:T(8,128)(2,1)S(1)}, bf16[480,128]{1,0:T(8,128)(2,1)S(1)}, u32[]{:S(2)}, u32[]{:S(2)}) collective-permute-start(bf16[480,128]{1,0:T(8,128)(2,1)S(1)} %pad_maximum_fusion.8), channel_id=1, source_target_pairs={{0,5},{1,6},{2,7},{3,0},{4,1},{5,2},{6,3},{7,4},{8,13},{9,14},{10,... | collective-permute-start | bytes 368648 | tf_op jit(solution)/shard_map/ppermute | solution.py:17
  162.9 0.0 collective-permute-done.6
  162.9 0.1 fusion.17
  163.0 0.0 copy-start.12
  163.0 8.2 %collective-permute-done.14 = bf16[480,128]{1,0:T(8,128)(2,1)S(1)} collective-permute-done((bf16[480,128]{1,0:T(8,128)(2,1)S(1)}, bf16[480,128]{1,0:T(8,128)(2,1)S(1)}, u32[]{:S(2)}, u32[]{:S(2)}) %collective-permute-start.14) | collective-permute-done | bytes 122912 | tf_op jit(solution)/shard_map/ppermute | solution.py:17
  171.2 1.9 collective-permute-done.15
  173.0 0.1 fusion.14
  173.1 0.1 reshape.28
  173.2 33.5 %all_to_all.11 = bf16[32,30,128]{2,1,0:T(8,128)(2,1)S(1)} all-to-all(bf16[32,30,128]{2,1,0:T(8,128)(2,1)S(1)} %reshape.28), channel_id=1, replica_groups=mesh['groups'=2,'expert'=32,'mp'=8] {'expert'}, dimensions={0} | all-to-all | bytes 491520 | tf_op jit(solution)/shard_map/all_to_all | solution.py:179
  206.7 0.1 reshape.29
  206.7 0.0 reduce-scatter.2.cloned.1.call-done
  206.8 2.3 %fusion.7 = bf16[768,128]{1,0:T(8,128)(2,1)} fusion(bf16[960,128]{1,0:T(8,128)(2,1)S(1)} %reshape.29, s32[768]{0:T(1024)S(1)} %add_select_fusion, bf16[1,768,128]{2,1,0:T(8,128)(2,1)} %reduce-scatter.2.cloned.1.call-done, f32[768]{0:T(1024)S(1)} %copy-done.12), kind=kOutput, calls=%fused_computation.9 | convolution fusion | flops 189874176 | bytes 645120 | tf_op jit(solution)/shard_map/dot_general | solution.py:210
  (41 shorter events, 0.5 us)
Async XLA Ops:
  6.5 120.5 %all-gather.3.cloned.1.call-start = ((), (), s32[]{:S(2)}) async-start(), calls=%async_computation.4 | async-start | bytes 1769472 | tf_op jit(solution)/shard_map/all_gather | solution.py:187
  7.3 199.5 %reduce-scatter.2.cloned.1.call-start = ((), (), s32[]{:S(2)}) async-start(), calls=%async_computation.3 | async-start | bytes 1769472 | tf_op jit(solution)/shard_map/reduce_scatter | solution.py:192
  76.8 36.3 %copy-start.11 = (f32[1024]{0:T(1024)S(1)}, f32[1024]{0:T(1024)}, u32[]{:S(2)}) copy-start(f32[1024]{0:T(1024)} %param.10) | copy-start | bytes 12292
  76.9 17.3 %collective-permute-start.1 = (bf16[480,128]{1,0:T(8,128)(2,1)S(1)}, bf16[480,128]{1,0:T(8,128)(2,1)S(1)}, u32[]{:S(2)}, u32[]{:S(2)}) collective-permute-start(bf16[480,128]{1,0:T(8,128)(2,1)S(1)} %slice.107.own_ref), channel_id=1, source_target_pairs={{0,5},{1,6},{2,7},{3,0},{4,1},{5,2},{6,3},{7,4},{8,13},{9,14},{10,... | collective-permute-start | bytes 368648 | tf_op jit(solution)/shard_map/ppermute | solution.py:17
  83.8 15.3 %collective-permute-start = (bf16[480,128]{1,0:T(8,128)(2,1)S(1)}, bf16[480,128]{1,0:T(8,128)(2,1)S(1)}, u32[]{:S(2)}, u32[]{:S(2)}) collective-permute-start(bf16[480,128]{1,0:T(8,128)(2,1)S(1)} %slice.107.own_ref), channel_id=1, source_target_pairs={{0,3},{1,4},{2,5},{3,6},{4,7},{5,0},{6,1},{7,2},{8,11},{9,12},{10,... | collective-permute-start | bytes 368648 | tf_op jit(solution)/shard_map/ppermute | solution.py:17
  85.8 18.7 %collective-permute-start.9 = (bf16[480,128]{1,0:T(8,128)(2,1)S(1)}, bf16[480,128]{1,0:T(8,128)(2,1)S(1)}, u32[]{:S(2)}, u32[]{:S(2)}) collective-permute-start(bf16[480,128]{1,0:T(8,128)(2,1)S(1)} %slice.124.own_ref), channel_id=1, source_target_pairs={{0,5},{1,6},{2,7},{3,0},{4,1},{5,2},{6,3},{7,4},{8,13},{9,14},{10,... | collective-permute-start | bytes 368648 | tf_op jit(solution)/shard_map/ppermute | solution.py:17
  92.2 13.2 %collective-permute-start.8 = (bf16[480,128]{1,0:T(8,128)(2,1)S(1)}, bf16[480,128]{1,0:T(8,128)(2,1)S(1)}, u32[]{:S(2)}, u32[]{:S(2)}) collective-permute-start(bf16[480,128]{1,0:T(8,128)(2,1)S(1)} %slice.124.own_ref), channel_id=1, source_target_pairs={{0,3},{1,4},{2,5},{3,6},{4,7},{5,0},{6,1},{7,2},{8,11},{9,12},{10,... | collective-permute-start | bytes 368648 | tf_op jit(solution)/shard_map/ppermute | solution.py:17
  99.2 12.5 %collective-permute-start.3 = (bf16[1200,128]{1,0:T(8,128)(2,1)S(1)}, bf16[1200,128]{1,0:T(8,128)(2,1)S(1)}, u32[]{:S(2)}, u32[]{:S(2)}) collective-permute-start(bf16[1200,128]{1,0:T(8,128)(2,1)S(1)} %get-tuple-element.23), channel_id=1, source_target_pairs={{0,7},{1,0},{2,1},{3,2},{4,3},{5,4},{6,5},{7,6},{8,15},{9,8},{10,9... | collective-permute-start | bytes 921608 | tf_op jit(solution)/shard_map/ppermute | solution.py:17
  101.2 11.3 %collective-permute-start.2 = (bf16[1200,128]{1,0:T(8,128)(2,1)S(1)}, bf16[1200,128]{1,0:T(8,128)(2,1)S(1)}, u32[]{:S(2)}, u32[]{:S(2)}) collective-permute-start(bf16[1200,128]{1,0:T(8,128)(2,1)S(1)} %get-tuple-element.24), channel_id=1, source_target_pairs={{0,1},{1,2},{2,3},{3,4},{4,5},{5,6},{6,7},{7,0},{8,9},{9,10},{10,1... | collective-permute-start | bytes 921608 | tf_op jit(solution)/shard_map/ppermute | solution.py:17
  106.3 26.0 %collective-permute-start.11 = (bf16[1200,128]{1,0:T(8,128)(2,1)}, bf16[1200,128]{1,0:T(8,128)(2,1)}, u32[]{:S(2)}, u32[]{:S(2)}) collective-permute-start(bf16[1200,128]{1,0:T(8,128)(2,1)} %get-tuple-element.25), channel_id=1, source_target_pairs={{0,7},{1,0},{2,1},{3,2},{4,3},{5,4},{6,5},{7,6},{8,15},{9,8},{10,9... | collective-permute-start | bytes 921608 | tf_op jit(solution)/shard_map/ppermute | solution.py:17
  108.7 23.7 %collective-permute-start.10 = (bf16[1200,128]{1,0:T(8,128)(2,1)}, bf16[1200,128]{1,0:T(8,128)(2,1)}, u32[]{:S(2)}, u32[]{:S(2)}) collective-permute-start(bf16[1200,128]{1,0:T(8,128)(2,1)} %get-tuple-element.26), channel_id=1, source_target_pairs={{0,1},{1,2},{2,3},{3,4},{4,5},{5,6},{6,7},{7,0},{8,9},{9,10},{10,1... | collective-permute-start | bytes 921608 | tf_op jit(solution)/shard_map/ppermute | solution.py:17
  111.7 0.7 copy-start.7
  112.4 0.7 copy-start.9
  113.1 1.2 copy-start.3
  114.4 1.2 copy-start.5
  115.6 1.0 copy-start.8
  116.6 1.0 copy-start.10
  117.5 9.5 %copy-start.1 = (bf16[1024,512]{1,0:T(8,128)(2,1)S(1)}, bf16[1024,512]{1,0:T(8,128)(2,1)}, u32[]{:S(2)}) copy-start(bf16[1024,512]{1,0:T(8,128)(2,1)} %w_in_ref.1) | copy-start | bytes 3145732
  117.5 9.5 %copy-start.2 = (bf16[512,1024]{1,0:T(8,128)(2,1)S(1)}, bf16[512,1024]{1,0:T(8,128)(2,1)}, u32[]{:S(2)}) copy-start(bf16[512,1024]{1,0:T(8,128)(2,1)} %w_out_ref.1) | copy-start | bytes 3145732
  120.5 23.2 %collective-permute-start.4 = (bf16[1200,128]{1,0:T(8,128)(2,1)}, bf16[1200,128]{1,0:T(8,128)(2,1)}, u32[]{:S(2)}, u32[]{:S(2)}) collective-permute-start(bf16[1200,128]{1,0:T(8,128)(2,1)} %get-tuple-element.12), channel_id=1, source_target_pairs={{0,1},{1,2},{2,3},{3,4},{4,5},{5,6},{6,7},{7,0},{8,9},{9,10},{10,1... | collective-permute-start | bytes 921608 | tf_op jit(solution)/shard_map/ppermute | solution.py:17
  123.0 21.6 %collective-permute-start.5 = (bf16[1200,128]{1,0:T(8,128)(2,1)S(1)}, bf16[1200,128]{1,0:T(8,128)(2,1)}, u32[]{:S(2)}, u32[]{:S(2)}) collective-permute-start(bf16[1200,128]{1,0:T(8,128)(2,1)S(1)} %get-tuple-element.13), channel_id=1, source_target_pairs={{0,7},{1,0},{2,1},{3,2},{4,3},{5,4},{6,5},{7,6},{8,15},{9,8},{10,9... | collective-permute-start | bytes 921608 | tf_op jit(solution)/shard_map/ppermute | solution.py:17
  127.1 1.4 copy-start
  132.2 1.2 copy-start.4
  132.2 1.5 copy-start.6
  137.0 17.2 %collective-permute-start.12 = (bf16[1200,128]{1,0:T(8,128)(2,1)S(1)}, bf16[1200,128]{1,0:T(8,128)(2,1)S(1)}, u32[]{:S(2)}, u32[]{:S(2)}) collective-permute-start(bf16[1200,128]{1,0:T(8,128)(2,1)S(1)} %get-tuple-element.15), channel_id=1, source_target_pairs={{0,1},{1,2},{2,3},{3,4},{4,5},{5,6},{6,7},{7,0},{8,9},{9,10},{10,1... | collective-permute-start | bytes 921608 | tf_op jit(solution)/shard_map/ppermute | solution.py:17
  138.9 15.3 %collective-permute-start.13 = (bf16[1200,128]{1,0:T(8,128)(2,1)S(1)}, bf16[1200,128]{1,0:T(8,128)(2,1)S(1)}, u32[]{:S(2)}, u32[]{:S(2)}) collective-permute-start(bf16[1200,128]{1,0:T(8,128)(2,1)S(1)} %get-tuple-element.16), channel_id=1, source_target_pairs={{0,7},{1,0},{2,1},{3,2},{4,3},{5,4},{6,5},{7,6},{8,15},{9,8},{10,9... | collective-permute-start | bytes 921608 | tf_op jit(solution)/shard_map/ppermute | solution.py:17
  145.8 17.1 %collective-permute-start.6 = (bf16[480,128]{1,0:T(8,128)(2,1)S(1)}, bf16[480,128]{1,0:T(8,128)(2,1)S(1)}, u32[]{:S(2)}, u32[]{:S(2)}) collective-permute-start(bf16[480,128]{1,0:T(8,128)(2,1)S(1)} %pad_maximum_fusion.5), channel_id=1, source_target_pairs={{0,3},{1,4},{2,5},{3,6},{4,7},{5,0},{6,1},{7,2},{8,11},{9,12},{10,... | collective-permute-start | bytes 368648 | tf_op jit(solution)/shard_map/ppermute | solution.py:17
  147.8 15.1 %collective-permute-start.7 = (bf16[480,128]{1,0:T(8,128)(2,1)S(1)}, bf16[480,128]{1,0:T(8,128)(2,1)S(1)}, u32[]{:S(2)}, u32[]{:S(2)}) collective-permute-start(bf16[480,128]{1,0:T(8,128)(2,1)S(1)} %pad_maximum_fusion.6), channel_id=1, source_target_pairs={{0,5},{1,6},{2,7},{3,0},{4,1},{5,2},{6,3},{7,4},{8,13},{9,14},{10,... | collective-permute-start | bytes 368648 | tf_op jit(solution)/shard_map/ppermute | solution.py:17
  154.5 16.7 %collective-permute-start.14 = (bf16[480,128]{1,0:T(8,128)(2,1)S(1)}, bf16[480,128]{1,0:T(8,128)(2,1)S(1)}, u32[]{:S(2)}, u32[]{:S(2)}) collective-permute-start(bf16[480,128]{1,0:T(8,128)(2,1)S(1)} %pad_maximum_fusion.7), channel_id=1, source_target_pairs={{0,3},{1,4},{2,5},{3,6},{4,7},{5,0},{6,1},{7,2},{8,11},{9,12},{10,... | collective-permute-start | bytes 368648 | tf_op jit(solution)/shard_map/ppermute | solution.py:17
  156.5 16.5 %collective-permute-start.15 = (bf16[480,128]{1,0:T(8,128)(2,1)S(1)}, bf16[480,128]{1,0:T(8,128)(2,1)S(1)}, u32[]{:S(2)}, u32[]{:S(2)}) collective-permute-start(bf16[480,128]{1,0:T(8,128)(2,1)S(1)} %pad_maximum_fusion.8), channel_id=1, source_target_pairs={{0,5},{1,6},{2,7},{3,0},{4,1},{5,2},{6,3},{7,4},{8,13},{9,14},{10,... | collective-permute-start | bytes 368648 | tf_op jit(solution)/shard_map/ppermute | solution.py:17
  163.0 43.8 %copy-start.12 = (f32[768]{0:T(1024)S(1)}, f32[768]{0:T(1024)}, u32[]{:S(2)}) copy-start(f32[768]{0:T(1024)} %param.17) | copy-start | bytes 9220
Sparse Core Ops, SparseCore 0:
  9.4 76.4 all-gather.2
  132.4 52.4 reduce-scatter.1

commit v6 on v3

--- a/solution.py
+++ b/solution.py
@@ -11,9 +11,13 @@
 RING = 8
 
 
-def shift(value, step, axis="mp"):
-    ring = lax.axis_size(axis)
-    return lax.ppermute(value, axis, [(i, (i + step) % ring) for i in range(ring)])
+def shift(value, step):
+    experts, ring = lax.axis_size("expert"), lax.axis_size("mp")
+    pairs = []
+    for e in range(experts):
+        along = step if e % 2 == 0 else -step
+        pairs += [(e * ring + i, e * ring + (i + along) % ring) for i in range(ring)]
+    return lax.ppermute(value, ("expert", "mp"), pairs)
 
 
 def gather_far(own):
@@ -45,10 +49,10 @@
     *,
     block,
 ):
-    me = me_ref[0]
+    me, sign = me_ref[0], me_ref[1]
     count, width = own_ref.shape
     half = count // 2
-    place = [lax.rem(me + step, RING) for step in range(RING)]
+    place = [lax.rem(me + RING + sign * step, RING) for step in range(RING)]
     for start in range(0, count, block):
         at = pl.ds(start, block)
         rows_ref[place[0], at] = own_ref[at]
@@ -135,7 +139,8 @@
     experts = lax.axis_size("expert")
     capacity = max(2, 5 * row_count // (4 * experts))
     slots = experts * capacity
-    me = lax.axis_index("mp").astype(jnp.int32).reshape(1)
+    odd = lax.rem(lax.axis_index("expert"), 2)
+    me = jnp.stack([lax.axis_index("mp"), 1 - 2 * odd]).astype(jnp.int32)
     slot_id = jnp.where(slot_of >= 0, expert_of * capacity + slot_of, -1)
     slot_index = jnp.arange(slots, dtype=jnp.int32)
     send_table = (slot_index[:, None] == slot_id[None, :]).astype(jnp.bfloat16)

time: 222 us -> 216 us (0.973)
  starting transfers between devices: 82.9 us -> 61.4 us
  waiting for transfers between devices: 50.6 us -> 67 us
    ppermute x16, waiting for transfers between devices: 39.4 us -> 55.6 us  [shift(): return lax.ppermute(value, ('expert', 'mp'), pairs)]
    ppermute x16, starting transfers between devices: 68.7 us -> 57.2 us  [shift(): return lax.ppermute(value, ('expert', 'mp'), pairs)]
    all_to_all x1, starting transfers between devices: 14.1 us -> 4.19 us  [exchange(): lax.all_to_all(rows.reshape(experts, capacity, feat_width), 'expert', spl...]
  transfers between devices with their start and end apart: 17 -> 17, of which waited for: 7 -> 9; matrix products, arithmetic and copies ran while one was open for 1% -> 1% of each run, Pallas kernels for 3% -> 4%
where the time goes in v6:
time: 216 us; the launch traced here: 214 us
  blocking collectives  67.1 us (31%)
  waiting for transfers between devices  67 us (31%)
  starting transfers between devices  61.4 us (28%)
  Pallas kernels  8.28 us (4%)
  other arithmetic  4.29 us (2%)
  matrix products  4.12 us (2%)
    all_to_all x1, blocking collectives, exchange(): lax.all_to_all(rows.reshape(experts, capacity, feat_width), 'expert', spl...  67.1 us
    ppermute x16, starting transfers between devices, shift(): return lax.ppermute(value, ('expert', 'mp'), pairs)  57.2 us
    ppermute x16, waiting for transfers between devices, shift(): return lax.ppermute(value, ('expert', 'mp'), pairs)  55.6 us
    all_to_all x1, waiting for transfers between devices, exchange(): lax.all_to_all(rows.reshape(experts, capacity, feat_width), 'expert', spl...  11.5 us
    pallas_call x2, Pallas kernels, ffn(): pl.pallas_call(functools.partial(ffn_body, block=count // 4), in_specs=[p...  8.28 us
  transfers between devices with their start and end apart: 17, of which 9 were waited for; matrix products, arithmetic and copies ran while one was open for 1% of the time, Pallas kernels for 4%

profile of v6, /device:TPU:65, one launch (start us, length us, event | category | flops | bytes accessed | tf_op | source)
XLA Modules:
  0.0 214.5 jit_solution(16945425473639809958)
XLA Ops:
  0.0 0.7 add_select_fusion
  0.7 1.5 fusion.5
  2.3 0.1 reshape.20
  2.3 67.1 %all_to_all.10 = bf16[32,30,128]{2,1,0:T(8,128)(2,1)S(1)} all-to-all(bf16[32,30,128]{2,1,0:T(8,128)(2,1)S(1)} %reshape.20), channel_id=1, replica_groups=mesh['groups'=2,'expert'=32,'mp'=8] {'expert'}, dimensions={0} | all-to-all | bytes 491520 | tf_op jit(solution)/shard_map/all_to_all | solution.py:150
  69.4 0.1 reshape.21.own_ref
  69.5 7.0 %collective-permute-start.8 = (bf16[960,128]{1,0:T(8,128)(2,1)S(1)}, bf16[960,128]{1,0:T(8,128)(2,1)S(1)}, u32[]{:S(2)}, u32[]{:S(2)}) collective-permute-start(bf16[960,128]{1,0:T(8,128)(2,1)S(1)} %reshape.21.own_ref), channel_id=1, source_target_pairs={{0,3},{1,4},{2,5},{3,6},{4,7},{5,0},{6,1},{7,2},{8,13},{9,14},{10,... | collective-permute-start | bytes 737288 | tf_op jit(solution)/shard_map/ppermute | solution.py:20
  76.4 2.0 collective-permute-start.9
  78.4 13.3 %collective-permute-done.8.below_ref = bf16[960,128]{1,0:T(8,128)(2,1)S(1)} collective-permute-done((bf16[960,128]{1,0:T(8,128)(2,1)S(1)}, bf16[960,128]{1,0:T(8,128)(2,1)S(1)}, u32[]{:S(2)}, u32[]{:S(2)}) %collective-permute-start.8) | collective-permute-done | bytes 245792 | tf_op jit(solution)/shard_map/ppermute | solution.py:20
  91.7 0.0 copy-start
  91.8 1.8 collective-permute-done.9.above_ref
  93.6 1.2 fusion.7
  94.7 4.2 %collective-permute-start.10 = (bf16[2400,128]{1,0:T(8,128)(2,1)}, bf16[2400,128]{1,0:T(8,128)(2,1)}, u32[]{:S(2)}, u32[]{:S(2)}) collective-permute-start(bf16[2400,128]{1,0:T(8,128)(2,1)} %get-tuple-element.22), channel_id=1, source_target_pairs={{0,1},{1,2},{2,3},{3,4},{4,5},{5,6},{6,7},{7,0},{8,15},{9,8},{10,9... | collective-permute-start | bytes 1843208 | tf_op jit(solution)/shard_map/ppermute | solution.py:20
  99.0 2.0 collective-permute-start.11
  100.9 0.0 copy-done
  100.9 5.7 %collective-permute-start = (bf16[768,128]{1,0:T(8,128)(2,1)S(1)}, bf16[768,128]{1,0:T(8,128)(2,1)S(1)}, u32[]{:S(2)}, u32[]{:S(2)}) collective-permute-start(bf16[768,128]{1,0:T(8,128)(2,1)S(1)} %copy-done), channel_id=1, source_target_pairs={{0,3},{1,4},{2,5},{3,6},{4,7},{5,0},{6,1},{7,2},{8,13},{9,14},{10,... | collective-permute-start | bytes 589832 | tf_op jit(solution)/shard_map/ppermute | solution.py:20
  106.7 2.0 collective-permute-start.1
  108.6 0.1 pad_add_fusion.me_ref
  108.7 10.5 %collective-permute-done.below_ref = bf16[768,128]{1,0:T(8,128)(2,1)S(1)} collective-permute-done((bf16[768,128]{1,0:T(8,128)(2,1)S(1)}, bf16[768,128]{1,0:T(8,128)(2,1)S(1)}, u32[]{:S(2)}, u32[]{:S(2)}) %collective-permute-start) | collective-permute-done | bytes 196640 | tf_op jit(solution)/shard_map/ppermute | solution.py:20
  119.2 7.0 %collective-permute-done.1.above_ref = bf16[768,128]{1,0:T(8,128)(2,1)S(1)} collective-permute-done((bf16[768,128]{1,0:T(8,128)(2,1)S(1)}, bf16[768,128]{1,0:T(8,128)(2,1)S(1)}, u32[]{:S(2)}, u32[]{:S(2)}) %collective-permute-start.1) | collective-permute-done | bytes 196640 | tf_op jit(solution)/shard_map/ppermute | solution.py:20
  126.1 0.1 fusion.9
  126.2 2.0 collective-permute-start.2
  128.2 3.3 %collective-permute-start.3 = (bf16[1920,128]{1,0:T(8,128)(2,1)S(1)}, bf16[1920,128]{1,0:T(8,128)(2,1)S(1)}, u32[]{:S(2)}, u32[]{:S(2)}) collective-permute-start(bf16[1920,128]{1,0:T(8,128)(2,1)S(1)} %get-tuple-element.23), channel_id=1, source_target_pairs={{0,7},{1,0},{2,1},{3,2},{4,3},{5,4},{6,5},{7,6},{8,9},{9,10},{10,1... | collective-permute-start | bytes 1474568 | tf_op jit(solution)/shard_map/ppermute | solution.py:20
  131.6 0.0 collective-permute-done.10.left_ref
  131.6 0.0 collective-permute-done.11.right_ref
  131.6 0.0 copy-start.3
  131.6 0.0 copy-start.4
  131.6 4.8 %shard_map.92 = (bf16[2400,128]{1,0:T(8,128)(2,1)S(1)}, bf16[2400,128]{1,0:T(8,128)(2,1)S(1)}, bf16[3,960,128]{2,1,0:T(8,128)(2,1)S(1)}) custom-call(s32[2]{0:T(128)S(1)} %pad_add_fusion.me_ref, bf16[960,128]{1,0:T(8,128)(2,1)S(1)} %reshape.21.own_ref, bf16[960,128]{1,0:T(8,128)(2,1)S(1)} %collective-permute-done.8.below_ref, ...), custom_call_target="tpu_custom_call" | custom-call | flops 2013265920 | bytes 6029312 | tf_op jit(solution)/shard_map/pallas_call | solution.py:97
  136.5 6.3 %collective-permute-start.12 = (bf16[2400,128]{1,0:T(8,128)(2,1)S(1)}, bf16[2400,128]{1,0:T(8,128)(2,1)S(1)}, u32[]{:S(2)}, u32[]{:S(2)}) collective-permute-start(bf16[2400,128]{1,0:T(8,128)(2,1)S(1)} %get-tuple-element.15), channel_id=1, source_target_pairs={{0,1},{1,2},{2,3},{3,4},{4,5},{5,6},{6,7},{7,0},{8,15},{9,8},{10,9... | collective-permute-start | bytes 1843208 | tf_op jit(solution)/shard_map/ppermute | solution.py:20
  142.8 2.0 collective-permute-start.13
  144.8 0.0 collective-permute-done.2.left_ref
  144.8 0.0 collective-permute-done.3.right_ref
  144.8 3.5 %shard_map.91 = (bf16[1920,128]{1,0:T(8,128)(2,1)S(1)}, bf16[1920,128]{1,0:T(8,128)(2,1)S(1)}, bf16[3,768,128]{2,1,0:T(8,128)(2,1)S(1)}) custom-call(s32[2]{0:T(128)S(1)} %pad_add_fusion.me_ref, bf16[768,128]{1,0:T(8,128)(2,1)S(1)} %copy-done, bf16[768,128]{1,0:T(8,128)(2,1)S(1)} %collective-permute-done.below_ref, ...), custom_call_target="tpu_custom_call" | custom-call | flops 1610612736 | bytes 5242880 | tf_op jit(solution)/shard_map/pallas_call | solution.py:97
  148.3 4.6 %collective-permute-start.4 = (bf16[1920,128]{1,0:T(8,128)(2,1)S(1)}, bf16[1920,128]{1,0:T(8,128)(2,1)S(1)}, u32[]{:S(2)}, u32[]{:S(2)}) collective-permute-start(bf16[1920,128]{1,0:T(8,128)(2,1)S(1)} %get-tuple-element.12), channel_id=1, source_target_pairs={{0,1},{1,2},{2,3},{3,4},{4,5},{5,6},{6,7},{7,0},{8,15},{9,8},{10,9... | collective-permute-start | bytes 1474568 | tf_op jit(solution)/shard_map/ppermute | solution.py:20
  152.9 2.0 collective-permute-start.5
  154.9 0.1 convert_element_type.51
  155.0 0.0 collective-permute-done.12
  155.0 0.1 convert_element_type.52
  155.1 6.1 %collective-permute-done.13 = bf16[2400,128]{1,0:T(8,128)(2,1)S(1)} collective-permute-done((bf16[2400,128]{1,0:T(8,128)(2,1)S(1)}, bf16[2400,128]{1,0:T(8,128)(2,1)S(1)}, u32[]{:S(2)}, u32[]{:S(2)}) %collective-permute-start.13) | collective-permute-done | bytes 614432 | tf_op jit(solution)/shard_map/ppermute | solution.py:20
  161.2 0.1 convert_element_type.53
  161.2 0.1 slice_add_fusion.1
  161.3 0.1 fusion.17
  161.5 3.4 %collective-permute-start.14 = (bf16[960,128]{1,0:T(8,128)(2,1)S(1)}, bf16[960,128]{1,0:T(8,128)(2,1)S(1)}, u32[]{:S(2)}, u32[]{:S(2)}) collective-permute-start(bf16[960,128]{1,0:T(8,128)(2,1)S(1)} %pad_maximum_fusion.4), channel_id=1, source_target_pairs={{0,3},{1,4},{2,5},{3,6},{4,7},{5,0},{6,1},{7,2},{8,13},{9,14},{10,... | collective-permute-start | bytes 737288 | tf_op jit(solution)/shard_map/ppermute | solution.py:20
  165.0 3.7 %collective-permute-start.15 = (bf16[960,128]{1,0:T(8,128)(2,1)S(1)}, bf16[960,128]{1,0:T(8,128)(2,1)S(1)}, u32[]{:S(2)}, u32[]{:S(2)}) collective-permute-start(bf16[960,128]{1,0:T(8,128)(2,1)S(1)} %pad_maximum_fusion.5), channel_id=1, source_target_pairs={{0,5},{1,6},{2,7},{3,0},{4,1},{5,2},{6,3},{7,4},{8,11},{9,12},{10,... | collective-permute-start | bytes 737288 | tf_op jit(solution)/shard_map/ppermute | solution.py:20
  168.7 0.1 convert_element_type.45
  168.7 0.0 collective-permute-done.4
  168.8 0.1 convert_element_type.46
  168.8 3.9 %collective-permute-done.5 = bf16[1920,128]{1,0:T(8,128)(2,1)S(1)} collective-permute-done((bf16[1920,128]{1,0:T(8,128)(2,1)S(1)}, bf16[1920,128]{1,0:T(8,128)(2,1)S(1)}, u32[]{:S(2)}, u32[]{:S(2)}) %collective-permute-start.5) | collective-permute-done | bytes 491552 | tf_op jit(solution)/shard_map/ppermute | solution.py:20
  172.7 0.1 convert_element_type.47
  172.8 4.5 %collective-permute-done.14 = bf16[960,128]{1,0:T(8,128)(2,1)S(1)} collective-permute-done((bf16[960,128]{1,0:T(8,128)(2,1)S(1)}, bf16[960,128]{1,0:T(8,128)(2,1)S(1)}, u32[]{:S(2)}, u32[]{:S(2)}) %collective-permute-start.14) | collective-permute-done | bytes 245792 | tf_op jit(solution)/shard_map/ppermute | solution.py:20
  177.3 8.5 %collective-permute-done.15 = bf16[960,128]{1,0:T(8,128)(2,1)S(1)} collective-permute-done((bf16[960,128]{1,0:T(8,128)(2,1)S(1)}, bf16[960,128]{1,0:T(8,128)(2,1)S(1)}, u32[]{:S(2)}, u32[]{:S(2)}) %collective-permute-start.15) | collective-permute-done | bytes 245792 | tf_op jit(solution)/shard_map/ppermute | solution.py:20
  185.8 0.1 fusion.12
  186.0 0.8 reshape.22
  186.7 4.2 %all-to-all-start.1 = ((bf16[32,30,128]{2,1,0:T(8,128)(2,1)}), bf16[32,30,128]{2,1,0:T(8,128)(2,1)S(1)}, u32[]{:S(2)}, u32[]{:S(2)}) async-start(bf16[32,30,128]{2,1,0:T(8,128)(2,1)} %reshape.22), calls=%async_computation.1 | async-start | bytes 524288 | tf_op jit(solution)/shard_map/all_to_all | solution.py:150
  190.9 0.1 slice_add_fusion.5
  191.0 0.0 copy-start.6
  191.1 0.7 pad_maximum_fusion.6
  191.8 4.4 %collective-permute-start.6 = (bf16[768,128]{1,0:T(8,128)(2,1)}, bf16[768,128]{1,0:T(8,128)(2,1)}, u32[]{:S(2)}, u32[]{:S(2)}) collective-permute-start(bf16[768,128]{1,0:T(8,128)(2,1)} %pad_maximum_fusion.6), channel_id=1, source_target_pairs={{0,3},{1,4},{2,5},{3,6},{4,7},{5,0},{6,1},{7,2},{8,13},{9,14},{10,... | collective-permute-start | bytes 589832 | tf_op jit(solution)/shard_map/ppermute | solution.py:20
  196.2 0.7 pad_maximum_fusion.7
  196.9 2.7 %collective-permute-start.7 = (bf16[768,128]{1,0:T(8,128)(2,1)}, bf16[768,128]{1,0:T(8,128)(2,1)}, u32[]{:S(2)}, u32[]{:S(2)}) collective-permute-start(bf16[768,128]{1,0:T(8,128)(2,1)} %pad_maximum_fusion.7), channel_id=1, source_target_pairs={{0,5},{1,6},{2,7},{3,0},{4,1},{5,2},{6,3},{7,4},{8,11},{9,12},{10,... | collective-permute-start | bytes 589832 | tf_op jit(solution)/shard_map/ppermute | solution.py:20
  199.6 11.5 %all-to-all-done.1 = bf16[32,30,128]{2,1,0:T(8,128)(2,1)S(1)} async-done(((bf16[32,30,128]{2,1,0:T(8,128)(2,1)}), bf16[32,30,128]{2,1,0:T(8,128)(2,1)S(1)}, u32[]{:S(2)}, u32[]{:S(2)}) %all-to-all-start.1) | async-done | bytes 245792 | tf_op jit(solution)/shard_map/all_to_all | solution.py:150
  211.1 0.8 reshape.23
  211.9 0.0 collective-permute-done.6
  211.9 0.0 collective-permute-done.7
  211.9 2.6 %fusion.16 = bf16[768,128]{1,0:T(8,128)(2,1)} fusion(f32[1920,128]{1,0:T(8,128)S(1)} %convert_element_type.47, f32[1920,128]{1,0:T(8,128)S(1)} %convert_element_type.46, f32[3,768,128]{2,1,0:T(8,128)S(1)} %convert_element_type.45, bf16[768,128]{1,0:T(8,128)(2,1)} %collective-permute-done.7, bf16[768,128]{1,0:T(8,128)(2,1)} %collective-permute-done.6, ...), kind=kOutput, calls=%fused_computation.34 | convolution fusion | flops 190365696 | bytes 2021376 | tf_op jit(solution)/shard_map/dot_general | solution.py:178
  (20 shorter events, 0.2 us)
Async XLA Ops:
  69.5 22.2 %collective-permute-start.8 = (bf16[960,128]{1,0:T(8,128)(2,1)S(1)}, bf16[960,128]{1,0:T(8,128)(2,1)S(1)}, u32[]{:S(2)}, u32[]{:S(2)}) collective-permute-start(bf16[960,128]{1,0:T(8,128)(2,1)S(1)} %reshape.21.own_ref), channel_id=1, source_target_pairs={{0,3},{1,4},{2,5},{3,6},{4,7},{5,0},{6,1},{7,2},{8,13},{9,14},{10,... | collective-permute-start | bytes 737288 | tf_op jit(solution)/shard_map/ppermute | solution.py:20
  76.4 17.1 %collective-permute-start.9 = (bf16[960,128]{1,0:T(8,128)(2,1)S(1)}, bf16[960,128]{1,0:T(8,128)(2,1)S(1)}, u32[]{:S(2)}, u32[]{:S(2)}) collective-permute-start(bf16[960,128]{1,0:T(8,128)(2,1)S(1)} %reshape.21.own_ref), channel_id=1, source_target_pairs={{0,5},{1,6},{2,7},{3,0},{4,1},{5,2},{6,3},{7,4},{8,11},{9,12},{10,... | collective-permute-start | bytes 737288 | tf_op jit(solution)/shard_map/ppermute | solution.py:20
  91.7 9.2 %copy-start = (bf16[768,128]{1,0:T(8,128)(2,1)S(1)}, bf16[768,128]{1,0:T(8,128)(2,1)}, u32[]{:S(2)}) copy-start(bf16[768,128]{1,0:T(8,128)(2,1)} %own_ref.1) | copy-start | bytes 589828
  94.7 36.9 %copy-start.1 = (bf16[1,1024,512]{2,1,0:T(8,128)(2,1)S(1)}, bf16[1,1024,512]{2,1,0:T(8,128)(2,1)}, u32[]{:S(2)}) copy-start(bf16[1,1024,512]{2,1,0:T(8,128)(2,1)} %param.13) | copy-start | bytes 3145732
  94.7 36.9 %copy-start.2 = (bf16[1,512,1024]{2,1,0:T(8,128)(2,1)S(1)}, bf16[1,512,1024]{2,1,0:T(8,128)(2,1)}, u32[]{:S(2)}) copy-start(bf16[1,512,1024]{2,1,0:T(8,128)(2,1)} %param.14) | copy-start | bytes 3145732
  94.7 36.9 %copy-start.5 = (f32[1024]{0:T(1024)S(1)}, f32[1024]{0:T(1024)}, u32[]{:S(2)}) copy-start(f32[1024]{0:T(1024)} %param.10) | copy-start | bytes 12292
  94.7 36.8 %collective-permute-start.10 = (bf16[2400,128]{1,0:T(8,128)(2,1)}, bf16[2400,128]{1,0:T(8,128)(2,1)}, u32[]{:S(2)}, u32[]{:S(2)}) collective-permute-start(bf16[2400,128]{1,0:T(8,128)(2,1)} %get-tuple-element.22), channel_id=1, source_target_pairs={{0,1},{1,2},{2,3},{3,4},{4,5},{5,6},{6,7},{7,0},{8,15},{9,8},{10,9... | collective-permute-start | bytes 1843208 | tf_op jit(solution)/shard_map/ppermute | solution.py:20
  99.0 32.6 %collective-permute-start.11 = (bf16[2400,128]{1,0:T(8,128)(2,1)}, bf16[2400,128]{1,0:T(8,128)(2,1)}, u32[]{:S(2)}, u32[]{:S(2)}) collective-permute-start(bf16[2400,128]{1,0:T(8,128)(2,1)} %get-tuple-element.21), channel_id=1, source_target_pairs={{0,7},{1,0},{2,1},{3,2},{4,3},{5,4},{6,5},{7,6},{8,9},{9,10},{10,1... | collective-permute-start | bytes 1843208 | tf_op jit(solution)/shard_map/ppermute | solution.py:20
  100.9 18.2 %collective-permute-start = (bf16[768,128]{1,0:T(8,128)(2,1)S(1)}, bf16[768,128]{1,0:T(8,128)(2,1)S(1)}, u32[]{:S(2)}, u32[]{:S(2)}) collective-permute-start(bf16[768,128]{1,0:T(8,128)(2,1)S(1)} %copy-done), channel_id=1, source_target_pairs={{0,3},{1,4},{2,5},{3,6},{4,7},{5,0},{6,1},{7,2},{8,13},{9,14},{10,... | collective-permute-start | bytes 589832 | tf_op jit(solution)/shard_map/ppermute | solution.py:20
  106.7 19.5 %collective-permute-start.1 = (bf16[768,128]{1,0:T(8,128)(2,1)S(1)}, bf16[768,128]{1,0:T(8,128)(2,1)S(1)}, u32[]{:S(2)}, u32[]{:S(2)}) collective-permute-start(bf16[768,128]{1,0:T(8,128)(2,1)S(1)} %copy-done), channel_id=1, source_target_pairs={{0,5},{1,6},{2,7},{3,0},{4,1},{5,2},{6,3},{7,4},{8,11},{9,12},{10,... | collective-permute-start | bytes 589832 | tf_op jit(solution)/shard_map/ppermute | solution.py:20
  126.2 18.6 %collective-permute-start.2 = (bf16[1920,128]{1,0:T(8,128)(2,1)S(1)}, bf16[1920,128]{1,0:T(8,128)(2,1)S(1)}, u32[]{:S(2)}, u32[]{:S(2)}) collective-permute-start(bf16[1920,128]{1,0:T(8,128)(2,1)S(1)} %get-tuple-element.24), channel_id=1, source_target_pairs={{0,1},{1,2},{2,3},{3,4},{4,5},{5,6},{6,7},{7,0},{8,15},{9,8},{10,9... | collective-permute-start | bytes 1474568 | tf_op jit(solution)/shard_map/ppermute | solution.py:20
  128.2 16.5 %collective-permute-start.3 = (bf16[1920,128]{1,0:T(8,128)(2,1)S(1)}, bf16[1920,128]{1,0:T(8,128)(2,1)S(1)}, u32[]{:S(2)}, u32[]{:S(2)}) collective-permute-start(bf16[1920,128]{1,0:T(8,128)(2,1)S(1)} %get-tuple-element.23), channel_id=1, source_target_pairs={{0,7},{1,0},{2,1},{3,2},{4,3},{5,4},{6,5},{7,6},{8,9},{9,10},{10,1... | collective-permute-start | bytes 1474568 | tf_op jit(solution)/shard_map/ppermute | solution.py:20
  131.6 13.2 %copy-start.3 = (bf16[1024,512]{1,0:T(8,128)(2,1)S(1)}, bf16[1024,512]{1,0:T(8,128)(2,1)}, u32[]{:S(2)}) copy-start(bf16[1024,512]{1,0:T(8,128)(2,1)} %w_in_ref.1) | copy-start | bytes 3145732
  131.6 13.2 %copy-start.4 = (bf16[512,1024]{1,0:T(8,128)(2,1)S(1)}, bf16[512,1024]{1,0:T(8,128)(2,1)}, u32[]{:S(2)}) copy-start(bf16[512,1024]{1,0:T(8,128)(2,1)} %w_out_ref.1) | copy-start | bytes 3145732
  136.5 18.5 %collective-permute-start.12 = (bf16[2400,128]{1,0:T(8,128)(2,1)S(1)}, bf16[2400,128]{1,0:T(8,128)(2,1)S(1)}, u32[]{:S(2)}, u32[]{:S(2)}) collective-permute-start(bf16[2400,128]{1,0:T(8,128)(2,1)S(1)} %get-tuple-element.15), channel_id=1, source_target_pairs={{0,1},{1,2},{2,3},{3,4},{4,5},{5,6},{6,7},{7,0},{8,15},{9,8},{10,9... | collective-permute-start | bytes 1843208 | tf_op jit(solution)/shard_map/ppermute | solution.py:20
  142.8 18.3 %collective-permute-start.13 = (bf16[2400,128]{1,0:T(8,128)(2,1)S(1)}, bf16[2400,128]{1,0:T(8,128)(2,1)S(1)}, u32[]{:S(2)}, u32[]{:S(2)}) collective-permute-start(bf16[2400,128]{1,0:T(8,128)(2,1)S(1)} %get-tuple-element.16), channel_id=1, source_target_pairs={{0,7},{1,0},{2,1},{3,2},{4,3},{5,4},{6,5},{7,6},{8,9},{9,10},{10,1... | collective-permute-start | bytes 1843208 | tf_op jit(solution)/shard_map/ppermute | solution.py:20
  148.3 20.4 %collective-permute-start.4 = (bf16[1920,128]{1,0:T(8,128)(2,1)S(1)}, bf16[1920,128]{1,0:T(8,128)(2,1)S(1)}, u32[]{:S(2)}, u32[]{:S(2)}) collective-permute-start(bf16[1920,128]{1,0:T(8,128)(2,1)S(1)} %get-tuple-element.12), channel_id=1, source_target_pairs={{0,1},{1,2},{2,3},{3,4},{4,5},{5,6},{6,7},{7,0},{8,15},{9,8},{10,9... | collective-permute-start | bytes 1474568 | tf_op jit(solution)/shard_map/ppermute | solution.py:20
  152.9 19.8 %collective-permute-start.5 = (bf16[1920,128]{1,0:T(8,128)(2,1)S(1)}, bf16[1920,128]{1,0:T(8,128)(2,1)S(1)}, u32[]{:S(2)}, u32[]{:S(2)}) collective-permute-start(bf16[1920,128]{1,0:T(8,128)(2,1)S(1)} %get-tuple-element.13), channel_id=1, source_target_pairs={{0,7},{1,0},{2,1},{3,2},{4,3},{5,4},{6,5},{7,6},{8,9},{9,10},{10,1... | collective-permute-start | bytes 1474568 | tf_op jit(solution)/shard_map/ppermute | solution.py:20
  161.5 15.9 %collective-permute-start.14 = (bf16[960,128]{1,0:T(8,128)(2,1)S(1)}, bf16[960,128]{1,0:T(8,128)(2,1)S(1)}, u32[]{:S(2)}, u32[]{:S(2)}) collective-permute-start(bf16[960,128]{1,0:T(8,128)(2,1)S(1)} %pad_maximum_fusion.4), channel_id=1, source_target_pairs={{0,3},{1,4},{2,5},{3,6},{4,7},{5,0},{6,1},{7,2},{8,13},{9,14},{10,... | collective-permute-start | bytes 737288 | tf_op jit(solution)/shard_map/ppermute | solution.py:20
  165.0 20.9 %collective-permute-start.15 = (bf16[960,128]{1,0:T(8,128)(2,1)S(1)}, bf16[960,128]{1,0:T(8,128)(2,1)S(1)}, u32[]{:S(2)}, u32[]{:S(2)}) collective-permute-start(bf16[960,128]{1,0:T(8,128)(2,1)S(1)} %pad_maximum_fusion.5), channel_id=1, source_target_pairs={{0,5},{1,6},{2,7},{3,0},{4,1},{5,2},{6,3},{7,4},{8,11},{9,12},{10,... | collective-permute-start | bytes 737288 | tf_op jit(solution)/shard_map/ppermute | solution.py:20
  186.7 24.4 %all-to-all-start.1 = ((bf16[32,30,128]{2,1,0:T(8,128)(2,1)}), bf16[32,30,128]{2,1,0:T(8,128)(2,1)S(1)}, u32[]{:S(2)}, u32[]{:S(2)}) async-start(bf16[32,30,128]{2,1,0:T(8,128)(2,1)} %reshape.22), calls=%async_computation.1 | async-start | bytes 524288 | tf_op jit(solution)/shard_map/all_to_all | solution.py:150
  191.0 20.8 %copy-start.6 = (f32[768]{0:T(1024)S(1)}, f32[768]{0:T(1024)}, u32[]{:S(2)}) copy-start(f32[768]{0:T(1024)} %param.17) | copy-start | bytes 9220
  191.8 20.1 %collective-permute-start.6 = (bf16[768,128]{1,0:T(8,128)(2,1)}, bf16[768,128]{1,0:T(8,128)(2,1)}, u32[]{:S(2)}, u32[]{:S(2)}) collective-permute-start(bf16[768,128]{1,0:T(8,128)(2,1)} %pad_maximum_fusion.6), channel_id=1, source_target_pairs={{0,3},{1,4},{2,5},{3,6},{4,7},{5,0},{6,1},{7,2},{8,13},{9,14},{10,... | collective-permute-start | bytes 589832 | tf_op jit(solution)/shard_map/ppermute | solution.py:20
  196.9 15.0 %collective-permute-start.7 = (bf16[768,128]{1,0:T(8,128)(2,1)}, bf16[768,128]{1,0:T(8,128)(2,1)}, u32[]{:S(2)}, u32[]{:S(2)}) collective-permute-start(bf16[768,128]{1,0:T(8,128)(2,1)} %pad_maximum_fusion.7), channel_id=1, source_target_pairs={{0,5},{1,6},{2,7},{3,0},{4,1},{5,2},{6,3},{7,4},{8,11},{9,12},{10,... | collective-permute-start | bytes 589832 | tf_op jit(solution)/shard_map/ppermute | solution.py:20

commit v7 on v4

--- a/solution.py
+++ b/solution.py
@@ -8,7 +8,6 @@
 from jax.sharding import PartitionSpec as P
 
 
-CHUNKS = 2
 RING = 8
 
 
@@ -28,8 +27,8 @@
     return from_left, from_right
 
 
-def ffn_body(
-    me_ref,
+def branch(
+    me,
     own_ref,
     below_ref,
     above_ref,
@@ -43,15 +42,16 @@
     keep_ref,
     rows_ref,
     sums_ref,
-    *,
     block,
+    base,
 ):
-    me = me_ref[0]
     count, width = own_ref.shape
     half = count // 2
     place = [lax.rem(me + step, RING) for step in range(RING)]
     for start in range(0, count, block):
         at = pl.ds(start, block)
+        first = pl.ds(base + start, block)
+        second = pl.ds(base + count + start, block)
         rows_ref[place[0], at] = own_ref[at]
         rows_ref[place[1], at] = right_ref[at]
         rows_ref[place[7], at] = left_ref[at]
@@ -73,21 +73,91 @@
         sums = sums.astype(jnp.bfloat16)
         for k in range(RING):
             sums_ref[k, at] = sums[:, k * width : (k + 1) * width]
-        to_right_ref[at] = sums_ref[place[1], at]
-        to_right_ref[pl.ds(count + start, block)] = sums_ref[place[6], at]
-        to_left_ref[at] = sums_ref[place[7], at]
-        to_left_ref[pl.ds(count + start, block)] = sums_ref[place[2], at]
+        to_right_ref[first] = sums_ref[place[1], at]
+        to_right_ref[second] = sums_ref[place[6], at]
+        to_left_ref[first] = sums_ref[place[7], at]
+        to_left_ref[second] = sums_ref[place[2], at]
         if start < half:
-            to_right_ref[pl.ds(2 * count + start, block)] = sums_ref[place[4], at]
+            to_right_ref[pl.ds(base + 2 * count + start, block)] = sums_ref[place[4], at]
         else:
-            to_left_ref[pl.ds(2 * count + start - half, block)] = sums_ref[place[4], at]
+            third = pl.ds(base + 2 * count + start - half, block)
+            to_left_ref[third] = sums_ref[place[4], at]
         keep_ref[0, at] = sums_ref[place[0], at]
         keep_ref[1, at] = sums_ref[place[3], at]
         keep_ref[2, at] = sums_ref[place[5], at]
 
 
-def ffn(me, own, below, above, left, right, gain, w_in, w_out):
-    count, width = own.shape
+def ffn_body(me_ref, *refs, block):
+    branch(me_ref[0], *refs, block, 0)
+
+
+def pair_body(me_ref, *refs, block, later_block):
+    own, below, above, left, right, gain, w_in, w_out = refs[:8]
+    sources = refs[8:15]
+    to_right, to_left, keep, later_keep = refs[15:19]
+    rows, sums, later_rows, later_sums = refs[19:23]
+    targets = refs[23:30]
+    done = refs[30]
+    copies = [
+        pltpu.make_async_copy(source, target, done.at[n])
+        for n, (source, target) in enumerate(zip(sources, targets))
+    ]
+    for copy in copies:
+        copy.start()
+    me = me_ref[0]
+    branch(
+        me,
+        own,
+        below,
+        above,
+        left,
+        right,
+        gain,
+        w_in,
+        w_out,
+        to_right,
+        to_left,
+        keep,
+        rows,
+        sums,
+        block,
+        0,
+    )
+    for copy in copies:
+        copy.wait()
+    branch(
+        me,
+        *targets[:5],
+        gain,
+        *targets[5:],
+        to_right,
+        to_left,
+        later_keep,
+        later_rows,
+        later_sums,
+        later_block,
+        5 * own.shape[0] // 2,
+    )
+
+
+def sums_of(count, width):
+    return jax.ShapeDtypeStruct((3, count, width), jnp.bfloat16)
+
+
+def tiles_of(count, width):
+    return pltpu.VMEM((RING, count, width), jnp.bfloat16)
+
+
+def estimate(count, model, hidden):
+    return pl.CostEstimate(
+        flops=4 * count * model * hidden,
+        transcendentals=count * hidden,
+        bytes_accessed=4 * count * model + 4 * model * hidden,
+    )
+
+
+def ffn(me, pieces, gain, w_in, w_out):
+    count, width = pieces[0].shape
     model = RING * width
     vmem = pl.BlockSpec(memory_space=pltpu.VMEM)
     edge = jax.ShapeDtypeStruct((5 * count // 2, width), jnp.bfloat16)
@@ -95,37 +165,60 @@
         functools.partial(ffn_body, block=count // 4),
         in_specs=[pl.BlockSpec(memory_space=pltpu.SMEM)] + [vmem] * 8,
         out_specs=[vmem] * 3,
-        out_shape=[edge, edge, jax.ShapeDtypeStruct((3, count, width), jnp.bfloat16)],
-        scratch_shapes=[
-            pltpu.VMEM((RING, count, width), jnp.bfloat16),
-            pltpu.VMEM((RING, count, width), jnp.bfloat16),
-        ],
+        out_shape=[edge, edge, sums_of(count, width)],
+        scratch_shapes=[tiles_of(count, width)] * 2,
         compiler_params=pltpu.CompilerParams(vmem_limit_bytes=32 * 1024 * 1024),
-        cost_estimate=pl.CostEstimate(
-            flops=4 * count * model * w_in.shape[1],
-            transcendentals=count * w_in.shape[1],
-            bytes_accessed=4 * count * model + 4 * model * w_in.shape[1],
-        ),
-    )(me, own, below, above, left, right, gain.reshape(1, model), w_in, w_out)
+        cost_estimate=estimate(count, model, w_in.shape[1]),
+        name="exp",
+    )(me, *pieces, gain.reshape(1, model), w_in, w_out)
+
+
+def ffn_pair(me, pieces, gain, w_in, w_out, later_pieces, later_in, later_out):
+    count, width = pieces[0].shape
+    later = later_pieces[0].shape[0]
+    model = RING * width
+    vmem = pl.BlockSpec(memory_space=pltpu.VMEM)
+    anywhere = pl.BlockSpec(memory_space=pl.ANY)
+    edge = jax.ShapeDtypeStruct((5 * (count + later) // 2, width), jnp.bfloat16)
+    operands = [*later_pieces, later_in, later_out]
+    return pl.pallas_call(
+        functools.partial(pair_body, block=count // 4, later_block=later // 4),
+        in_specs=[pl.BlockSpec(memory_space=pltpu.SMEM)] + [vmem] * 8 + [anywhere] * 7,
+        out_specs=[vmem] * 4,
+        out_shape=[edge, edge, sums_of(count, width), sums_of(later, width)],
+        scratch_shapes=[tiles_of(count, width)] * 2
+        + [tiles_of(later, width)] * 2
+        + [pltpu.VMEM(value.shape, value.dtype) for value in operands]
+        + [pltpu.SemaphoreType.DMA((7,))],
+        compiler_params=pltpu.CompilerParams(vmem_limit_bytes=40 * 1024 * 1024),
+        cost_estimate=estimate(count + later, model, w_in.shape[1]),
+        name="pair",
+    )(me, *pieces, gain.reshape(1, model), w_in, w_out, *operands)
 
 
 def scatter_near(to_right, to_left):
     return shift(to_right, 1), shift(to_left, -1)
 
 
-def scatter_far(keep, from_left, from_right):
+def scatter_far(keep, from_left, from_right, base=0):
     count = keep.shape[1]
     half = count // 2
-    keep = keep.astype(jnp.float32)
-    from_left = from_left.astype(jnp.float32)
-    from_right = from_right.astype(jnp.float32)
-    own = keep[0] + from_left[:count] + from_right[:count]
-    above = keep[1] + from_right[count : 2 * count]
-    above = jnp.concatenate([above[:half] + from_left[2 * count :], above[half:]], axis=0)
-    below = keep[2] + from_left[count : 2 * count]
-    below = jnp.concatenate([below[:half], below[half:] + from_right[2 * count :]], axis=0)
-    first = shift(above.astype(jnp.bfloat16), 3)
-    second = shift(below.astype(jnp.bfloat16), -3)
+    one, two = base + count, base + 2 * count
+
+    def wide(value):
+        return value.astype(jnp.float32)
+
+    own = wide(keep[0]) + wide(from_left[base:one]) + wide(from_right[base:one])
+    above = wide(keep[1]) + wide(from_right[one:two])
+    to_above = jnp.concatenate(
+        [above[:half] + wide(from_left[two : two + half]), above[half:]], axis=0
+    )
+    below = wide(keep[2]) + wide(from_left[one:two])
+    to_below = jnp.concatenate(
+        [below[:half], below[half:] + wide(from_right[two : two + half])], axis=0
+    )
+    first = shift(to_above.astype(jnp.bfloat16), 3)
+    second = shift(to_below.astype(jnp.bfloat16), -3)
     return own, first, second
 
 
@@ -157,27 +250,35 @@
     incoming = exchange(outgoing)
     res_above = shift(tokens, -3)
     res_left, res_right = gather_near(tokens, res_below, res_above)
-    res_to_right, res_to_left, res_keep = ffn(
-        me, tokens, res_below, res_above, res_left, res_right, gain, w_res_in, w_res_out
-    )
-
-    chunk = slots // CHUNKS
-    summed = []
-    for c in range(CHUNKS):
+    res_pieces = (tokens, res_below, res_above, res_left, res_right)
+    chunk = slots // 2
+    pieces = []
+    for c in range(2):
         rows = incoming[c * chunk : (c + 1) * chunk]
         below, above = gather_far(rows)
         left, right = gather_near(rows, below, above)
-        to_right, to_left, keep = ffn(
-            me, rows, below, above, left, right, gain, w_exp_in[0], w_exp_out[0]
-        )
-        edges = scatter_near(to_right, to_left)
+        pieces.append((rows, below, above, left, right))
+    to_right, to_left, keep_0 = ffn(me, pieces[0], gain, w_exp_in[0], w_exp_out[0])
+    edges_0 = scatter_near(to_right, to_left)
+    to_right, to_left, keep_1, res_keep = ffn_pair(
+        me,
+        pieces[1],
+        gain,
+        w_exp_in[0],
+        w_exp_out[0],
+        res_pieces,
+        w_res_in,
+        w_res_out,
+    )
+    edges_1 = scatter_near(to_right, to_left)
+    summed = []
+    for keep, edges in ((keep_0, edges_0), (keep_1, edges_1)):
         own, first, second = scatter_far(keep, *edges)
         own = own + first.astype(jnp.float32) + second.astype(jnp.float32)
         summed.append(own.astype(jnp.bfloat16))
 
     returned = exchange(jnp.concatenate(summed, axis=0))
-    res_edges = scatter_near(res_to_right, res_to_left)
-    res_own, res_first, res_second = scatter_far(res_keep, *res_edges)
+    res_own, res_first, res_second = scatter_far(res_keep, *edges_1, 5 * chunk // 2)
     res_sum = res_own + res_first.astype(jnp.float32) + res_second.astype(jnp.float32)
     moe_value = jnp.dot(take_table, returned, preferred_element_type=jnp.float32)
     return (res_sum + gate_prob[:, None] * moe_value).astype(jnp.bfloat16)

time: 224 us -> 220 us (0.982)
  waiting for transfers between devices: 47.8 us -> 53.1 us
  starting transfers between devices: 146 us -> 142 us
  other arithmetic: 7.97 us -> 4.86 us
    all_to_all x2, waiting for transfers between devices: 10.8 us -> 23.9 us  [exchange(): lax.all_to_all(rows.reshape(experts, capacity, feat_width), 'expert', spl...]
    ppermute x24 -> x22, waiting for transfers between devices: 37 us -> 29.1 us  [shift(): lax.ppermute(value, axis, [(i, (i + step) % ring) for i in range(ring)])]
    pallas_call x0 -> x1, Pallas kernels: none -> 7.17 us  [ffn_pair(): pl.pallas_call(functools.partial(pair_body, block=count // 4, later_block...]
    pallas_call x3 -> x1, Pallas kernels: 9.99 us -> 3.23 us  [ffn(): pl.pallas_call(functools.partial(ffn_body, block=count // 4), in_specs=[p...]
    convert_element_type x9 -> x0, other arithmetic: 2.9 us -> none  [the longest x3 1.54 us: scatter_far(): from_right = from_right.astype(jnp.float32)]
    ppermute x24 -> x22, starting transfers between devices: 82.7 us -> 80 us  [shift(): lax.ppermute(value, axis, [(i, (i + step) % ring) for i in range(ring)])]
  transfers between devices with their start and end apart: 26 -> 24, of which waited for: 8 -> 9; matrix products, arithmetic and copies ran while one was open for 3% -> 2% of each run, Pallas kernels for 5% -> 5%
where the time goes in v7:
time: 220 us; the launch traced here: 218 us
  starting transfers between devices  142 us (65%)
  waiting for transfers between devices  53.1 us (24%)
  Pallas kernels  10.4 us (5%)
  other arithmetic  4.86 us (2%)
  local copies, waits for them, and re-layouts  4.71 us (2%)
  matrix products  2.32 us (1%)
    ppermute x22, starting transfers between devices, shift(): lax.ppermute(value, axis, [(i, (i + step) % ring) for i in range(ring)])  80 us
    all_to_all x2, starting transfers between devices, exchange(): lax.all_to_all(rows.reshape(experts, capacity, feat_width), 'expert', spl...  62.2 us
    ppermute x22, waiting for transfers between devices, shift(): lax.ppermute(value, axis, [(i, (i + step) % ring) for i in range(ring)])  29.1 us
    all_to_all x2, waiting for transfers between devices, exchange(): lax.all_to_all(rows.reshape(experts, capacity, feat_width), 'expert', spl...  23.9 us
    pallas_call x1, Pallas kernels, ffn_pair(): pl.pallas_call(functools.partial(pair_body, block=count // 4, later_block...  7.17 us
  transfers between devices with their start and end apart: 24, of which 9 were waited for; matrix products, arithmetic and copies ran while one was open for 2% of the time, Pallas kernels for 5%

profile of v7, /device:TPU:65, one launch (start us, length us, event | category | flops | bytes accessed | tf_op | source)
XLA Modules:
  0.0 218.2 jit_solution(13181196392866056960)
XLA Ops:
  0.0 0.7 add_select_fusion
  0.7 1.6 fusion.5
  2.3 0.8 reshape.41
  3.1 45.2 %all-to-all-start = ((bf16[32,30,128]{2,1,0:T(8,128)(2,1)}), bf16[32,30,128]{2,1,0:T(8,128)(2,1)S(1)}, u32[]{:S(2)}, u32[]{:S(2)}) async-start(bf16[32,30,128]{2,1,0:T(8,128)(2,1)} %reshape.41), calls=%async_computation | async-start | bytes 524288 | tf_op jit(solution)/shard_map/all_to_all | solution.py:239
  48.3 6.9 %collective-permute-start.5 = (bf16[768,128]{1,0:T(8,128)(2,1)S(1)}, bf16[768,128]{1,0:T(8,128)(2,1)S(1)}, u32[]{:S(2)}, u32[]{:S(2)}) collective-permute-start(bf16[768,128]{1,0:T(8,128)(2,1)S(1)} %copy-done), channel_id=1, source_target_pairs={{0,5},{1,6},{2,7},{3,0},{4,1},{5,2},{6,3},{7,4},{8,13},{9,14},{10,... | collective-permute-start | bytes 589832 | tf_op jit(solution)/shard_map/ppermute | solution.py:16
  55.2 2.0 collective-permute-start.4
  57.2 12.5 %all-to-all-done = bf16[32,30,128]{2,1,0:T(8,128)(2,1)S(1)} async-done(((bf16[32,30,128]{2,1,0:T(8,128)(2,1)}), bf16[32,30,128]{2,1,0:T(8,128)(2,1)S(1)}, u32[]{:S(2)}, u32[]{:S(2)}) %all-to-all-start) | async-done | bytes 245792 | tf_op jit(solution)/shard_map/all_to_all | solution.py:239
  69.8 7.6 %collective-permute-start.13 = (bf16[480,128]{1,0:T(8,128)(2,1)S(1)}, bf16[480,128]{1,0:T(8,128)(2,1)S(1)}, u32[]{:S(2)}, u32[]{:S(2)}) collective-permute-start(bf16[480,128]{1,0:T(8,128)(2,1)S(1)} %slice.173.refs_0_), channel_id=1, source_target_pairs={{0,5},{1,6},{2,7},{3,0},{4,1},{5,2},{6,3},{7,4},{8,13},{9,14},{10,... | collective-permute-start | bytes 368648 | tf_op jit(solution)/shard_map/ppermute | solution.py:16
  77.4 2.0 collective-permute-start.12
  79.4 0.0 collective-permute-done.5.refs_10_
  79.4 0.0 collective-permute-done.4.refs_9_
  79.5 6.4 %collective-permute-start.1 = (bf16[480,128]{1,0:T(8,128)(2,1)S(1)}, bf16[480,128]{1,0:T(8,128)(2,1)S(1)}, u32[]{:S(2)}, u32[]{:S(2)}) collective-permute-start(bf16[480,128]{1,0:T(8,128)(2,1)S(1)} %slice.154.refs_0_), channel_id=1, source_target_pairs={{0,5},{1,6},{2,7},{3,0},{4,1},{5,2},{6,3},{7,4},{8,13},{9,14},{10,... | collective-permute-start | bytes 368648 | tf_op jit(solution)/shard_map/ppermute | solution.py:16
  85.9 2.0 collective-permute-start
  87.8 0.0 collective-permute-done.13.refs_2_
  87.9 5.5 %collective-permute-done.12.refs_1_ = bf16[480,128]{1,0:T(8,128)(2,1)S(1)} collective-permute-done((bf16[480,128]{1,0:T(8,128)(2,1)S(1)}, bf16[480,128]{1,0:T(8,128)(2,1)S(1)}, u32[]{:S(2)}, u32[]{:S(2)}) %collective-permute-start.12) | collective-permute-done | bytes 122912 | tf_op jit(solution)/shard_map/ppermute | solution.py:16
  93.4 0.8 fusion.14
  94.2 1.9 collective-permute-start.15
  96.1 1.1 fusion.7
  97.2 2.1 collective-permute-start.7
  99.3 3.4 %collective-permute-start.6 = (bf16[1920,128]{1,0:T(8,128)(2,1)}, bf16[1920,128]{1,0:T(8,128)(2,1)}, u32[]{:S(2)}, u32[]{:S(2)}) collective-permute-start(bf16[1920,128]{1,0:T(8,128)(2,1)} %get-tuple-element.28), channel_id=1, source_target_pairs={{0,1},{1,2},{2,3},{3,4},{4,5},{5,6},{6,7},{7,0},{8,9},{9,10},{10,1... | collective-permute-start | bytes 1474568 | tf_op jit(solution)/shard_map/ppermute | solution.py:16
  102.7 0.0 collective-permute-done.1.refs_2_
  102.7 3.4 %collective-permute-start.14 = (bf16[1200,128]{1,0:T(8,128)(2,1)}, bf16[1200,128]{1,0:T(8,128)(2,1)}, u32[]{:S(2)}, u32[]{:S(2)}) collective-permute-start(bf16[1200,128]{1,0:T(8,128)(2,1)} %get-tuple-element.30), channel_id=1, source_target_pairs={{0,1},{1,2},{2,3},{3,4},{4,5},{5,6},{6,7},{7,0},{8,9},{9,10},{10,1... | collective-permute-start | bytes 921608 | tf_op jit(solution)/shard_map/ppermute | solution.py:16
  106.1 0.0 collective-permute-done.refs_1_
  106.1 0.9 fusion.16
  107.0 3.1 %collective-permute-start.3 = (bf16[1200,128]{1,0:T(8,128)(2,1)}, bf16[1200,128]{1,0:T(8,128)(2,1)S(1)}, u32[]{:S(2)}, u32[]{:S(2)}) collective-permute-start(bf16[1200,128]{1,0:T(8,128)(2,1)} %get-tuple-element.31), channel_id=1, source_target_pairs={{0,7},{1,0},{2,1},{3,2},{4,3},{5,4},{6,5},{7,6},{8,15},{9,8},{10,9... | collective-permute-start | bytes 921608 | tf_op jit(solution)/shard_map/ppermute | solution.py:16
  110.2 0.0 collective-permute-done.15.refs_4_
  110.2 0.7 copy-done.6
  110.9 2.2 collective-permute-start.2
  113.1 8.3 %collective-permute-done.14.refs_3_ = bf16[1200,128]{1,0:T(8,128)(2,1)} collective-permute-done((bf16[1200,128]{1,0:T(8,128)(2,1)}, bf16[1200,128]{1,0:T(8,128)(2,1)}, u32[]{:S(2)}, u32[]{:S(2)}) %collective-permute-start.14) | collective-permute-done | bytes 307232 | tf_op jit(solution)/shard_map/ppermute | solution.py:16
  121.3 1.2 copy-done.2
  122.6 1.0 copy-done.7
  123.5 3.2 %exp.1 = (bf16[1200,128]{1,0:T(8,128)(2,1)S(1)}, bf16[1200,128]{1,0:T(8,128)(2,1)S(1)}, bf16[3,480,128]{2,1,0:T(8,128)(2,1)S(1)}) custom-call(s32[1]{0:T(128)} %bitcast.me_ref, bf16[480,128]{1,0:T(8,128)(2,1)S(1)} %slice.173.refs_0_, bf16[480,128]{1,0:T(8,128)(2,1)S(1)} %collective-permute-done.12.refs_1_, ...), custom_call_target="tpu_custom_call" | custom-call | flops 1006632960 | bytes 4063232 | tf_op jit(solution)/shard_map/exp/pallas_call | solution.py:164
  126.8 2.0 collective-permute-start.16
  128.8 0.0 collective-permute-done.7.refs_12_
  128.8 4.5 %collective-permute-start.17 = (bf16[1200,128]{1,0:T(8,128)(2,1)S(1)}, bf16[1200,128]{1,0:T(8,128)(2,1)S(1)}, u32[]{:S(2)}, u32[]{:S(2)}) collective-permute-start(bf16[1200,128]{1,0:T(8,128)(2,1)S(1)} %get-tuple-element.17), channel_id=1, source_target_pairs={{0,7},{1,0},{2,1},{3,2},{4,3},{5,4},{6,5},{7,6},{8,15},{9,8},{10,9... | collective-permute-start | bytes 921608 | tf_op jit(solution)/shard_map/ppermute | solution.py:16
  133.4 0.0 collective-permute-done.6.refs_11_
  133.4 0.0 collective-permute-done.2.refs_3_
  133.4 7.2 %pair.1 = (bf16[3120,128]{1,0:T(8,128)(2,1)S(1)}, bf16[3120,128]{1,0:T(8,128)(2,1)S(1)}, bf16[3,480,128]{2,1,0:T(8,128)(2,1)S(1)}, bf16[3,768,128]{2,1,0:T(8,128)(2,1)S(1)}) custom-call(s32[1]{0:T(128)} %bitcast.me_ref, bf16[480,128]{1,0:T(8,128)(2,1)S(1)} %slice.154.refs_0_, bf16[480,128]{1,0:T(8,128)(2,1)S(1)} %collective-permute-done.refs_1_, ...), custom_call_target="tpu_custom_call" | custom-call | flops 2617245696 | bytes 7208960 | tf_op jit(solution)/shard_map/pair/pallas_call | solution.py:184
  140.6 2.0 collective-permute-start.8
  142.6 4.6 %collective-permute-start.9 = (bf16[3120,128]{1,0:T(8,128)(2,1)S(1)}, bf16[3120,128]{1,0:T(8,128)(2,1)S(1)}, u32[]{:S(2)}, u32[]{:S(2)}) collective-permute-start(bf16[3120,128]{1,0:T(8,128)(2,1)S(1)} %get-tuple-element.14), channel_id=1, source_target_pairs={{0,7},{1,0},{2,1},{3,2},{4,3},{5,4},{6,5},{7,6},{8,15},{9,8},{10,9... | collective-permute-start | bytes 2396168 | tf_op jit(solution)/shard_map/ppermute | solution.py:16
  147.2 0.0 collective-permute-done.16
  147.2 0.1 convert_add_fusion.7
  147.3 2.0 collective-permute-start.19
  149.3 5.2 %collective-permute-start.18 = (bf16[480,128]{1,0:T(8,128)(2,1)S(1)}, bf16[480,128]{1,0:T(8,128)(2,1)S(1)}, u32[]{:S(2)}, u32[]{:S(2)}) collective-permute-start(bf16[480,128]{1,0:T(8,128)(2,1)S(1)} %pad_maximum_fusion.9), channel_id=1, source_target_pairs={{0,3},{1,4},{2,5},{3,6},{4,7},{5,0},{6,1},{7,2},{8,11},{9,12},{10,... | collective-permute-start | bytes 368648 | tf_op jit(solution)/shard_map/ppermute | solution.py:16
  154.5 6.1 %collective-permute-done.8 = bf16[3120,128]{1,0:T(8,128)(2,1)S(1)} collective-permute-done((bf16[3120,128]{1,0:T(8,128)(2,1)S(1)}, bf16[3120,128]{1,0:T(8,128)(2,1)S(1)}, u32[]{:S(2)}, u32[]{:S(2)}) %collective-permute-start.8) | collective-permute-done | bytes 798752 | tf_op jit(solution)/shard_map/ppermute | solution.py:16
  160.6 2.0 collective-permute-done.9
  162.7 0.1 convert_add_fusion.4
  162.8 2.0 collective-permute-start.21
  164.8 5.2 %collective-permute-start.20 = (bf16[480,128]{1,0:T(8,128)(2,1)S(1)}, bf16[480,128]{1,0:T(8,128)(2,1)S(1)}, u32[]{:S(2)}, u32[]{:S(2)}) collective-permute-start(bf16[480,128]{1,0:T(8,128)(2,1)S(1)} %pad_maximum_fusion.11), channel_id=1, source_target_pairs={{0,3},{1,4},{2,5},{3,6},{4,7},{5,0},{6,1},{7,2},{8,11},{9,12},{10,... | collective-permute-start | bytes 368648 | tf_op jit(solution)/shard_map/ppermute | solution.py:16
  170.0 0.1 fusion.24
  170.1 2.1 collective-permute-done.21
  172.2 1.3 collective-permute-done.20
  173.6 0.1 fusion.20
  173.7 0.8 reshape.43
  174.4 17.0 %all-to-all-start.1 = ((bf16[32,30,128]{2,1,0:T(8,128)(2,1)}), bf16[32,30,128]{2,1,0:T(8,128)(2,1)S(1)}, u32[]{:S(2)}, u32[]{:S(2)}) async-start(bf16[32,30,128]{2,1,0:T(8,128)(2,1)} %reshape.43), calls=%async_computation.1 | async-start | bytes 524288 | tf_op jit(solution)/shard_map/all_to_all | solution.py:239
  191.5 0.1 convert_add_fusion.1
  191.6 0.0 copy-start.9
  191.7 7.8 %collective-permute-start.11 = (bf16[768,128]{1,0:T(8,128)(2,1)S(1)}, bf16[768,128]{1,0:T(8,128)(2,1)S(1)}, u32[]{:S(2)}, u32[]{:S(2)}) collective-permute-start(bf16[768,128]{1,0:T(8,128)(2,1)S(1)} %pad_maximum_fusion.8), channel_id=1, source_target_pairs={{0,5},{1,6},{2,7},{3,0},{4,1},{5,2},{6,3},{7,4},{8,13},{9,14},{10,... | collective-permute-start | bytes 589832 | tf_op jit(solution)/shard_map/ppermute | solution.py:16
  199.5 2.0 collective-permute-start.10
  201.5 11.4 %all-to-all-done.1 = bf16[32,30,128]{2,1,0:T(8,128)(2,1)S(1)} async-done(((bf16[32,30,128]{2,1,0:T(8,128)(2,1)}), bf16[32,30,128]{2,1,0:T(8,128)(2,1)S(1)}, u32[]{:S(2)}, u32[]{:S(2)}) %all-to-all-start.1) | async-done | bytes 245792 | tf_op jit(solution)/shard_map/all_to_all | solution.py:239
  212.9 0.1 reshape.44
  213.0 0.7 fusion.4
  213.7 3.7 %collective-permute-done.10 = bf16[768,128]{1,0:T(8,128)(2,1)S(1)} collective-permute-done((bf16[768,128]{1,0:T(8,128)(2,1)S(1)}, bf16[768,128]{1,0:T(8,128)(2,1)S(1)}, u32[]{:S(2)}, u32[]{:S(2)}) %collective-permute-start.10) | collective-permute-done | bytes 196640 | tf_op jit(solution)/shard_map/ppermute | solution.py:16
  217.4 0.8 fusion.12
  (49 shorter events, 0.5 us)
Async XLA Ops:
  0.7 47.6 %copy-start = (bf16[768,128]{1,0:T(8,128)(2,1)S(1)}, bf16[768,128]{1,0:T(8,128)(2,1)}, u32[]{:S(2)}) copy-start(bf16[768,128]{1,0:T(8,128)(2,1)} %refs_8_.1) | copy-start | bytes 589828
  3.1 66.6 %all-to-all-start = ((bf16[32,30,128]{2,1,0:T(8,128)(2,1)}), bf16[32,30,128]{2,1,0:T(8,128)(2,1)S(1)}, u32[]{:S(2)}, u32[]{:S(2)}) async-start(bf16[32,30,128]{2,1,0:T(8,128)(2,1)} %reshape.41), calls=%async_computation | async-start | bytes 524288 | tf_op jit(solution)/shard_map/all_to_all | solution.py:239
  48.3 31.1 %collective-permute-start.5 = (bf16[768,128]{1,0:T(8,128)(2,1)S(1)}, bf16[768,128]{1,0:T(8,128)(2,1)S(1)}, u32[]{:S(2)}, u32[]{:S(2)}) collective-permute-start(bf16[768,128]{1,0:T(8,128)(2,1)S(1)} %copy-done), channel_id=1, source_target_pairs={{0,5},{1,6},{2,7},{3,0},{4,1},{5,2},{6,3},{7,4},{8,13},{9,14},{10,... | collective-permute-start | bytes 589832 | tf_op jit(solution)/shard_map/ppermute | solution.py:16
  55.2 24.2 %collective-permute-start.4 = (bf16[768,128]{1,0:T(8,128)(2,1)S(1)}, bf16[768,128]{1,0:T(8,128)(2,1)S(1)}, u32[]{:S(2)}, u32[]{:S(2)}) collective-permute-start(bf16[768,128]{1,0:T(8,128)(2,1)S(1)} %copy-done), channel_id=1, source_target_pairs={{0,3},{1,4},{2,5},{3,6},{4,7},{5,0},{6,1},{7,2},{8,11},{9,12},{10,... | collective-permute-start | bytes 589832 | tf_op jit(solution)/shard_map/ppermute | solution.py:16
  69.8 18.0 %collective-permute-start.13 = (bf16[480,128]{1,0:T(8,128)(2,1)S(1)}, bf16[480,128]{1,0:T(8,128)(2,1)S(1)}, u32[]{:S(2)}, u32[]{:S(2)}) collective-permute-start(bf16[480,128]{1,0:T(8,128)(2,1)S(1)} %slice.173.refs_0_), channel_id=1, source_target_pairs={{0,5},{1,6},{2,7},{3,0},{4,1},{5,2},{6,3},{7,4},{8,13},{9,14},{10,... | collective-permute-start | bytes 368648 | tf_op jit(solution)/shard_map/ppermute | solution.py:16
  77.4 16.0 %collective-permute-start.12 = (bf16[480,128]{1,0:T(8,128)(2,1)S(1)}, bf16[480,128]{1,0:T(8,128)(2,1)S(1)}, u32[]{:S(2)}, u32[]{:S(2)}) collective-permute-start(bf16[480,128]{1,0:T(8,128)(2,1)S(1)} %slice.173.refs_0_), channel_id=1, source_target_pairs={{0,3},{1,4},{2,5},{3,6},{4,7},{5,0},{6,1},{7,2},{8,11},{9,12},{10,... | collective-permute-start | bytes 368648 | tf_op jit(solution)/shard_map/ppermute | solution.py:16
  79.5 23.2 %collective-permute-start.1 = (bf16[480,128]{1,0:T(8,128)(2,1)S(1)}, bf16[480,128]{1,0:T(8,128)(2,1)S(1)}, u32[]{:S(2)}, u32[]{:S(2)}) collective-permute-start(bf16[480,128]{1,0:T(8,128)(2,1)S(1)} %slice.154.refs_0_), channel_id=1, source_target_pairs={{0,5},{1,6},{2,7},{3,0},{4,1},{5,2},{6,3},{7,4},{8,13},{9,14},{10,... | collective-permute-start | bytes 368648 | tf_op jit(solution)/shard_map/ppermute | solution.py:16
  85.9 20.2 %collective-permute-start = (bf16[480,128]{1,0:T(8,128)(2,1)S(1)}, bf16[480,128]{1,0:T(8,128)(2,1)S(1)}, u32[]{:S(2)}, u32[]{:S(2)}) collective-permute-start(bf16[480,128]{1,0:T(8,128)(2,1)S(1)} %slice.154.refs_0_), channel_id=1, source_target_pairs={{0,3},{1,4},{2,5},{3,6},{4,7},{5,0},{6,1},{7,2},{8,11},{9,12},{10,... | collective-permute-start | bytes 368648 | tf_op jit(solution)/shard_map/ppermute | solution.py:16
  94.2 16.0 %collective-permute-start.15 = (bf16[1200,128]{1,0:T(8,128)(2,1)S(1)}, bf16[1200,128]{1,0:T(8,128)(2,1)S(1)}, u32[]{:S(2)}, u32[]{:S(2)}) collective-permute-start(bf16[1200,128]{1,0:T(8,128)(2,1)S(1)} %get-tuple-element.29), channel_id=1, source_target_pairs={{0,7},{1,0},{2,1},{3,2},{4,3},{5,4},{6,5},{7,6},{8,15},{9,8},{10,9... | collective-permute-start | bytes 921608 | tf_op jit(solution)/shard_map/ppermute | solution.py:16
  97.2 24.1 %copy-start.1 = (bf16[1,1024,512]{2,1,0:T(8,128)(2,1)S(1)}, bf16[1,1024,512]{2,1,0:T(8,128)(2,1)}, u32[]{:S(2)}) copy-start(bf16[1,1024,512]{2,1,0:T(8,128)(2,1)} %param.13) | copy-start | bytes 3145732
  97.2 24.1 %copy-start.8 = (f32[1024]{0:T(1024)S(1)}, f32[1024]{0:T(1024)}, u32[]{:S(2)}) copy-start(f32[1024]{0:T(1024)} %param.10) | copy-start | bytes 12292
  97.2 31.6 %collective-permute-start.7 = (bf16[1920,128]{1,0:T(8,128)(2,1)}, bf16[1920,128]{1,0:T(8,128)(2,1)S(1)}, u32[]{:S(2)}, u32[]{:S(2)}) collective-permute-start(bf16[1920,128]{1,0:T(8,128)(2,1)} %get-tuple-element.27), channel_id=1, source_target_pairs={{0,7},{1,0},{2,1},{3,2},{4,3},{5,4},{6,5},{7,6},{8,15},{9,8},{10,9... | collective-permute-start | bytes 1474568 | tf_op jit(solution)/shard_map/ppermute | solution.py:16
  99.3 34.1 %collective-permute-start.6 = (bf16[1920,128]{1,0:T(8,128)(2,1)}, bf16[1920,128]{1,0:T(8,128)(2,1)}, u32[]{:S(2)}, u32[]{:S(2)}) collective-permute-start(bf16[1920,128]{1,0:T(8,128)(2,1)} %get-tuple-element.28), channel_id=1, source_target_pairs={{0,1},{1,2},{2,3},{3,4},{4,5},{5,6},{6,7},{7,0},{8,9},{9,10},{10,1... | collective-permute-start | bytes 1474568 | tf_op jit(solution)/shard_map/ppermute | solution.py:16
  102.7 18.6 %collective-permute-start.14 = (bf16[1200,128]{1,0:T(8,128)(2,1)}, bf16[1200,128]{1,0:T(8,128)(2,1)}, u32[]{:S(2)}, u32[]{:S(2)}) collective-permute-start(bf16[1200,128]{1,0:T(8,128)(2,1)} %get-tuple-element.30), channel_id=1, source_target_pairs={{0,1},{1,2},{2,3},{3,4},{4,5},{5,6},{6,7},{7,0},{8,9},{9,10},{10,1... | collective-permute-start | bytes 921608 | tf_op jit(solution)/shard_map/ppermute | solution.py:16
  107.0 26.4 %collective-permute-start.3 = (bf16[1200,128]{1,0:T(8,128)(2,1)}, bf16[1200,128]{1,0:T(8,128)(2,1)S(1)}, u32[]{:S(2)}, u32[]{:S(2)}) collective-permute-start(bf16[1200,128]{1,0:T(8,128)(2,1)} %get-tuple-element.31), channel_id=1, source_target_pairs={{0,7},{1,0},{2,1},{3,2},{4,3},{5,4},{6,5},{7,6},{8,15},{9,8},{10,9... | collective-permute-start | bytes 921608 | tf_op jit(solution)/shard_map/ppermute | solution.py:16
  110.2 0.7 copy-start.6
  110.9 22.5 %collective-permute-start.2 = (bf16[1200,128]{1,0:T(8,128)(2,1)}, bf16[1200,128]{1,0:T(8,128)(2,1)}, u32[]{:S(2)}, u32[]{:S(2)}) collective-permute-start(bf16[1200,128]{1,0:T(8,128)(2,1)} %get-tuple-element.32), channel_id=1, source_target_pairs={{0,1},{1,2},{2,3},{3,4},{4,5},{5,6},{6,7},{7,0},{8,9},{9,10},{10,1... | collective-permute-start | bytes 921608 | tf_op jit(solution)/shard_map/ppermute | solution.py:16
  121.3 1.2 copy-start.2
  122.6 1.0 copy-start.7
  123.5 9.9 %copy-start.3 = (bf16[1,512,1024]{2,1,0:T(8,128)(2,1)S(1)}, bf16[1,512,1024]{2,1,0:T(8,128)(2,1)}, u32[]{:S(2)}) copy-start(bf16[1,512,1024]{2,1,0:T(8,128)(2,1)} %param.14) | copy-start | bytes 3145732
  123.5 9.9 %copy-start.4 = (bf16[1024,512]{1,0:T(8,128)(2,1)S(1)}, bf16[1024,512]{1,0:T(8,128)(2,1)}, u32[]{:S(2)}) copy-start(bf16[1024,512]{1,0:T(8,128)(2,1)} %refs_13_.1) | copy-start | bytes 3145732
  123.5 9.9 %copy-start.5 = (bf16[512,1024]{1,0:T(8,128)(2,1)S(1)}, bf16[512,1024]{1,0:T(8,128)(2,1)}, u32[]{:S(2)}) copy-start(bf16[512,1024]{1,0:T(8,128)(2,1)} %refs_14_.1) | copy-start | bytes 3145732
  126.8 20.4 %collective-permute-start.16 = (bf16[1200,128]{1,0:T(8,128)(2,1)S(1)}, bf16[1200,128]{1,0:T(8,128)(2,1)S(1)}, u32[]{:S(2)}, u32[]{:S(2)}) collective-permute-start(bf16[1200,128]{1,0:T(8,128)(2,1)S(1)} %get-tuple-element.16), channel_id=1, source_target_pairs={{0,1},{1,2},{2,3},{3,4},{4,5},{5,6},{6,7},{7,0},{8,9},{9,10},{10,1... | collective-permute-start | bytes 921608 | tf_op jit(solution)/shard_map/ppermute | solution.py:16
  128.8 18.3 %collective-permute-start.17 = (bf16[1200,128]{1,0:T(8,128)(2,1)S(1)}, bf16[1200,128]{1,0:T(8,128)(2,1)S(1)}, u32[]{:S(2)}, u32[]{:S(2)}) collective-permute-start(bf16[1200,128]{1,0:T(8,128)(2,1)S(1)} %get-tuple-element.17), channel_id=1, source_target_pairs={{0,7},{1,0},{2,1},{3,2},{4,3},{5,4},{6,5},{7,6},{8,15},{9,8},{10,9... | collective-permute-start | bytes 921608 | tf_op jit(solution)/shard_map/ppermute | solution.py:16
  140.6 20.0 %collective-permute-start.8 = (bf16[3120,128]{1,0:T(8,128)(2,1)S(1)}, bf16[3120,128]{1,0:T(8,128)(2,1)S(1)}, u32[]{:S(2)}, u32[]{:S(2)}) collective-permute-start(bf16[3120,128]{1,0:T(8,128)(2,1)S(1)} %get-tuple-element.13), channel_id=1, source_target_pairs={{0,1},{1,2},{2,3},{3,4},{4,5},{5,6},{6,7},{7,0},{8,9},{9,10},{10,1... | collective-permute-start | bytes 2396168 | tf_op jit(solution)/shard_map/ppermute | solution.py:16
  142.6 20.1 %collective-permute-start.9 = (bf16[3120,128]{1,0:T(8,128)(2,1)S(1)}, bf16[3120,128]{1,0:T(8,128)(2,1)S(1)}, u32[]{:S(2)}, u32[]{:S(2)}) collective-permute-start(bf16[3120,128]{1,0:T(8,128)(2,1)S(1)} %get-tuple-element.14), channel_id=1, source_target_pairs={{0,7},{1,0},{2,1},{3,2},{4,3},{5,4},{6,5},{7,6},{8,15},{9,8},{10,9... | collective-permute-start | bytes 2396168 | tf_op jit(solution)/shard_map/ppermute | solution.py:16
  147.3 22.7 %collective-permute-start.19 = (bf16[480,128]{1,0:T(8,128)(2,1)S(1)}, bf16[480,128]{1,0:T(8,128)(2,1)S(1)}, u32[]{:S(2)}, u32[]{:S(2)}) collective-permute-start(bf16[480,128]{1,0:T(8,128)(2,1)S(1)} %pad_maximum_fusion.10), channel_id=1, source_target_pairs={{0,5},{1,6},{2,7},{3,0},{4,1},{5,2},{6,3},{7,4},{8,13},{9,14},{10,... | collective-permute-start | bytes 368648 | tf_op jit(solution)/shard_map/ppermute | solution.py:16
  149.3 20.7 %collective-permute-start.18 = (bf16[480,128]{1,0:T(8,128)(2,1)S(1)}, bf16[480,128]{1,0:T(8,128)(2,1)S(1)}, u32[]{:S(2)}, u32[]{:S(2)}) collective-permute-start(bf16[480,128]{1,0:T(8,128)(2,1)S(1)} %pad_maximum_fusion.9), channel_id=1, source_target_pairs={{0,3},{1,4},{2,5},{3,6},{4,7},{5,0},{6,1},{7,2},{8,11},{9,12},{10,... | collective-permute-start | bytes 368648 | tf_op jit(solution)/shard_map/ppermute | solution.py:16
  162.8 9.4 %collective-permute-start.21 = (bf16[480,128]{1,0:T(8,128)(2,1)S(1)}, bf16[480,128]{1,0:T(8,128)(2,1)S(1)}, u32[]{:S(2)}, u32[]{:S(2)}) collective-permute-start(bf16[480,128]{1,0:T(8,128)(2,1)S(1)} %pad_maximum_fusion.12), channel_id=1, source_target_pairs={{0,5},{1,6},{2,7},{3,0},{4,1},{5,2},{6,3},{7,4},{8,13},{9,14},{10,... | collective-permute-start | bytes 368648 | tf_op jit(solution)/shard_map/ppermute | solution.py:16
  164.8 8.8 %collective-permute-start.20 = (bf16[480,128]{1,0:T(8,128)(2,1)S(1)}, bf16[480,128]{1,0:T(8,128)(2,1)S(1)}, u32[]{:S(2)}, u32[]{:S(2)}) collective-permute-start(bf16[480,128]{1,0:T(8,128)(2,1)S(1)} %pad_maximum_fusion.11), channel_id=1, source_target_pairs={{0,3},{1,4},{2,5},{3,6},{4,7},{5,0},{6,1},{7,2},{8,11},{9,12},{10,... | collective-permute-start | bytes 368648 | tf_op jit(solution)/shard_map/ppermute | solution.py:16
  174.4 38.5 %all-to-all-start.1 = ((bf16[32,30,128]{2,1,0:T(8,128)(2,1)}), bf16[32,30,128]{2,1,0:T(8,128)(2,1)S(1)}, u32[]{:S(2)}, u32[]{:S(2)}) async-start(bf16[32,30,128]{2,1,0:T(8,128)(2,1)} %reshape.43), calls=%async_computation.1 | async-start | bytes 524288 | tf_op jit(solution)/shard_map/all_to_all | solution.py:239
  191.6 21.4 %copy-start.9 = (f32[768]{0:T(1024)S(1)}, f32[768]{0:T(1024)}, u32[]{:S(2)}) copy-start(f32[768]{0:T(1024)} %param.17) | copy-start | bytes 9220
  191.7 22.0 %collective-permute-start.11 = (bf16[768,128]{1,0:T(8,128)(2,1)S(1)}, bf16[768,128]{1,0:T(8,128)(2,1)S(1)}, u32[]{:S(2)}, u32[]{:S(2)}) collective-permute-start(bf16[768,128]{1,0:T(8,128)(2,1)S(1)} %pad_maximum_fusion.8), channel_id=1, source_target_pairs={{0,5},{1,6},{2,7},{3,0},{4,1},{5,2},{6,3},{7,4},{8,13},{9,14},{10,... | collective-permute-start | bytes 589832 | tf_op jit(solution)/shard_map/ppermute | solution.py:16
  199.5 17.9 %collective-permute-start.10 = (bf16[768,128]{1,0:T(8,128)(2,1)S(1)}, bf16[768,128]{1,0:T(8,128)(2,1)S(1)}, u32[]{:S(2)}, u32[]{:S(2)}) collective-permute-start(bf16[768,128]{1,0:T(8,128)(2,1)S(1)} %pad_maximum_fusion.7), channel_id=1, source_target_pairs={{0,3},{1,4},{2,5},{3,6},{4,7},{5,0},{6,1},{7,2},{8,11},{9,12},{10,... | collective-permute-start | bytes 589832 | tf_op jit(solution)/shard_map/ppermute | solution.py:16

commit v8 on v7

--- a/solution.py
+++ b/solution.py
@@ -43,15 +43,13 @@
     rows_ref,
     sums_ref,
     block,
-    base,
 ):
     count, width = own_ref.shape
     half = count // 2
     place = [lax.rem(me + step, RING) for step in range(RING)]
     for start in range(0, count, block):
         at = pl.ds(start, block)
-        first = pl.ds(base + start, block)
-        second = pl.ds(base + count + start, block)
+        second = pl.ds(count + start, block)
         rows_ref[place[0], at] = own_ref[at]
         rows_ref[place[1], at] = right_ref[at]
         rows_ref[place[7], at] = left_ref[at]
@@ -73,14 +71,14 @@
         sums = sums.astype(jnp.bfloat16)
         for k in range(RING):
             sums_ref[k, at] = sums[:, k * width : (k + 1) * width]
-        to_right_ref[first] = sums_ref[place[1], at]
+        to_right_ref[at] = sums_ref[place[1], at]
         to_right_ref[second] = sums_ref[place[6], at]
-        to_left_ref[first] = sums_ref[place[7], at]
+        to_left_ref[at] = sums_ref[place[7], at]
         to_left_ref[second] = sums_ref[place[2], at]
         if start < half:
-            to_right_ref[pl.ds(base + 2 * count + start, block)] = sums_ref[place[4], at]
+            to_right_ref[pl.ds(2 * count + start, block)] = sums_ref[place[4], at]
         else:
-            third = pl.ds(base + 2 * count + start - half, block)
+            third = pl.ds(2 * count + start - half, block)
             to_left_ref[third] = sums_ref[place[4], at]
         keep_ref[0, at] = sums_ref[place[0], at]
         keep_ref[1, at] = sums_ref[place[3], at]
@@ -88,16 +86,17 @@
 
 
 def ffn_body(me_ref, *refs, block):
-    branch(me_ref[0], *refs, block, 0)
+    branch(me_ref[0], *refs, block)
 
 
 def pair_body(me_ref, *refs, block, later_block):
     own, below, above, left, right, gain, w_in, w_out = refs[:8]
     sources = refs[8:15]
-    to_right, to_left, keep, later_keep = refs[15:19]
-    rows, sums, later_rows, later_sums = refs[19:23]
-    targets = refs[23:30]
-    done = refs[30]
+    to_right, to_left, keep = refs[15:18]
+    later_outs = refs[18:21]
+    rows, sums, later_rows, later_sums = refs[21:25]
+    targets = refs[25:32]
+    done = refs[32]
     copies = [
         pltpu.make_async_copy(source, target, done.at[n])
         for n, (source, target) in enumerate(zip(sources, targets))
@@ -121,7 +120,6 @@
         rows,
         sums,
         block,
-        0,
     )
     for copy in copies:
         copy.wait()
@@ -130,13 +128,10 @@
         *targets[:5],
         gain,
         *targets[5:],
-        to_right,
-        to_left,
-        later_keep,
+        *later_outs,
         later_rows,
         later_sums,
         later_block,
-        5 * own.shape[0] // 2,
     )
 
 
@@ -179,13 +174,15 @@
     model = RING * width
     vmem = pl.BlockSpec(memory_space=pltpu.VMEM)
     anywhere = pl.BlockSpec(memory_space=pl.ANY)
-    edge = jax.ShapeDtypeStruct((5 * (count + later) // 2, width), jnp.bfloat16)
+    edge = jax.ShapeDtypeStruct((5 * count // 2, width), jnp.bfloat16)
+    later_edge = jax.ShapeDtypeStruct((5 * later // 2, width), jnp.bfloat16)
     operands = [*later_pieces, later_in, later_out]
     return pl.pallas_call(
         functools.partial(pair_body, block=count // 4, later_block=later // 4),
         in_specs=[pl.BlockSpec(memory_space=pltpu.SMEM)] + [vmem] * 8 + [anywhere] * 7,
-        out_specs=[vmem] * 4,
-        out_shape=[edge, edge, sums_of(count, width), sums_of(later, width)],
+        out_specs=[vmem] * 6,
+        out_shape=[edge, edge, sums_of(count, width)]
+        + [later_edge, later_edge, sums_of(later, width)],
         scratch_shapes=[tiles_of(count, width)] * 2
         + [tiles_of(later, width)] * 2
         + [pltpu.VMEM(value.shape, value.dtype) for value in operands]
@@ -200,15 +197,15 @@
     return shift(to_right, 1), shift(to_left, -1)
 
 
-def scatter_far(keep, from_left, from_right, base=0):
+def scatter_far(keep, from_left, from_right):
     count = keep.shape[1]
     half = count // 2
-    one, two = base + count, base + 2 * count
+    one, two = count, 2 * count
 
     def wide(value):
         return value.astype(jnp.float32)
 
-    own = wide(keep[0]) + wide(from_left[base:one]) + wide(from_right[base:one])
+    own = wide(keep[0]) + wide(from_left[:one]) + wide(from_right[:one])
     above = wide(keep[1]) + wide(from_right[one:two])
     to_above = jnp.concatenate(
         [above[:half] + wide(from_left[two : two + half]), above[half:]], axis=0
@@ -260,7 +257,7 @@
         pieces.append((rows, below, above, left, right))
     to_right, to_left, keep_0 = ffn(me, pieces[0], gain, w_exp_in[0], w_exp_out[0])
     edges_0 = scatter_near(to_right, to_left)
-    to_right, to_left, keep_1, res_keep = ffn_pair(
+    to_right, to_left, keep_1, res_to_right, res_to_left, res_keep = ffn_pair(
         me,
         pieces[1],
         gain,
@@ -271,6 +268,7 @@
         w_res_out,
     )
     edges_1 = scatter_near(to_right, to_left)
+    res_edges = scatter_near(res_to_right, res_to_left)
     summed = []
     for keep, edges in ((keep_0, edges_0), (keep_1, edges_1)):
         own, first, second = scatter_far(keep, *edges)
@@ -278,7 +276,7 @@
         summed.append(own.astype(jnp.bfloat16))
 
     returned = exchange(jnp.concatenate(summed, axis=0))
-    res_own, res_first, res_second = scatter_far(res_keep, *edges_1, 5 * chunk // 2)
+    res_own, res_first, res_second = scatter_far(res_keep, *res_edges)
     res_sum = res_own + res_first.astype(jnp.float32) + res_second.astype(jnp.float32)
     moe_value = jnp.dot(take_table, returned, preferred_element_type=jnp.float32)
     return (res_sum + gate_prob[:, None] * moe_value).astype(jnp.bfloat16)

time: 220 us -> 225 us (1.023)
    ppermute x22 -> x24, starting transfers between devices: 80 us -> 83.3 us  [shift(): lax.ppermute(value, axis, [(i, (i + step) % ring) for i in range(ring)])]
    unnamed x20 -> x24, local copies, waits for them, and re-layouts: 2.92 us -> 4.75 us
    ppermute x22 -> x24, waiting for transfers between devices: 29.1 us -> 28.5 us  [shift(): lax.ppermute(value, axis, [(i, (i + step) % ring) for i in range(ring)])]
  transfers between devices with their start and end apart: 24 -> 26, of which waited for: 9 -> 8; matrix products, arithmetic and copies ran while one was open for 2% -> 2% of each run, Pallas kernels for 5% -> 5%
where the time goes in v8:
time: 225 us; the launch traced here: 223 us
  starting transfers between devices  144 us (64%)
  waiting for transfers between devices  53.6 us (24%)
  Pallas kernels  11.1 us (5%)
  local copies, waits for them, and re-layouts  6.57 us (3%)
  other arithmetic  4.8 us (2%)
  matrix products  2.32 us (1%)
    ppermute x24, starting transfers between devices, shift(): lax.ppermute(value, axis, [(i, (i + step) % ring) for i in range(ring)])  83.3 us
    all_to_all x2, starting transfers between devices, exchange(): lax.all_to_all(rows.reshape(experts, capacity, feat_width), 'expert', spl...  61 us
    ppermute x24, waiting for transfers between devices, shift(): lax.ppermute(value, axis, [(i, (i + step) % ring) for i in range(ring)])  28.5 us
    all_to_all x2, waiting for transfers between devices, exchange(): lax.all_to_all(rows.reshape(experts, capacity, feat_width), 'expert', spl...  25.1 us
    pallas_call x1, Pallas kernels, ffn_pair(): pl.pallas_call(functools.partial(pair_body, block=count // 4, later_block...  7.89 us
    unnamed x24, local copies, waits for them, and re-layouts  4.75 us
  transfers between devices with their start and end apart: 26, of which 8 were waited for; matrix products, arithmetic and copies ran while one was open for 2% of the time, Pallas kernels for 5%

profile of v8, /device:TPU:65, one launch (start us, length us, event | category | flops | bytes accessed | tf_op | source)
XLA Modules:
  0.0 223.5 jit_solution(2653819354120137129)
XLA Ops:
  0.0 0.7 add_select_fusion
  0.7 1.6 fusion.5
  2.3 0.8 reshape.41
  3.1 45.2 %all-to-all-start = ((bf16[32,30,128]{2,1,0:T(8,128)(2,1)}), bf16[32,30,128]{2,1,0:T(8,128)(2,1)S(1)}, u32[]{:S(2)}, u32[]{:S(2)}) async-start(bf16[32,30,128]{2,1,0:T(8,128)(2,1)} %reshape.41), calls=%async_computation | async-start | bytes 524288 | tf_op jit(solution)/shard_map/all_to_all | solution.py:236
  48.3 6.9 %collective-permute-start.5 = (bf16[768,128]{1,0:T(8,128)(2,1)S(1)}, bf16[768,128]{1,0:T(8,128)(2,1)S(1)}, u32[]{:S(2)}, u32[]{:S(2)}) collective-permute-start(bf16[768,128]{1,0:T(8,128)(2,1)S(1)} %copy-done), channel_id=1, source_target_pairs={{0,5},{1,6},{2,7},{3,0},{4,1},{5,2},{6,3},{7,4},{8,13},{9,14},{10,... | collective-permute-start | bytes 589832 | tf_op jit(solution)/shard_map/ppermute | solution.py:16
  55.3 2.0 collective-permute-start.4
  57.2 12.5 %all-to-all-done = bf16[32,30,128]{2,1,0:T(8,128)(2,1)S(1)} async-done(((bf16[32,30,128]{2,1,0:T(8,128)(2,1)}), bf16[32,30,128]{2,1,0:T(8,128)(2,1)S(1)}, u32[]{:S(2)}, u32[]{:S(2)}) %all-to-all-start) | async-done | bytes 245792 | tf_op jit(solution)/shard_map/all_to_all | solution.py:236
  69.8 7.6 %collective-permute-start.13 = (bf16[480,128]{1,0:T(8,128)(2,1)S(1)}, bf16[480,128]{1,0:T(8,128)(2,1)S(1)}, u32[]{:S(2)}, u32[]{:S(2)}) collective-permute-start(bf16[480,128]{1,0:T(8,128)(2,1)S(1)} %slice.173.refs_0_), channel_id=1, source_target_pairs={{0,5},{1,6},{2,7},{3,0},{4,1},{5,2},{6,3},{7,4},{8,13},{9,14},{10,... | collective-permute-start | bytes 368648 | tf_op jit(solution)/shard_map/ppermute | solution.py:16
  77.4 2.0 collective-permute-start.12
  79.4 0.0 collective-permute-done.5.refs_10_
  79.5 6.4 %collective-permute-start.1 = (bf16[480,128]{1,0:T(8,128)(2,1)S(1)}, bf16[480,128]{1,0:T(8,128)(2,1)S(1)}, u32[]{:S(2)}, u32[]{:S(2)}) collective-permute-start(bf16[480,128]{1,0:T(8,128)(2,1)S(1)} %slice.154.refs_0_), channel_id=1, source_target_pairs={{0,5},{1,6},{2,7},{3,0},{4,1},{5,2},{6,3},{7,4},{8,13},{9,14},{10,... | collective-permute-start | bytes 368648 | tf_op jit(solution)/shard_map/ppermute | solution.py:16
  85.9 2.0 collective-permute-start
  87.8 0.0 collective-permute-done.13.refs_2_
  87.9 5.5 %collective-permute-done.12.refs_1_ = bf16[480,128]{1,0:T(8,128)(2,1)S(1)} collective-permute-done((bf16[480,128]{1,0:T(8,128)(2,1)S(1)}, bf16[480,128]{1,0:T(8,128)(2,1)S(1)}, u32[]{:S(2)}, u32[]{:S(2)}) %collective-permute-start.12) | collective-permute-done | bytes 122912 | tf_op jit(solution)/shard_map/ppermute | solution.py:16
  93.4 0.8 fusion.14
  94.2 1.9 collective-permute-start.15
  96.1 1.0 fusion.7
  97.2 2.1 collective-permute-start.7
  99.2 3.4 %collective-permute-start.6 = (bf16[1920,128]{1,0:T(8,128)(2,1)}, bf16[1920,128]{1,0:T(8,128)(2,1)}, u32[]{:S(2)}, u32[]{:S(2)}) collective-permute-start(bf16[1920,128]{1,0:T(8,128)(2,1)} %get-tuple-element.32), channel_id=1, source_target_pairs={{0,1},{1,2},{2,3},{3,4},{4,5},{5,6},{6,7},{7,0},{8,9},{9,10},{10,1... | collective-permute-start | bytes 1474568 | tf_op jit(solution)/shard_map/ppermute | solution.py:16
  102.6 3.4 %collective-permute-start.14 = (bf16[1200,128]{1,0:T(8,128)(2,1)}, bf16[1200,128]{1,0:T(8,128)(2,1)}, u32[]{:S(2)}, u32[]{:S(2)}) collective-permute-start(bf16[1200,128]{1,0:T(8,128)(2,1)} %get-tuple-element.34), channel_id=1, source_target_pairs={{0,1},{1,2},{2,3},{3,4},{4,5},{5,6},{6,7},{7,0},{8,9},{9,10},{10,1... | collective-permute-start | bytes 921608 | tf_op jit(solution)/shard_map/ppermute | solution.py:16
  106.1 0.9 fusion.16
  107.0 3.1 %collective-permute-start.3 = (bf16[1200,128]{1,0:T(8,128)(2,1)}, bf16[1200,128]{1,0:T(8,128)(2,1)S(1)}, u32[]{:S(2)}, u32[]{:S(2)}) collective-permute-start(bf16[1200,128]{1,0:T(8,128)(2,1)} %get-tuple-element.35), channel_id=1, source_target_pairs={{0,7},{1,0},{2,1},{3,2},{4,3},{5,4},{6,5},{7,6},{8,15},{9,8},{10,9... | collective-permute-start | bytes 921608 | tf_op jit(solution)/shard_map/ppermute | solution.py:16
  110.1 0.0 collective-permute-done.15.refs_4_
  110.1 0.7 copy-done.8
  110.9 2.2 collective-permute-start.2
  113.0 8.2 %collective-permute-done.14.refs_3_ = bf16[1200,128]{1,0:T(8,128)(2,1)} collective-permute-done((bf16[1200,128]{1,0:T(8,128)(2,1)}, bf16[1200,128]{1,0:T(8,128)(2,1)}, u32[]{:S(2)}, u32[]{:S(2)}) %collective-permute-start.14) | collective-permute-done | bytes 307232 | tf_op jit(solution)/shard_map/ppermute | solution.py:16
  121.3 1.2 copy-done.2
  122.5 1.0 copy-done.9
  123.5 3.2 %exp.1 = (bf16[1200,128]{1,0:T(8,128)(2,1)S(1)}, bf16[1200,128]{1,0:T(8,128)(2,1)S(1)}, bf16[3,480,128]{2,1,0:T(8,128)(2,1)S(1)}) custom-call(s32[1]{0:T(128)} %bitcast.me_ref, bf16[480,128]{1,0:T(8,128)(2,1)S(1)} %slice.173.refs_0_, bf16[480,128]{1,0:T(8,128)(2,1)S(1)} %collective-permute-done.12.refs_1_, ...), custom_call_target="tpu_custom_call" | custom-call | flops 1006632960 | bytes 4063232 | tf_op jit(solution)/shard_map/exp/pallas_call | solution.py:159
  126.7 2.1 collective-permute-start.16
  128.8 0.8 copy-done.6
  129.6 4.5 %collective-permute-start.17 = (bf16[1200,128]{1,0:T(8,128)(2,1)S(1)}, bf16[1200,128]{1,0:T(8,128)(2,1)S(1)}, u32[]{:S(2)}, u32[]{:S(2)}) collective-permute-start(bf16[1200,128]{1,0:T(8,128)(2,1)S(1)} %get-tuple-element.19), channel_id=1, source_target_pairs={{0,7},{1,0},{2,1},{3,2},{4,3},{5,4},{6,5},{7,6},{8,15},{9,8},{10,9... | collective-permute-start | bytes 921608 | tf_op jit(solution)/shard_map/ppermute | solution.py:16
  134.1 0.0 collective-permute-done.3.refs_4_
  134.1 0.0 collective-permute-done.2.refs_3_
  134.2 1.0 copy-done.7
  135.2 7.9 %pair.1 = (bf16[1200,128]{1,0:T(8,128)(2,1)S(1)}, bf16[1200,128]{1,0:T(8,128)(2,1)S(1)}, bf16[3,480,128]{2,1,0:T(8,128)(2,1)S(1)}, bf16[1920,128]{1,0:T(8,128)(2...) custom-call(s32[1]{0:T(128)} %bitcast.me_ref, bf16[480,128]{1,0:T(8,128)(2,1)S(1)} %slice.154.refs_0_, ...), custom_call_target="tpu_custom_call" | custom-call | flops 2617245696 | bytes 7208960 | tf_op jit(solution)/shard_map/pair/pallas_call | solution.py:180
  143.1 2.0 collective-permute-start.20
  145.0 4.6 %collective-permute-start.21 = (bf16[1200,128]{1,0:T(8,128)(2,1)S(1)}, bf16[1200,128]{1,0:T(8,128)(2,1)S(1)}, u32[]{:S(2)}, u32[]{:S(2)}) collective-permute-start(bf16[1200,128]{1,0:T(8,128)(2,1)S(1)} %get-tuple-element.22), channel_id=1, source_target_pairs={{0,7},{1,0},{2,1},{3,2},{4,3},{5,4},{6,5},{7,6},{8,15},{9,8},{10,9... | collective-permute-start | bytes 921608 | tf_op jit(solution)/shard_map/ppermute | solution.py:16
  149.6 2.0 collective-permute-start.8
  151.6 4.6 %collective-permute-start.9 = (bf16[1920,128]{1,0:T(8,128)(2,1)S(1)}, bf16[1920,128]{1,0:T(8,128)(2,1)S(1)}, u32[]{:S(2)}, u32[]{:S(2)}) collective-permute-start(bf16[1920,128]{1,0:T(8,128)(2,1)S(1)} %get-tuple-element.16), channel_id=1, source_target_pairs={{0,7},{1,0},{2,1},{3,2},{4,3},{5,4},{6,5},{7,6},{8,15},{9,8},{10,9... | collective-permute-start | bytes 1474568 | tf_op jit(solution)/shard_map/ppermute | solution.py:16
  156.2 0.1 convert_add_fusion.7
  156.4 2.0 collective-permute-start.19
  158.4 0.0 collective-permute-done.20
  158.4 5.2 %collective-permute-start.18 = (bf16[480,128]{1,0:T(8,128)(2,1)S(1)}, bf16[480,128]{1,0:T(8,128)(2,1)S(1)}, u32[]{:S(2)}, u32[]{:S(2)}) collective-permute-start(bf16[480,128]{1,0:T(8,128)(2,1)S(1)} %pad_maximum_fusion.9), channel_id=1, source_target_pairs={{0,3},{1,4},{2,5},{3,6},{4,7},{5,0},{6,1},{7,2},{8,11},{9,12},{10,... | collective-permute-start | bytes 368648 | tf_op jit(solution)/shard_map/ppermute | solution.py:16
  163.6 0.0 collective-permute-done.21
  163.6 0.1 convert_add_fusion.4
  163.7 3.2 %collective-permute-start.23 = (bf16[480,128]{1,0:T(8,128)(2,1)S(1)}, bf16[480,128]{1,0:T(8,128)(2,1)S(1)}, u32[]{:S(2)}, u32[]{:S(2)}) collective-permute-start(bf16[480,128]{1,0:T(8,128)(2,1)S(1)} %pad_maximum_fusion.12), channel_id=1, source_target_pairs={{0,5},{1,6},{2,7},{3,0},{4,1},{5,2},{6,3},{7,4},{8,13},{9,14},{10,... | collective-permute-start | bytes 368648 | tf_op jit(solution)/shard_map/ppermute | solution.py:16
  166.9 3.9 %collective-permute-done.19 = bf16[480,128]{1,0:T(8,128)(2,1)S(1)} collective-permute-done((bf16[480,128]{1,0:T(8,128)(2,1)S(1)}, bf16[480,128]{1,0:T(8,128)(2,1)S(1)}, u32[]{:S(2)}, u32[]{:S(2)}) %collective-permute-start.19) | collective-permute-done | bytes 122912 | tf_op jit(solution)/shard_map/ppermute | solution.py:16
  170.8 1.9 collective-permute-start.22
  172.8 0.1 fusion.24
  172.9 1.6 collective-permute-done.23
  174.5 6.7 %collective-permute-done.22 = bf16[480,128]{1,0:T(8,128)(2,1)S(1)} collective-permute-done((bf16[480,128]{1,0:T(8,128)(2,1)S(1)}, bf16[480,128]{1,0:T(8,128)(2,1)S(1)}, u32[]{:S(2)}, u32[]{:S(2)}) %collective-permute-start.22) | collective-permute-done | bytes 122912 | tf_op jit(solution)/shard_map/ppermute | solution.py:16
  181.2 0.1 fusion.20
  181.3 0.8 reshape.43
  182.1 15.9 %all-to-all-start.1 = ((bf16[32,30,128]{2,1,0:T(8,128)(2,1)}), bf16[32,30,128]{2,1,0:T(8,128)(2,1)S(1)}, u32[]{:S(2)}, u32[]{:S(2)}) async-start(bf16[32,30,128]{2,1,0:T(8,128)(2,1)} %reshape.43), calls=%async_computation.1 | async-start | bytes 524288 | tf_op jit(solution)/shard_map/all_to_all | solution.py:236
  198.0 0.1 convert_add_fusion.1
  198.1 0.0 copy-start.11
  198.2 6.6 %collective-permute-start.11 = (bf16[768,128]{1,0:T(8,128)(2,1)S(1)}, bf16[768,128]{1,0:T(8,128)(2,1)S(1)}, u32[]{:S(2)}, u32[]{:S(2)}) collective-permute-start(bf16[768,128]{1,0:T(8,128)(2,1)S(1)} %pad_maximum_fusion.8), channel_id=1, source_target_pairs={{0,5},{1,6},{2,7},{3,0},{4,1},{5,2},{6,3},{7,4},{8,13},{9,14},{10,... | collective-permute-start | bytes 589832 | tf_op jit(solution)/shard_map/ppermute | solution.py:16
  204.9 2.0 collective-permute-start.10
  206.8 12.6 %all-to-all-done.1 = bf16[32,30,128]{2,1,0:T(8,128)(2,1)S(1)} async-done(((bf16[32,30,128]{2,1,0:T(8,128)(2,1)}), bf16[32,30,128]{2,1,0:T(8,128)(2,1)S(1)}, u32[]{:S(2)}, u32[]{:S(2)}) %all-to-all-start.1) | async-done | bytes 245792 | tf_op jit(solution)/shard_map/all_to_all | solution.py:236
  219.4 0.1 reshape.44
  219.5 0.7 fusion.4
  220.2 2.4 %collective-permute-done.10 = bf16[768,128]{1,0:T(8,128)(2,1)S(1)} collective-permute-done((bf16[768,128]{1,0:T(8,128)(2,1)S(1)}, bf16[768,128]{1,0:T(8,128)(2,1)S(1)}, u32[]{:S(2)}, u32[]{:S(2)}) %collective-permute-start.10) | collective-permute-done | bytes 196640 | tf_op jit(solution)/shard_map/ppermute | solution.py:16
  222.7 0.8 fusion.12
  (57 shorter events, 0.5 us)
Async XLA Ops:
  0.7 47.6 %copy-start = (bf16[768,128]{1,0:T(8,128)(2,1)S(1)}, bf16[768,128]{1,0:T(8,128)(2,1)}, u32[]{:S(2)}) copy-start(bf16[768,128]{1,0:T(8,128)(2,1)} %refs_8_.1) | copy-start | bytes 589828
  3.1 66.6 %all-to-all-start = ((bf16[32,30,128]{2,1,0:T(8,128)(2,1)}), bf16[32,30,128]{2,1,0:T(8,128)(2,1)S(1)}, u32[]{:S(2)}, u32[]{:S(2)}) async-start(bf16[32,30,128]{2,1,0:T(8,128)(2,1)} %reshape.41), calls=%async_computation | async-start | bytes 524288 | tf_op jit(solution)/shard_map/all_to_all | solution.py:236
  48.3 31.1 %collective-permute-start.5 = (bf16[768,128]{1,0:T(8,128)(2,1)S(1)}, bf16[768,128]{1,0:T(8,128)(2,1)S(1)}, u32[]{:S(2)}, u32[]{:S(2)}) collective-permute-start(bf16[768,128]{1,0:T(8,128)(2,1)S(1)} %copy-done), channel_id=1, source_target_pairs={{0,5},{1,6},{2,7},{3,0},{4,1},{5,2},{6,3},{7,4},{8,13},{9,14},{10,... | collective-permute-start | bytes 589832 | tf_op jit(solution)/shard_map/ppermute | solution.py:16
  55.3 24.2 %collective-permute-start.4 = (bf16[768,128]{1,0:T(8,128)(2,1)S(1)}, bf16[768,128]{1,0:T(8,128)(2,1)S(1)}, u32[]{:S(2)}, u32[]{:S(2)}) collective-permute-start(bf16[768,128]{1,0:T(8,128)(2,1)S(1)} %copy-done), channel_id=1, source_target_pairs={{0,3},{1,4},{2,5},{3,6},{4,7},{5,0},{6,1},{7,2},{8,11},{9,12},{10,... | collective-permute-start | bytes 589832 | tf_op jit(solution)/shard_map/ppermute | solution.py:16
  69.8 18.0 %collective-permute-start.13 = (bf16[480,128]{1,0:T(8,128)(2,1)S(1)}, bf16[480,128]{1,0:T(8,128)(2,1)S(1)}, u32[]{:S(2)}, u32[]{:S(2)}) collective-permute-start(bf16[480,128]{1,0:T(8,128)(2,1)S(1)} %slice.173.refs_0_), channel_id=1, source_target_pairs={{0,5},{1,6},{2,7},{3,0},{4,1},{5,2},{6,3},{7,4},{8,13},{9,14},{10,... | collective-permute-start | bytes 368648 | tf_op jit(solution)/shard_map/ppermute | solution.py:16
  77.4 16.0 %collective-permute-start.12 = (bf16[480,128]{1,0:T(8,128)(2,1)S(1)}, bf16[480,128]{1,0:T(8,128)(2,1)S(1)}, u32[]{:S(2)}, u32[]{:S(2)}) collective-permute-start(bf16[480,128]{1,0:T(8,128)(2,1)S(1)} %slice.173.refs_0_), channel_id=1, source_target_pairs={{0,3},{1,4},{2,5},{3,6},{4,7},{5,0},{6,1},{7,2},{8,11},{9,12},{10,... | collective-permute-start | bytes 368648 | tf_op jit(solution)/shard_map/ppermute | solution.py:16
  79.5 23.2 %collective-permute-start.1 = (bf16[480,128]{1,0:T(8,128)(2,1)S(1)}, bf16[480,128]{1,0:T(8,128)(2,1)S(1)}, u32[]{:S(2)}, u32[]{:S(2)}) collective-permute-start(bf16[480,128]{1,0:T(8,128)(2,1)S(1)} %slice.154.refs_0_), channel_id=1, source_target_pairs={{0,5},{1,6},{2,7},{3,0},{4,1},{5,2},{6,3},{7,4},{8,13},{9,14},{10,... | collective-permute-start | bytes 368648 | tf_op jit(solution)/shard_map/ppermute | solution.py:16
  85.9 20.2 %collective-permute-start = (bf16[480,128]{1,0:T(8,128)(2,1)S(1)}, bf16[480,128]{1,0:T(8,128)(2,1)S(1)}, u32[]{:S(2)}, u32[]{:S(2)}) collective-permute-start(bf16[480,128]{1,0:T(8,128)(2,1)S(1)} %slice.154.refs_0_), channel_id=1, source_target_pairs={{0,3},{1,4},{2,5},{3,6},{4,7},{5,0},{6,1},{7,2},{8,11},{9,12},{10,... | collective-permute-start | bytes 368648 | tf_op jit(solution)/shard_map/ppermute | solution.py:16
  94.2 16.0 %collective-permute-start.15 = (bf16[1200,128]{1,0:T(8,128)(2,1)S(1)}, bf16[1200,128]{1,0:T(8,128)(2,1)S(1)}, u32[]{:S(2)}, u32[]{:S(2)}) collective-permute-start(bf16[1200,128]{1,0:T(8,128)(2,1)S(1)} %get-tuple-element.33), channel_id=1, source_target_pairs={{0,7},{1,0},{2,1},{3,2},{4,3},{5,4},{6,5},{7,6},{8,15},{9,8},{10,9... | collective-permute-start | bytes 921608 | tf_op jit(solution)/shard_map/ppermute | solution.py:16
  97.1 24.1 %copy-start.1 = (bf16[1,1024,512]{2,1,0:T(8,128)(2,1)S(1)}, bf16[1,1024,512]{2,1,0:T(8,128)(2,1)}, u32[]{:S(2)}) copy-start(bf16[1,1024,512]{2,1,0:T(8,128)(2,1)} %param.13) | copy-start | bytes 3145732
  97.1 24.1 %copy-start.10 = (f32[1024]{0:T(1024)S(1)}, f32[1024]{0:T(1024)}, u32[]{:S(2)}) copy-start(f32[1024]{0:T(1024)} %param.10) | copy-start | bytes 12292
  97.2 31.6 %collective-permute-start.7 = (bf16[1920,128]{1,0:T(8,128)(2,1)}, bf16[1920,128]{1,0:T(8,128)(2,1)S(1)}, u32[]{:S(2)}, u32[]{:S(2)}) collective-permute-start(bf16[1920,128]{1,0:T(8,128)(2,1)} %get-tuple-element.31), channel_id=1, source_target_pairs={{0,7},{1,0},{2,1},{3,2},{4,3},{5,4},{6,5},{7,6},{8,15},{9,8},{10,9... | collective-permute-start | bytes 1474568 | tf_op jit(solution)/shard_map/ppermute | solution.py:16
  99.2 34.9 %collective-permute-start.6 = (bf16[1920,128]{1,0:T(8,128)(2,1)}, bf16[1920,128]{1,0:T(8,128)(2,1)}, u32[]{:S(2)}, u32[]{:S(2)}) collective-permute-start(bf16[1920,128]{1,0:T(8,128)(2,1)} %get-tuple-element.32), channel_id=1, source_target_pairs={{0,1},{1,2},{2,3},{3,4},{4,5},{5,6},{6,7},{7,0},{8,9},{9,10},{10,1... | collective-permute-start | bytes 1474568 | tf_op jit(solution)/shard_map/ppermute | solution.py:16
  102.6 18.6 %collective-permute-start.14 = (bf16[1200,128]{1,0:T(8,128)(2,1)}, bf16[1200,128]{1,0:T(8,128)(2,1)}, u32[]{:S(2)}, u32[]{:S(2)}) collective-permute-start(bf16[1200,128]{1,0:T(8,128)(2,1)} %get-tuple-element.34), channel_id=1, source_target_pairs={{0,1},{1,2},{2,3},{3,4},{4,5},{5,6},{6,7},{7,0},{8,9},{9,10},{10,1... | collective-permute-start | bytes 921608 | tf_op jit(solution)/shard_map/ppermute | solution.py:16
  107.0 27.1 %collective-permute-start.3 = (bf16[1200,128]{1,0:T(8,128)(2,1)}, bf16[1200,128]{1,0:T(8,128)(2,1)S(1)}, u32[]{:S(2)}, u32[]{:S(2)}) collective-permute-start(bf16[1200,128]{1,0:T(8,128)(2,1)} %get-tuple-element.35), channel_id=1, source_target_pairs={{0,7},{1,0},{2,1},{3,2},{4,3},{5,4},{6,5},{7,6},{8,15},{9,8},{10,9... | collective-permute-start | bytes 921608 | tf_op jit(solution)/shard_map/ppermute | solution.py:16
  110.1 0.7 copy-start.8
  110.9 23.2 %collective-permute-start.2 = (bf16[1200,128]{1,0:T(8,128)(2,1)}, bf16[1200,128]{1,0:T(8,128)(2,1)}, u32[]{:S(2)}, u32[]{:S(2)}) collective-permute-start(bf16[1200,128]{1,0:T(8,128)(2,1)} %get-tuple-element.36), channel_id=1, source_target_pairs={{0,1},{1,2},{2,3},{3,4},{4,5},{5,6},{6,7},{7,0},{8,9},{9,10},{10,1... | collective-permute-start | bytes 921608 | tf_op jit(solution)/shard_map/ppermute | solution.py:16
  121.3 1.2 copy-start.2
  122.5 1.0 copy-start.9
  123.5 10.6 %copy-start.3 = (bf16[1,512,1024]{2,1,0:T(8,128)(2,1)S(1)}, bf16[1,512,1024]{2,1,0:T(8,128)(2,1)}, u32[]{:S(2)}) copy-start(bf16[1,512,1024]{2,1,0:T(8,128)(2,1)} %param.14) | copy-start | bytes 3145732
  123.5 10.6 %copy-start.4 = (bf16[1024,512]{1,0:T(8,128)(2,1)S(1)}, bf16[1024,512]{1,0:T(8,128)(2,1)}, u32[]{:S(2)}) copy-start(bf16[1024,512]{1,0:T(8,128)(2,1)} %refs_13_.1) | copy-start | bytes 3145732
  123.5 10.6 %copy-start.5 = (bf16[512,1024]{1,0:T(8,128)(2,1)S(1)}, bf16[512,1024]{1,0:T(8,128)(2,1)}, u32[]{:S(2)}) copy-start(bf16[512,1024]{1,0:T(8,128)(2,1)} %refs_14_.1) | copy-start | bytes 3145732
  126.7 24.9 %collective-permute-start.16 = (bf16[1200,128]{1,0:T(8,128)(2,1)S(1)}, bf16[1200,128]{1,0:T(8,128)(2,1)S(1)}, u32[]{:S(2)}, u32[]{:S(2)}) collective-permute-start(bf16[1200,128]{1,0:T(8,128)(2,1)S(1)} %get-tuple-element.18), channel_id=1, source_target_pairs={{0,1},{1,2},{2,3},{3,4},{4,5},{5,6},{6,7},{7,0},{8,9},{9,10},{10,1... | collective-permute-start | bytes 921608 | tf_op jit(solution)/shard_map/ppermute | solution.py:16
  128.8 0.8 copy-start.6
  129.6 26.6 %collective-permute-start.17 = (bf16[1200,128]{1,0:T(8,128)(2,1)S(1)}, bf16[1200,128]{1,0:T(8,128)(2,1)S(1)}, u32[]{:S(2)}, u32[]{:S(2)}) collective-permute-start(bf16[1200,128]{1,0:T(8,128)(2,1)S(1)} %get-tuple-element.19), channel_id=1, source_target_pairs={{0,7},{1,0},{2,1},{3,2},{4,3},{5,4},{6,5},{7,6},{8,15},{9,8},{10,9... | collective-permute-start | bytes 921608 | tf_op jit(solution)/shard_map/ppermute | solution.py:16
  134.1 1.0 copy-start.7
  143.1 15.3 %collective-permute-start.20 = (bf16[1200,128]{1,0:T(8,128)(2,1)S(1)}, bf16[1200,128]{1,0:T(8,128)(2,1)S(1)}, u32[]{:S(2)}, u32[]{:S(2)}) collective-permute-start(bf16[1200,128]{1,0:T(8,128)(2,1)S(1)} %get-tuple-element.21), channel_id=1, source_target_pairs={{0,1},{1,2},{2,3},{3,4},{4,5},{5,6},{6,7},{7,0},{8,9},{9,10},{10,1... | collective-permute-start | bytes 921608 | tf_op jit(solution)/shard_map/ppermute | solution.py:16
  145.0 18.6 %collective-permute-start.21 = (bf16[1200,128]{1,0:T(8,128)(2,1)S(1)}, bf16[1200,128]{1,0:T(8,128)(2,1)S(1)}, u32[]{:S(2)}, u32[]{:S(2)}) collective-permute-start(bf16[1200,128]{1,0:T(8,128)(2,1)S(1)} %get-tuple-element.22), channel_id=1, source_target_pairs={{0,7},{1,0},{2,1},{3,2},{4,3},{5,4},{6,5},{7,6},{8,15},{9,8},{10,9... | collective-permute-start | bytes 921608 | tf_op jit(solution)/shard_map/ppermute | solution.py:16
  149.6 48.4 %collective-permute-start.8 = (bf16[1920,128]{1,0:T(8,128)(2,1)}, bf16[1920,128]{1,0:T(8,128)(2,1)S(1)}, u32[]{:S(2)}, u32[]{:S(2)}) collective-permute-start(bf16[1920,128]{1,0:T(8,128)(2,1)} %get-tuple-element.15), channel_id=1, source_target_pairs={{0,1},{1,2},{2,3},{3,4},{4,5},{5,6},{6,7},{7,0},{8,9},{9,10},{10,1... | collective-permute-start | bytes 1474568 | tf_op jit(solution)/shard_map/ppermute | solution.py:16
  151.6 46.4 %collective-permute-start.9 = (bf16[1920,128]{1,0:T(8,128)(2,1)S(1)}, bf16[1920,128]{1,0:T(8,128)(2,1)S(1)}, u32[]{:S(2)}, u32[]{:S(2)}) collective-permute-start(bf16[1920,128]{1,0:T(8,128)(2,1)S(1)} %get-tuple-element.16), channel_id=1, source_target_pairs={{0,7},{1,0},{2,1},{3,2},{4,3},{5,4},{6,5},{7,6},{8,15},{9,8},{10,9... | collective-permute-start | bytes 1474568 | tf_op jit(solution)/shard_map/ppermute | solution.py:16
  156.4 14.5 %collective-permute-start.19 = (bf16[480,128]{1,0:T(8,128)(2,1)S(1)}, bf16[480,128]{1,0:T(8,128)(2,1)S(1)}, u32[]{:S(2)}, u32[]{:S(2)}) collective-permute-start(bf16[480,128]{1,0:T(8,128)(2,1)S(1)} %pad_maximum_fusion.10), channel_id=1, source_target_pairs={{0,5},{1,6},{2,7},{3,0},{4,1},{5,2},{6,3},{7,4},{8,13},{9,14},{10,... | collective-permute-start | bytes 368648 | tf_op jit(solution)/shard_map/ppermute | solution.py:16
  158.4 14.4 %collective-permute-start.18 = (bf16[480,128]{1,0:T(8,128)(2,1)S(1)}, bf16[480,128]{1,0:T(8,128)(2,1)S(1)}, u32[]{:S(2)}, u32[]{:S(2)}) collective-permute-start(bf16[480,128]{1,0:T(8,128)(2,1)S(1)} %pad_maximum_fusion.9), channel_id=1, source_target_pairs={{0,3},{1,4},{2,5},{3,6},{4,7},{5,0},{6,1},{7,2},{8,11},{9,12},{10,... | collective-permute-start | bytes 368648 | tf_op jit(solution)/shard_map/ppermute | solution.py:16
  163.7 10.8 %collective-permute-start.23 = (bf16[480,128]{1,0:T(8,128)(2,1)S(1)}, bf16[480,128]{1,0:T(8,128)(2,1)S(1)}, u32[]{:S(2)}, u32[]{:S(2)}) collective-permute-start(bf16[480,128]{1,0:T(8,128)(2,1)S(1)} %pad_maximum_fusion.12), channel_id=1, source_target_pairs={{0,5},{1,6},{2,7},{3,0},{4,1},{5,2},{6,3},{7,4},{8,13},{9,14},{10,... | collective-permute-start | bytes 368648 | tf_op jit(solution)/shard_map/ppermute | solution.py:16
  170.8 10.4 %collective-permute-start.22 = (bf16[480,128]{1,0:T(8,128)(2,1)S(1)}, bf16[480,128]{1,0:T(8,128)(2,1)S(1)}, u32[]{:S(2)}, u32[]{:S(2)}) collective-permute-start(bf16[480,128]{1,0:T(8,128)(2,1)S(1)} %pad_maximum_fusion.11), channel_id=1, source_target_pairs={{0,3},{1,4},{2,5},{3,6},{4,7},{5,0},{6,1},{7,2},{8,11},{9,12},{10,... | collective-permute-start | bytes 368648 | tf_op jit(solution)/shard_map/ppermute | solution.py:16
  182.1 37.3 %all-to-all-start.1 = ((bf16[32,30,128]{2,1,0:T(8,128)(2,1)}), bf16[32,30,128]{2,1,0:T(8,128)(2,1)S(1)}, u32[]{:S(2)}, u32[]{:S(2)}) async-start(bf16[32,30,128]{2,1,0:T(8,128)(2,1)} %reshape.43), calls=%async_computation.1 | async-start | bytes 524288 | tf_op jit(solution)/shard_map/all_to_all | solution.py:236
  198.1 21.4 %copy-start.11 = (f32[768]{0:T(1024)S(1)}, f32[768]{0:T(1024)}, u32[]{:S(2)}) copy-start(f32[768]{0:T(1024)} %param.17) | copy-start | bytes 9220
  198.2 22.0 %collective-permute-start.11 = (bf16[768,128]{1,0:T(8,128)(2,1)S(1)}, bf16[768,128]{1,0:T(8,128)(2,1)S(1)}, u32[]{:S(2)}, u32[]{:S(2)}) collective-permute-start(bf16[768,128]{1,0:T(8,128)(2,1)S(1)} %pad_maximum_fusion.8), channel_id=1, source_target_pairs={{0,5},{1,6},{2,7},{3,0},{4,1},{5,2},{6,3},{7,4},{8,13},{9,14},{10,... | collective-permute-start | bytes 589832 | tf_op jit(solution)/shard_map/ppermute | solution.py:16
  204.9 17.8 %collective-permute-start.10 = (bf16[768,128]{1,0:T(8,128)(2,1)S(1)}, bf16[768,128]{1,0:T(8,128)(2,1)S(1)}, u32[]{:S(2)}, u32[]{:S(2)}) collective-permute-start(bf16[768,128]{1,0:T(8,128)(2,1)S(1)} %pad_maximum_fusion.7), channel_id=1, source_target_pairs={{0,3},{1,4},{2,5},{3,6},{4,7},{5,0},{6,1},{7,2},{8,11},{9,12},{10,... | collective-permute-start | bytes 589832 | tf_op jit(solution)/shard_map/ppermute | solution.py:16

commit v9 on v8

--- a/solution.py
+++ b/solution.py
@@ -17,7 +17,9 @@
 
 
 def gather_far(own):
-    return shift(own, 3), shift(own, -3)
+    below = shift(own, 3)
+    above = shift(own, -3)
+    return below, above
 
 
 def gather_near(own, below, above):
@@ -157,7 +159,7 @@
     vmem = pl.BlockSpec(memory_space=pltpu.VMEM)
     edge = jax.ShapeDtypeStruct((5 * count // 2, width), jnp.bfloat16)
     return pl.pallas_call(
-        functools.partial(ffn_body, block=count // 4),
+        functools.partial(ffn_body, block=count // 2),
         in_specs=[pl.BlockSpec(memory_space=pltpu.SMEM)] + [vmem] * 8,
         out_specs=[vmem] * 3,
         out_shape=[edge, edge, sums_of(count, width)],
@@ -178,7 +180,7 @@
     later_edge = jax.ShapeDtypeStruct((5 * later // 2, width), jnp.bfloat16)
     operands = [*later_pieces, later_in, later_out]
     return pl.pallas_call(
-        functools.partial(pair_body, block=count // 4, later_block=later // 4),
+        functools.partial(pair_body, block=count // 2, later_block=later // 2),
         in_specs=[pl.BlockSpec(memory_space=pltpu.SMEM)] + [vmem] * 8 + [anywhere] * 7,
         out_specs=[vmem] * 6,
         out_shape=[edge, edge, sums_of(count, width)]

time: 225 us -> 223 us (level)
  no operation moved by 1% of the time
where the time goes in v9:
time: 223 us; the launch traced here: 222 us
  starting transfers between devices  144 us (65%)
  waiting for transfers between devices  52.9 us (24%)
  Pallas kernels  10.1 us (5%)
  local copies, waits for them, and re-layouts  6.57 us (3%)
  other arithmetic  4.8 us (2%)
  matrix products  2.32 us (1%)
    ppermute x24, starting transfers between devices, shift(): lax.ppermute(value, axis, [(i, (i + step) % ring) for i in range(ring)])  83.4 us
    all_to_all x2, starting transfers between devices, exchange(): lax.all_to_all(rows.reshape(experts, capacity, feat_width), 'expert', spl...  61 us
    ppermute x24, waiting for transfers between devices, shift(): lax.ppermute(value, axis, [(i, (i + step) % ring) for i in range(ring)])  27.8 us
    all_to_all x2, waiting for transfers between devices, exchange(): lax.all_to_all(rows.reshape(experts, capacity, feat_width), 'expert', spl...  25.1 us
    pallas_call x1, Pallas kernels, ffn_pair(): pl.pallas_call(functools.partial(pair_body, block=count // 2, later_block...  7.24 us
    unnamed x24, local copies, waits for them, and re-layouts  4.75 us
  transfers between devices with their start and end apart: 26, of which 8 were waited for; matrix products, arithmetic and copies ran while one was open for 2% of the time, Pallas kernels for 5%

profile of v9, /device:TPU:65, one launch (start us, length us, event | category | flops | bytes accessed | tf_op | source)
XLA Modules:
  0.0 221.8 jit_solution(12442678603224202765)
XLA Ops:
  0.0 0.7 add_select_fusion
  0.7 1.6 fusion.5
  2.3 0.8 reshape.41
  3.1 45.2 %all-to-all-start = ((bf16[32,30,128]{2,1,0:T(8,128)(2,1)}), bf16[32,30,128]{2,1,0:T(8,128)(2,1)S(1)}, u32[]{:S(2)}, u32[]{:S(2)}) async-start(bf16[32,30,128]{2,1,0:T(8,128)(2,1)} %reshape.41), calls=%async_computation | async-start | bytes 524288 | tf_op jit(solution)/shard_map/all_to_all | solution.py:238
  48.3 6.9 %collective-permute-start.5 = (bf16[768,128]{1,0:T(8,128)(2,1)S(1)}, bf16[768,128]{1,0:T(8,128)(2,1)S(1)}, u32[]{:S(2)}, u32[]{:S(2)}) collective-permute-start(bf16[768,128]{1,0:T(8,128)(2,1)S(1)} %copy-done), channel_id=1, source_target_pairs={{0,5},{1,6},{2,7},{3,0},{4,1},{5,2},{6,3},{7,4},{8,13},{9,14},{10,... | collective-permute-start | bytes 589832 | tf_op jit(solution)/shard_map/ppermute | solution.py:16
  55.3 2.0 collective-permute-start.4
  57.2 12.5 %all-to-all-done = bf16[32,30,128]{2,1,0:T(8,128)(2,1)S(1)} async-done(((bf16[32,30,128]{2,1,0:T(8,128)(2,1)}), bf16[32,30,128]{2,1,0:T(8,128)(2,1)S(1)}, u32[]{:S(2)}, u32[]{:S(2)}) %all-to-all-start) | async-done | bytes 245792 | tf_op jit(solution)/shard_map/all_to_all | solution.py:238
  69.8 7.6 %collective-permute-start.13 = (bf16[480,128]{1,0:T(8,128)(2,1)S(1)}, bf16[480,128]{1,0:T(8,128)(2,1)S(1)}, u32[]{:S(2)}, u32[]{:S(2)}) collective-permute-start(bf16[480,128]{1,0:T(8,128)(2,1)S(1)} %slice.173.refs_0_), channel_id=1, source_target_pairs={{0,5},{1,6},{2,7},{3,0},{4,1},{5,2},{6,3},{7,4},{8,13},{9,14},{10,... | collective-permute-start | bytes 368648 | tf_op jit(solution)/shard_map/ppermute | solution.py:16
  77.4 2.0 collective-permute-start.12
  79.4 0.0 collective-permute-done.5.refs_10_
  79.5 6.4 %collective-permute-start.1 = (bf16[480,128]{1,0:T(8,128)(2,1)S(1)}, bf16[480,128]{1,0:T(8,128)(2,1)S(1)}, u32[]{:S(2)}, u32[]{:S(2)}) collective-permute-start(bf16[480,128]{1,0:T(8,128)(2,1)S(1)} %slice.154.refs_0_), channel_id=1, source_target_pairs={{0,5},{1,6},{2,7},{3,0},{4,1},{5,2},{6,3},{7,4},{8,13},{9,14},{10,... | collective-permute-start | bytes 368648 | tf_op jit(solution)/shard_map/ppermute | solution.py:16
  85.9 2.0 collective-permute-start
  87.8 0.0 collective-permute-done.13.refs_2_
  87.9 5.5 %collective-permute-done.12.refs_1_ = bf16[480,128]{1,0:T(8,128)(2,1)S(1)} collective-permute-done((bf16[480,128]{1,0:T(8,128)(2,1)S(1)}, bf16[480,128]{1,0:T(8,128)(2,1)S(1)}, u32[]{:S(2)}, u32[]{:S(2)}) %collective-permute-start.12) | collective-permute-done | bytes 122912 | tf_op jit(solution)/shard_map/ppermute | solution.py:16
  93.4 0.8 fusion.14
  94.2 1.9 collective-permute-start.15
  96.1 1.0 fusion.7
  97.2 2.1 collective-permute-start.7
  99.2 3.4 %collective-permute-start.6 = (bf16[1920,128]{1,0:T(8,128)(2,1)}, bf16[1920,128]{1,0:T(8,128)(2,1)}, u32[]{:S(2)}, u32[]{:S(2)}) collective-permute-start(bf16[1920,128]{1,0:T(8,128)(2,1)} %get-tuple-element.32), channel_id=1, source_target_pairs={{0,1},{1,2},{2,3},{3,4},{4,5},{5,6},{6,7},{7,0},{8,9},{9,10},{10,1... | collective-permute-start | bytes 1474568 | tf_op jit(solution)/shard_map/ppermute | solution.py:16
  102.6 3.4 %collective-permute-start.14 = (bf16[1200,128]{1,0:T(8,128)(2,1)}, bf16[1200,128]{1,0:T(8,128)(2,1)}, u32[]{:S(2)}, u32[]{:S(2)}) collective-permute-start(bf16[1200,128]{1,0:T(8,128)(2,1)} %get-tuple-element.34), channel_id=1, source_target_pairs={{0,1},{1,2},{2,3},{3,4},{4,5},{5,6},{6,7},{7,0},{8,9},{9,10},{10,1... | collective-permute-start | bytes 921608 | tf_op jit(solution)/shard_map/ppermute | solution.py:16
  106.1 0.9 fusion.16
  107.0 3.1 %collective-permute-start.3 = (bf16[1200,128]{1,0:T(8,128)(2,1)}, bf16[1200,128]{1,0:T(8,128)(2,1)S(1)}, u32[]{:S(2)}, u32[]{:S(2)}) collective-permute-start(bf16[1200,128]{1,0:T(8,128)(2,1)} %get-tuple-element.35), channel_id=1, source_target_pairs={{0,7},{1,0},{2,1},{3,2},{4,3},{5,4},{6,5},{7,6},{8,15},{9,8},{10,9... | collective-permute-start | bytes 921608 | tf_op jit(solution)/shard_map/ppermute | solution.py:16
  110.1 0.0 collective-permute-done.15.refs_4_
  110.1 0.7 copy-done.8
  110.9 2.2 collective-permute-start.2
  113.0 8.2 %collective-permute-done.14.refs_3_ = bf16[1200,128]{1,0:T(8,128)(2,1)} collective-permute-done((bf16[1200,128]{1,0:T(8,128)(2,1)}, bf16[1200,128]{1,0:T(8,128)(2,1)}, u32[]{:S(2)}, u32[]{:S(2)}) %collective-permute-start.14) | collective-permute-done | bytes 307232 | tf_op jit(solution)/shard_map/ppermute | solution.py:16
  121.3 1.2 copy-done.2
  122.5 1.0 copy-done.9
  123.5 2.9 %exp.1 = (bf16[1200,128]{1,0:T(8,128)(2,1)S(1)}, bf16[1200,128]{1,0:T(8,128)(2,1)S(1)}, bf16[3,480,128]{2,1,0:T(8,128)(2,1)S(1)}) custom-call(s32[1]{0:T(128)} %bitcast.me_ref, bf16[480,128]{1,0:T(8,128)(2,1)S(1)} %slice.173.refs_0_, bf16[480,128]{1,0:T(8,128)(2,1)S(1)} %collective-permute-done.12.refs_1_, ...), custom_call_target="tpu_custom_call" | custom-call | flops 1006632960 | bytes 4063232 | tf_op jit(solution)/shard_map/exp/pallas_call | solution.py:161
  126.4 2.1 collective-permute-start.16
  128.5 0.8 copy-done.6
  129.3 4.5 %collective-permute-start.17 = (bf16[1200,128]{1,0:T(8,128)(2,1)S(1)}, bf16[1200,128]{1,0:T(8,128)(2,1)S(1)}, u32[]{:S(2)}, u32[]{:S(2)}) collective-permute-start(bf16[1200,128]{1,0:T(8,128)(2,1)S(1)} %get-tuple-element.19), channel_id=1, source_target_pairs={{0,7},{1,0},{2,1},{3,2},{4,3},{5,4},{6,5},{7,6},{8,15},{9,8},{10,9... | collective-permute-start | bytes 921608 | tf_op jit(solution)/shard_map/ppermute | solution.py:16
  133.8 0.0 collective-permute-done.2.refs_3_
  133.8 1.0 copy-done.7
  134.9 7.2 %pair.1 = (bf16[1200,128]{1,0:T(8,128)(2,1)S(1)}, bf16[1200,128]{1,0:T(8,128)(2,1)S(1)}, bf16[3,480,128]{2,1,0:T(8,128)(2,1)S(1)}, bf16[1920,128]{1,0:T(8,128)(2...) custom-call(s32[1]{0:T(128)} %bitcast.me_ref, bf16[480,128]{1,0:T(8,128)(2,1)S(1)} %slice.154.refs_0_, ...), custom_call_target="tpu_custom_call" | custom-call | flops 2617245696 | bytes 7208960 | tf_op jit(solution)/shard_map/pair/pallas_call | solution.py:182
  142.1 2.0 collective-permute-start.20
  144.1 4.6 %collective-permute-start.21 = (bf16[1200,128]{1,0:T(8,128)(2,1)S(1)}, bf16[1200,128]{1,0:T(8,128)(2,1)S(1)}, u32[]{:S(2)}, u32[]{:S(2)}) collective-permute-start(bf16[1200,128]{1,0:T(8,128)(2,1)S(1)} %get-tuple-element.22), channel_id=1, source_target_pairs={{0,7},{1,0},{2,1},{3,2},{4,3},{5,4},{6,5},{7,6},{8,15},{9,8},{10,9... | collective-permute-start | bytes 921608 | tf_op jit(solution)/shard_map/ppermute | solution.py:16
  148.7 2.0 collective-permute-start.8
  150.6 4.6 %collective-permute-start.9 = (bf16[1920,128]{1,0:T(8,128)(2,1)S(1)}, bf16[1920,128]{1,0:T(8,128)(2,1)S(1)}, u32[]{:S(2)}, u32[]{:S(2)}) collective-permute-start(bf16[1920,128]{1,0:T(8,128)(2,1)S(1)} %get-tuple-element.16), channel_id=1, source_target_pairs={{0,7},{1,0},{2,1},{3,2},{4,3},{5,4},{6,5},{7,6},{8,15},{9,8},{10,9... | collective-permute-start | bytes 1474568 | tf_op jit(solution)/shard_map/ppermute | solution.py:16
  155.3 0.1 convert_add_fusion.7
  155.4 2.0 collective-permute-start.19
  157.4 5.2 %collective-permute-start.18 = (bf16[480,128]{1,0:T(8,128)(2,1)S(1)}, bf16[480,128]{1,0:T(8,128)(2,1)S(1)}, u32[]{:S(2)}, u32[]{:S(2)}) collective-permute-start(bf16[480,128]{1,0:T(8,128)(2,1)S(1)} %pad_maximum_fusion.9), channel_id=1, source_target_pairs={{0,3},{1,4},{2,5},{3,6},{4,7},{5,0},{6,1},{7,2},{8,11},{9,12},{10,... | collective-permute-start | bytes 368648 | tf_op jit(solution)/shard_map/ppermute | solution.py:16
  162.6 0.0 collective-permute-done.21
  162.6 0.1 convert_add_fusion.4
  162.8 3.2 %collective-permute-start.23 = (bf16[480,128]{1,0:T(8,128)(2,1)S(1)}, bf16[480,128]{1,0:T(8,128)(2,1)S(1)}, u32[]{:S(2)}, u32[]{:S(2)}) collective-permute-start(bf16[480,128]{1,0:T(8,128)(2,1)S(1)} %pad_maximum_fusion.12), channel_id=1, source_target_pairs={{0,5},{1,6},{2,7},{3,0},{4,1},{5,2},{6,3},{7,4},{8,13},{9,14},{10,... | collective-permute-start | bytes 368648 | tf_op jit(solution)/shard_map/ppermute | solution.py:16
  166.0 3.9 %collective-permute-done.19 = bf16[480,128]{1,0:T(8,128)(2,1)S(1)} collective-permute-done((bf16[480,128]{1,0:T(8,128)(2,1)S(1)}, bf16[480,128]{1,0:T(8,128)(2,1)S(1)}, u32[]{:S(2)}, u32[]{:S(2)}) %collective-permute-start.19) | collective-permute-done | bytes 122912 | tf_op jit(solution)/shard_map/ppermute | solution.py:16
  169.9 1.9 collective-permute-start.22
  171.8 0.1 fusion.24
  171.9 1.6 collective-permute-done.23
  173.6 6.7 %collective-permute-done.22 = bf16[480,128]{1,0:T(8,128)(2,1)S(1)} collective-permute-done((bf16[480,128]{1,0:T(8,128)(2,1)S(1)}, bf16[480,128]{1,0:T(8,128)(2,1)S(1)}, u32[]{:S(2)}, u32[]{:S(2)}) %collective-permute-start.22) | collective-permute-done | bytes 122912 | tf_op jit(solution)/shard_map/ppermute | solution.py:16
  180.3 0.1 fusion.20
  180.4 0.8 reshape.43
  181.2 15.8 %all-to-all-start.1 = ((bf16[32,30,128]{2,1,0:T(8,128)(2,1)}), bf16[32,30,128]{2,1,0:T(8,128)(2,1)S(1)}, u32[]{:S(2)}, u32[]{:S(2)}) async-start(bf16[32,30,128]{2,1,0:T(8,128)(2,1)} %reshape.43), calls=%async_computation.1 | async-start | bytes 524288 | tf_op jit(solution)/shard_map/all_to_all | solution.py:238
  197.0 0.0 collective-permute-done.9
  197.0 0.1 convert_add_fusion.1
  197.1 0.0 copy-start.11
  197.2 6.6 %collective-permute-start.11 = (bf16[768,128]{1,0:T(8,128)(2,1)S(1)}, bf16[768,128]{1,0:T(8,128)(2,1)S(1)}, u32[]{:S(2)}, u32[]{:S(2)}) collective-permute-start(bf16[768,128]{1,0:T(8,128)(2,1)S(1)} %pad_maximum_fusion.8), channel_id=1, source_target_pairs={{0,5},{1,6},{2,7},{3,0},{4,1},{5,2},{6,3},{7,4},{8,13},{9,14},{10,... | collective-permute-start | bytes 589832 | tf_op jit(solution)/shard_map/ppermute | solution.py:16
  203.9 2.0 collective-permute-start.10
  205.8 12.6 %all-to-all-done.1 = bf16[32,30,128]{2,1,0:T(8,128)(2,1)S(1)} async-done(((bf16[32,30,128]{2,1,0:T(8,128)(2,1)}), bf16[32,30,128]{2,1,0:T(8,128)(2,1)S(1)}, u32[]{:S(2)}, u32[]{:S(2)}) %all-to-all-start.1) | async-done | bytes 245792 | tf_op jit(solution)/shard_map/all_to_all | solution.py:238
  218.4 0.1 reshape.44
  218.5 0.7 fusion.4
  219.2 0.0 collective-permute-done.11
  219.2 1.8 collective-permute-done.10
  221.0 0.8 fusion.12
  (57 shorter events, 0.5 us)
Async XLA Ops:
  0.7 47.6 %copy-start = (bf16[768,128]{1,0:T(8,128)(2,1)S(1)}, bf16[768,128]{1,0:T(8,128)(2,1)}, u32[]{:S(2)}) copy-start(bf16[768,128]{1,0:T(8,128)(2,1)} %refs_8_.1) | copy-start | bytes 589828
  3.1 66.6 %all-to-all-start = ((bf16[32,30,128]{2,1,0:T(8,128)(2,1)}), bf16[32,30,128]{2,1,0:T(8,128)(2,1)S(1)}, u32[]{:S(2)}, u32[]{:S(2)}) async-start(bf16[32,30,128]{2,1,0:T(8,128)(2,1)} %reshape.41), calls=%async_computation | async-start | bytes 524288 | tf_op jit(solution)/shard_map/all_to_all | solution.py:238
  48.3 31.1 %collective-permute-start.5 = (bf16[768,128]{1,0:T(8,128)(2,1)S(1)}, bf16[768,128]{1,0:T(8,128)(2,1)S(1)}, u32[]{:S(2)}, u32[]{:S(2)}) collective-permute-start(bf16[768,128]{1,0:T(8,128)(2,1)S(1)} %copy-done), channel_id=1, source_target_pairs={{0,5},{1,6},{2,7},{3,0},{4,1},{5,2},{6,3},{7,4},{8,13},{9,14},{10,... | collective-permute-start | bytes 589832 | tf_op jit(solution)/shard_map/ppermute | solution.py:16
  55.3 24.2 %collective-permute-start.4 = (bf16[768,128]{1,0:T(8,128)(2,1)S(1)}, bf16[768,128]{1,0:T(8,128)(2,1)S(1)}, u32[]{:S(2)}, u32[]{:S(2)}) collective-permute-start(bf16[768,128]{1,0:T(8,128)(2,1)S(1)} %copy-done), channel_id=1, source_target_pairs={{0,3},{1,4},{2,5},{3,6},{4,7},{5,0},{6,1},{7,2},{8,11},{9,12},{10,... | collective-permute-start | bytes 589832 | tf_op jit(solution)/shard_map/ppermute | solution.py:16
  69.8 18.0 %collective-permute-start.13 = (bf16[480,128]{1,0:T(8,128)(2,1)S(1)}, bf16[480,128]{1,0:T(8,128)(2,1)S(1)}, u32[]{:S(2)}, u32[]{:S(2)}) collective-permute-start(bf16[480,128]{1,0:T(8,128)(2,1)S(1)} %slice.173.refs_0_), channel_id=1, source_target_pairs={{0,5},{1,6},{2,7},{3,0},{4,1},{5,2},{6,3},{7,4},{8,13},{9,14},{10,... | collective-permute-start | bytes 368648 | tf_op jit(solution)/shard_map/ppermute | solution.py:16
  77.4 16.0 %collective-permute-start.12 = (bf16[480,128]{1,0:T(8,128)(2,1)S(1)}, bf16[480,128]{1,0:T(8,128)(2,1)S(1)}, u32[]{:S(2)}, u32[]{:S(2)}) collective-permute-start(bf16[480,128]{1,0:T(8,128)(2,1)S(1)} %slice.173.refs_0_), channel_id=1, source_target_pairs={{0,3},{1,4},{2,5},{3,6},{4,7},{5,0},{6,1},{7,2},{8,11},{9,12},{10,... | collective-permute-start | bytes 368648 | tf_op jit(solution)/shard_map/ppermute | solution.py:16
  79.5 23.2 %collective-permute-start.1 = (bf16[480,128]{1,0:T(8,128)(2,1)S(1)}, bf16[480,128]{1,0:T(8,128)(2,1)S(1)}, u32[]{:S(2)}, u32[]{:S(2)}) collective-permute-start(bf16[480,128]{1,0:T(8,128)(2,1)S(1)} %slice.154.refs_0_), channel_id=1, source_target_pairs={{0,5},{1,6},{2,7},{3,0},{4,1},{5,2},{6,3},{7,4},{8,13},{9,14},{10,... | collective-permute-start | bytes 368648 | tf_op jit(solution)/shard_map/ppermute | solution.py:16
  85.9 20.2 %collective-permute-start = (bf16[480,128]{1,0:T(8,128)(2,1)S(1)}, bf16[480,128]{1,0:T(8,128)(2,1)S(1)}, u32[]{:S(2)}, u32[]{:S(2)}) collective-permute-start(bf16[480,128]{1,0:T(8,128)(2,1)S(1)} %slice.154.refs_0_), channel_id=1, source_target_pairs={{0,3},{1,4},{2,5},{3,6},{4,7},{5,0},{6,1},{7,2},{8,11},{9,12},{10,... | collective-permute-start | bytes 368648 | tf_op jit(solution)/shard_map/ppermute | solution.py:16
  94.2 16.0 %collective-permute-start.15 = (bf16[1200,128]{1,0:T(8,128)(2,1)S(1)}, bf16[1200,128]{1,0:T(8,128)(2,1)S(1)}, u32[]{:S(2)}, u32[]{:S(2)}) collective-permute-start(bf16[1200,128]{1,0:T(8,128)(2,1)S(1)} %get-tuple-element.33), channel_id=1, source_target_pairs={{0,7},{1,0},{2,1},{3,2},{4,3},{5,4},{6,5},{7,6},{8,15},{9,8},{10,9... | collective-permute-start | bytes 921608 | tf_op jit(solution)/shard_map/ppermute | solution.py:16
  97.1 24.1 %copy-start.1 = (bf16[1,1024,512]{2,1,0:T(8,128)(2,1)S(1)}, bf16[1,1024,512]{2,1,0:T(8,128)(2,1)}, u32[]{:S(2)}) copy-start(bf16[1,1024,512]{2,1,0:T(8,128)(2,1)} %param.13) | copy-start | bytes 3145732
  97.1 24.1 %copy-start.10 = (f32[1024]{0:T(1024)S(1)}, f32[1024]{0:T(1024)}, u32[]{:S(2)}) copy-start(f32[1024]{0:T(1024)} %param.10) | copy-start | bytes 12292
  97.2 31.3 %collective-permute-start.7 = (bf16[1920,128]{1,0:T(8,128)(2,1)}, bf16[1920,128]{1,0:T(8,128)(2,1)S(1)}, u32[]{:S(2)}, u32[]{:S(2)}) collective-permute-start(bf16[1920,128]{1,0:T(8,128)(2,1)} %get-tuple-element.31), channel_id=1, source_target_pairs={{0,7},{1,0},{2,1},{3,2},{4,3},{5,4},{6,5},{7,6},{8,15},{9,8},{10,9... | collective-permute-start | bytes 1474568 | tf_op jit(solution)/shard_map/ppermute | solution.py:16
  99.2 34.5 %collective-permute-start.6 = (bf16[1920,128]{1,0:T(8,128)(2,1)}, bf16[1920,128]{1,0:T(8,128)(2,1)}, u32[]{:S(2)}, u32[]{:S(2)}) collective-permute-start(bf16[1920,128]{1,0:T(8,128)(2,1)} %get-tuple-element.32), channel_id=1, source_target_pairs={{0,1},{1,2},{2,3},{3,4},{4,5},{5,6},{6,7},{7,0},{8,9},{9,10},{10,1... | collective-permute-start | bytes 1474568 | tf_op jit(solution)/shard_map/ppermute | solution.py:16
  102.6 18.6 %collective-permute-start.14 = (bf16[1200,128]{1,0:T(8,128)(2,1)}, bf16[1200,128]{1,0:T(8,128)(2,1)}, u32[]{:S(2)}, u32[]{:S(2)}) collective-permute-start(bf16[1200,128]{1,0:T(8,128)(2,1)} %get-tuple-element.34), channel_id=1, source_target_pairs={{0,1},{1,2},{2,3},{3,4},{4,5},{5,6},{6,7},{7,0},{8,9},{9,10},{10,1... | collective-permute-start | bytes 921608 | tf_op jit(solution)/shard_map/ppermute | solution.py:16
  107.0 26.8 %collective-permute-start.3 = (bf16[1200,128]{1,0:T(8,128)(2,1)}, bf16[1200,128]{1,0:T(8,128)(2,1)S(1)}, u32[]{:S(2)}, u32[]{:S(2)}) collective-permute-start(bf16[1200,128]{1,0:T(8,128)(2,1)} %get-tuple-element.35), channel_id=1, source_target_pairs={{0,7},{1,0},{2,1},{3,2},{4,3},{5,4},{6,5},{7,6},{8,15},{9,8},{10,9... | collective-permute-start | bytes 921608 | tf_op jit(solution)/shard_map/ppermute | solution.py:16
  110.1 0.7 copy-start.8
  110.9 22.9 %collective-permute-start.2 = (bf16[1200,128]{1,0:T(8,128)(2,1)}, bf16[1200,128]{1,0:T(8,128)(2,1)}, u32[]{:S(2)}, u32[]{:S(2)}) collective-permute-start(bf16[1200,128]{1,0:T(8,128)(2,1)} %get-tuple-element.36), channel_id=1, source_target_pairs={{0,1},{1,2},{2,3},{3,4},{4,5},{5,6},{6,7},{7,0},{8,9},{9,10},{10,1... | collective-permute-start | bytes 921608 | tf_op jit(solution)/shard_map/ppermute | solution.py:16
  121.3 1.2 copy-start.2
  122.5 1.0 copy-start.9
  123.5 10.3 %copy-start.3 = (bf16[1,512,1024]{2,1,0:T(8,128)(2,1)S(1)}, bf16[1,512,1024]{2,1,0:T(8,128)(2,1)}, u32[]{:S(2)}) copy-start(bf16[1,512,1024]{2,1,0:T(8,128)(2,1)} %param.14) | copy-start | bytes 3145732
  123.5 10.3 %copy-start.4 = (bf16[1024,512]{1,0:T(8,128)(2,1)S(1)}, bf16[1024,512]{1,0:T(8,128)(2,1)}, u32[]{:S(2)}) copy-start(bf16[1024,512]{1,0:T(8,128)(2,1)} %refs_13_.1) | copy-start | bytes 3145732
  123.5 10.3 %copy-start.5 = (bf16[512,1024]{1,0:T(8,128)(2,1)S(1)}, bf16[512,1024]{1,0:T(8,128)(2,1)}, u32[]{:S(2)}) copy-start(bf16[512,1024]{1,0:T(8,128)(2,1)} %refs_14_.1) | copy-start | bytes 3145732
  126.4 24.2 %collective-permute-start.16 = (bf16[1200,128]{1,0:T(8,128)(2,1)S(1)}, bf16[1200,128]{1,0:T(8,128)(2,1)S(1)}, u32[]{:S(2)}, u32[]{:S(2)}) collective-permute-start(bf16[1200,128]{1,0:T(8,128)(2,1)S(1)} %get-tuple-element.18), channel_id=1, source_target_pairs={{0,1},{1,2},{2,3},{3,4},{4,5},{5,6},{6,7},{7,0},{8,9},{9,10},{10,1... | collective-permute-start | bytes 921608 | tf_op jit(solution)/shard_map/ppermute | solution.py:16
  128.5 0.8 copy-start.6
  129.3 26.0 %collective-permute-start.17 = (bf16[1200,128]{1,0:T(8,128)(2,1)S(1)}, bf16[1200,128]{1,0:T(8,128)(2,1)S(1)}, u32[]{:S(2)}, u32[]{:S(2)}) collective-permute-start(bf16[1200,128]{1,0:T(8,128)(2,1)S(1)} %get-tuple-element.19), channel_id=1, source_target_pairs={{0,7},{1,0},{2,1},{3,2},{4,3},{5,4},{6,5},{7,6},{8,15},{9,8},{10,9... | collective-permute-start | bytes 921608 | tf_op jit(solution)/shard_map/ppermute | solution.py:16
  133.8 1.0 copy-start.7
  142.1 15.3 %collective-permute-start.20 = (bf16[1200,128]{1,0:T(8,128)(2,1)S(1)}, bf16[1200,128]{1,0:T(8,128)(2,1)S(1)}, u32[]{:S(2)}, u32[]{:S(2)}) collective-permute-start(bf16[1200,128]{1,0:T(8,128)(2,1)S(1)} %get-tuple-element.21), channel_id=1, source_target_pairs={{0,1},{1,2},{2,3},{3,4},{4,5},{5,6},{6,7},{7,0},{8,9},{9,10},{10,1... | collective-permute-start | bytes 921608 | tf_op jit(solution)/shard_map/ppermute | solution.py:16
  144.1 18.6 %collective-permute-start.21 = (bf16[1200,128]{1,0:T(8,128)(2,1)S(1)}, bf16[1200,128]{1,0:T(8,128)(2,1)S(1)}, u32[]{:S(2)}, u32[]{:S(2)}) collective-permute-start(bf16[1200,128]{1,0:T(8,128)(2,1)S(1)} %get-tuple-element.22), channel_id=1, source_target_pairs={{0,7},{1,0},{2,1},{3,2},{4,3},{5,4},{6,5},{7,6},{8,15},{9,8},{10,9... | collective-permute-start | bytes 921608 | tf_op jit(solution)/shard_map/ppermute | solution.py:16
  148.7 48.3 %collective-permute-start.8 = (bf16[1920,128]{1,0:T(8,128)(2,1)}, bf16[1920,128]{1,0:T(8,128)(2,1)S(1)}, u32[]{:S(2)}, u32[]{:S(2)}) collective-permute-start(bf16[1920,128]{1,0:T(8,128)(2,1)} %get-tuple-element.15), channel_id=1, source_target_pairs={{0,1},{1,2},{2,3},{3,4},{4,5},{5,6},{6,7},{7,0},{8,9},{9,10},{10,1... | collective-permute-start | bytes 1474568 | tf_op jit(solution)/shard_map/ppermute | solution.py:16
  150.6 46.4 %collective-permute-start.9 = (bf16[1920,128]{1,0:T(8,128)(2,1)S(1)}, bf16[1920,128]{1,0:T(8,128)(2,1)S(1)}, u32[]{:S(2)}, u32[]{:S(2)}) collective-permute-start(bf16[1920,128]{1,0:T(8,128)(2,1)S(1)} %get-tuple-element.16), channel_id=1, source_target_pairs={{0,7},{1,0},{2,1},{3,2},{4,3},{5,4},{6,5},{7,6},{8,15},{9,8},{10,9... | collective-permute-start | bytes 1474568 | tf_op jit(solution)/shard_map/ppermute | solution.py:16
  155.4 14.4 %collective-permute-start.19 = (bf16[480,128]{1,0:T(8,128)(2,1)S(1)}, bf16[480,128]{1,0:T(8,128)(2,1)S(1)}, u32[]{:S(2)}, u32[]{:S(2)}) collective-permute-start(bf16[480,128]{1,0:T(8,128)(2,1)S(1)} %pad_maximum_fusion.10), channel_id=1, source_target_pairs={{0,5},{1,6},{2,7},{3,0},{4,1},{5,2},{6,3},{7,4},{8,13},{9,14},{10,... | collective-permute-start | bytes 368648 | tf_op jit(solution)/shard_map/ppermute | solution.py:16
  157.4 14.4 %collective-permute-start.18 = (bf16[480,128]{1,0:T(8,128)(2,1)S(1)}, bf16[480,128]{1,0:T(8,128)(2,1)S(1)}, u32[]{:S(2)}, u32[]{:S(2)}) collective-permute-start(bf16[480,128]{1,0:T(8,128)(2,1)S(1)} %pad_maximum_fusion.9), channel_id=1, source_target_pairs={{0,3},{1,4},{2,5},{3,6},{4,7},{5,0},{6,1},{7,2},{8,11},{9,12},{10,... | collective-permute-start | bytes 368648 | tf_op jit(solution)/shard_map/ppermute | solution.py:16
  162.8 10.8 %collective-permute-start.23 = (bf16[480,128]{1,0:T(8,128)(2,1)S(1)}, bf16[480,128]{1,0:T(8,128)(2,1)S(1)}, u32[]{:S(2)}, u32[]{:S(2)}) collective-permute-start(bf16[480,128]{1,0:T(8,128)(2,1)S(1)} %pad_maximum_fusion.12), channel_id=1, source_target_pairs={{0,5},{1,6},{2,7},{3,0},{4,1},{5,2},{6,3},{7,4},{8,13},{9,14},{10,... | collective-permute-start | bytes 368648 | tf_op jit(solution)/shard_map/ppermute | solution.py:16
  169.9 10.4 %collective-permute-start.22 = (bf16[480,128]{1,0:T(8,128)(2,1)S(1)}, bf16[480,128]{1,0:T(8,128)(2,1)S(1)}, u32[]{:S(2)}, u32[]{:S(2)}) collective-permute-start(bf16[480,128]{1,0:T(8,128)(2,1)S(1)} %pad_maximum_fusion.11), channel_id=1, source_target_pairs={{0,3},{1,4},{2,5},{3,6},{4,7},{5,0},{6,1},{7,2},{8,11},{9,12},{10,... | collective-permute-start | bytes 368648 | tf_op jit(solution)/shard_map/ppermute | solution.py:16
  181.2 37.3 %all-to-all-start.1 = ((bf16[32,30,128]{2,1,0:T(8,128)(2,1)}), bf16[32,30,128]{2,1,0:T(8,128)(2,1)S(1)}, u32[]{:S(2)}, u32[]{:S(2)}) async-start(bf16[32,30,128]{2,1,0:T(8,128)(2,1)} %reshape.43), calls=%async_computation.1 | async-start | bytes 524288 | tf_op jit(solution)/shard_map/all_to_all | solution.py:238
  197.1 21.4 %copy-start.11 = (f32[768]{0:T(1024)S(1)}, f32[768]{0:T(1024)}, u32[]{:S(2)}) copy-start(f32[768]{0:T(1024)} %param.17) | copy-start | bytes 9220
  197.2 22.0 %collective-permute-start.11 = (bf16[768,128]{1,0:T(8,128)(2,1)S(1)}, bf16[768,128]{1,0:T(8,128)(2,1)S(1)}, u32[]{:S(2)}, u32[]{:S(2)}) collective-permute-start(bf16[768,128]{1,0:T(8,128)(2,1)S(1)} %pad_maximum_fusion.8), channel_id=1, source_target_pairs={{0,5},{1,6},{2,7},{3,0},{4,1},{5,2},{6,3},{7,4},{8,13},{9,14},{10,... | collective-permute-start | bytes 589832 | tf_op jit(solution)/shard_map/ppermute | solution.py:16
  203.9 17.1 %collective-permute-start.10 = (bf16[768,128]{1,0:T(8,128)(2,1)S(1)}, bf16[768,128]{1,0:T(8,128)(2,1)S(1)}, u32[]{:S(2)}, u32[]{:S(2)}) collective-permute-start(bf16[768,128]{1,0:T(8,128)(2,1)S(1)} %pad_maximum_fusion.7), channel_id=1, source_target_pairs={{0,3},{1,4},{2,5},{3,6},{4,7},{5,0},{6,1},{7,2},{8,11},{9,12},{10,... | collective-permute-start | bytes 589832 | tf_op jit(solution)/shard_map/ppermute | solution.py:16
